TPU v7x, 128 devices: a whole 4x4x4 slice. The times are simulated.
128 devices in a mesh: gx: 4 (over z_lo, core), gy: 4 (over y), gz: 8 (over x, z_hi).
Axes of the slice: x: 4, y: 4, z: 4 (z_hi: 2, z_lo: 2; z = z_hi * 2 + z_lo), core: 2. Of those that a mesh axis runs over, the one named last changes fastest.
Arguments:
- gradients: bfloat16 [128, 3072, 512], P(('gx', 'gy', 'gz')), may hold values from -24 to 24
- master_weights: float32 [3072, 512], P(('gx', 'gy', 'gz')), may hold values from -10 to 10
- first_moment: float32 [3072, 512], P(('gx', 'gy', 'gz')), may hold values from -8 to 8
- second_moment: float32 [3072, 512], P(('gx', 'gy', 'gz')), may hold values from 1 to 100
- tensor_ids: int32 [3072], P(('gx', 'gy', 'gz')), may hold values from 0 to 3, as said below
Outputs:
- new_master: float32 [3072, 512], P(('gx', 'gy', 'gz'))
- new_first: float32 [3072, 512], P(('gx', 'gy', 'gz'))
- new_second: float32 [3072, 512], P(('gx', 'gy', 'gz'))
- scaled_update: float32 [3072, 512], P(('gx', 'gy', 'gz'))
- params: bfloat16 [3072, 512], replicated
Inputs may be any that keep to these rules, and one draw needn't show every extreme that they name: `tensor_ids`: nondecreasing along the rows; every tensor of 4 owns one contiguous run of rows.
All inputs are finite; a program needn't handle non-finite values.
Results may differ from a plain program's by a relative error of at most 0.0045.
Values may be sent and summed in bfloat16 or wider, within the bound.
No kernel may reach another device: no remote copies, remote signals or barrier semaphores. Data moves between devices by JAX's collectives and lax.ppermute only.
A program may use at most 64 MiB of HBM per device.

v0:
```python
import functools

import jax
import jax.numpy as jnp
import numpy as np
from jax import lax
from jax.experimental import pallas as pl
from jax.experimental.pallas import tpu as pltpu
from jax.sharding import Mesh
from jax.sharding import PartitionSpec as P


decay_first = 0.9
decay_second = 0.999
epsilon = 1e-06
weight_decay = 0.01
step_size = 0.05


ROWS = 24
COLS = 512
CHIPS = 64
GROUP = 8
F32 = jnp.float32
BF16 = jnp.bfloat16

NUMBER = np.arange(2 * CHIPS).reshape(2, 2, 4, 4, 2)
PLACE = NUMBER.transpose(3, 2, 4, 0, 1).reshape(4, 4, 4, 2)

CORE_SWAP = [(int(a), int(b)) for pair in PLACE.reshape(CHIPS, 2) for a, b in (pair, pair[::-1])]


def grouping():
    grid = np.zeros((2, GROUP, GROUP), int)
    for core in range(2):
        for a in range(GROUP):
            for b in range(GROUP):
                x, low, z, high = (a >> 1, a & 1, b >> 1, b & 1) if core == 0 else (b >> 1, b & 1, a >> 1, a & 1)
                grid[core, a, b] = PLACE[x, 2 * high + (low ^ high), z, core]
    wide = [grid[core, :, b].tolist() for core in range(2) for b in range(GROUP)]
    narrow = [grid[core, a, :].tolist() for core in range(2) for a in range(GROUP)]
    return wide, narrow


WIDE, NARROW = grouping()


def place_of(device):
    return device >> 6, (device >> 5) & 1, (device >> 3) & 3, (device >> 1) & 3, device & 1


def wide_place(device):
    z_lo, core, y, x, z_hi = place_of(device)
    return jnp.where(core == 0, 2 * x + ((y ^ (y >> 1)) & 1), 2 * (2 * z_hi + z_lo) + (y >> 1))


OFFSETS = ((2, 1), (3, 1), (1, 1), (2, 0), (0, 1), (3, 0), (1, 0))


def source_place(a, offset):
    ring, pair = offset
    return ((((a >> 1) + 4 - ring) & 3) << 1) + ((a & 1) ^ pair)


def wide_shift(offset):
    return [(group[source_place(a, offset)], group[a]) for group in WIDE for a in range(GROUP)]


def owner_of(core, a, b):
    first = core == 0
    p = jnp.where(first, a, b)
    q = jnp.where(first, b, a)
    x, z = p >> 1, q >> 1
    y = 2 * (q & 1) + ((p ^ q) & 1)
    return ((z & 1) << 6) + (core << 5) + (y << 3) + (x << 1) + (z >> 1)


def exchange(value, groups):
    return lax.all_to_all(value, "i", 0, 0, axis_index_groups=groups, tiled=True)


def lane_index(rows):
    return lax.broadcasted_iota(jnp.int32, (rows, 128), 1)


def update_kernel(parts, weights, first, second, ids, new_first, new_second, update, sums):
    summed = parts[0].astype(F32)
    for k in range(1, GROUP):
        summed = summed + parts[k].astype(F32)
    w = weights[...]
    m = decay_first * first[...] + (1.0 - decay_first) * summed
    v = decay_second * second[...] + (1.0 - decay_second) * summed * summed
    u = m / (jnp.sqrt(v) + epsilon) + weight_decay * w
    new_first[...] = m
    new_second[...] = v
    update[...] = u
    lane = lane_index(ROWS)
    kind = lane // 4
    w_sq = jnp.sum(w * w, axis=1, keepdims=True)
    u_sq = jnp.sum(u * u, axis=1, keepdims=True)
    by_kind = jnp.where(kind == 0, w_sq, jnp.where(kind == 1, u_sq, jnp.where(kind == 2, float(COLS), 0.0)))
    row = lax.broadcasted_iota(jnp.int32, (ROWS, 128), 0)
    tensor = jnp.zeros((ROWS, 128), jnp.int32)
    for k in range(ROWS):
        tensor = jnp.where(row == k, ids[k], tensor)
    per_tensor = jnp.sum(jnp.where(tensor == lane % 4, by_kind, 0.0), axis=0, keepdims=True)
    sums[...] = jnp.broadcast_to(per_tensor, (8, 128))


PAY = 2 * ROWS + 8


def pay_kernel(update, weights, sums, pay):
    total = sums[0, 0:1, :]
    for k in range(1, GROUP):
        total = total + sums[k, 0:1, :]
    high = total.astype(BF16)
    rest = total - high.astype(F32)
    mid = rest.astype(BF16)
    low = (rest - mid.astype(F32)).astype(BF16)
    row = lax.broadcasted_iota(jnp.int32, (8, 128), 0)
    three = jnp.where(
        row == 0, high.astype(F32), jnp.where(row == 1, mid.astype(F32), jnp.where(row == 2, low.astype(F32), 0.0))
    )
    three = jnp.concatenate([three, jnp.zeros((8, COLS - 128), F32)], axis=1)
    one = jnp.concatenate([update[...], weights[...], three], axis=0).astype(BF16)
    for k in range(GROUP):
        pay[k] = one


def trust_and_runs(got):
    total = jnp.zeros((1, 128), F32)
    for k in range(GROUP):
        three = got[k, 2 * ROWS :, 0:128].astype(F32)
        total = total + ((three[0:1] + three[1:2]) + three[2:3])
    update_sq = pltpu.roll(total, 124, 1)
    count = pltpu.roll(total, 120, 1)
    lane = lane_index(1)
    used = lane < 4
    trust = jnp.where(used, jnp.sqrt(total / (update_sq + count)), 0.0)
    rows = jnp.where(used, count * (1.0 / COLS), 0.0)
    start = jnp.zeros((1, 128), F32)
    for k in range(1, 4):
        start = start + jnp.where(lane >= k, pltpu.roll(rows, k, 1), 0.0)
    return trust, start, jnp.where(used, start + rows, -1.0)


def row_trust(first_row, trust, start, end):
    row = (lax.broadcasted_iota(jnp.int32, (ROWS, 128), 0) + first_row).astype(F32)
    here = jnp.logical_and(row >= start, row < end)
    return jnp.sum(jnp.where(here, trust, 0.0), axis=1, keepdims=True)


def params_kernel(me, got, params):
    trust, start, end = trust_and_runs(got)
    core = (me[0] >> 5) & 1
    place = wide_place(me[0])
    for b in range(GROUP):
        factor = row_trust(owner_of(core, place, b) * ROWS, trust, start, end)
        update = got[b, 0:ROWS].astype(F32)
        weights = got[b, ROWS : 2 * ROWS].astype(F32)
        params[b] = (weights - step_size * (factor * update)).astype(BF16)


def own_rows_kernel(me, got, update, weights, new_master, scaled_update):
    trust, start, end = trust_and_runs(got)
    scaled = row_trust(me[0] * ROWS, trust, start, end) * update[...]
    scaled_update[...] = scaled
    new_master[...] = weights[...] - step_size * scaled


def take_kernel(me, gradients, half, done, *, other):
    core = (me[0] >> 5) & 1
    if other:
        core = 1 - core
    copies = [
        pltpu.make_async_copy(gradients.at[z_lo, core], half.at[pl.ds(z_lo * CHIPS // 2, CHIPS // 2)], done.at[z_lo])
        for z_lo in range(2)
    ]
    for copy in copies:
        copy.start()
    for copy in copies:
        copy.wait()


def add_kernel(me, kept, arrived, both):
    core = (me[0] >> 5) & 1

    def add(a, carry):
        for b in range(GROUP):
            device = owner_of(core, a, b)
            k = ((device >> 6) << 5) + (device & 31)
            both[a, b] = kept[k] + arrived[k]
        return carry

    lax.fori_loop(0, GROUP, add, 0)


def total_kernel(parts, total):
    for b in range(GROUP):
        summed = parts[0, b].astype(F32)
        for a in range(1, GROUP):
            summed = summed + parts[a, b].astype(F32)
        total[b] = summed.astype(BF16)


def chip_sums_kernel(sums, arrived, out):
    both = sums[...] + arrived[...]
    for k in range(GROUP):
        out[k] = both


def join_kernel(*refs):
    for k, part in enumerate(refs[:-1]):
        refs[-1][k] = part[...]


def place_kernel(me, *refs, chunks, first):
    count = 1 + max(chunk[0] for chunk in chunks)
    blocks, out, done = refs[:count], refs[-2], refs[-1]
    del first
    for array, index, other, offset in chunks:
        device = me[0] ^ (32 if other else 0)
        core = (device >> 5) & 1
        a = source_place(wide_place(device), offset)
        part = blocks[array] if index is None else blocks[array].at[index]
        for b in range(GROUP):
            pltpu.make_async_copy(part.at[b], out.at[owner_of(core, a, b)], done).start()
    total = len(chunks) * GROUP
    pltpu.make_async_copy(out.at[pl.ds(0, total)], out.at[pl.ds(0, total)], done).wait()


SMEM = pl.BlockSpec(memory_space=pltpu.SMEM)
VMEM = pl.BlockSpec(memory_space=pltpu.VMEM)
HBM = pl.BlockSpec(memory_space=pltpu.HBM)


def of(shape, dtype):
    return jax.ShapeDtypeStruct(shape, dtype)


def kernel(body, ins, outs, shapes, limit=8, **more):
    return pl.pallas_call(
        body,
        out_shape=shapes,
        in_specs=ins,
        out_specs=outs,
        compiler_params=pltpu.CompilerParams(vmem_limit_bytes=limit * 2**20),
        **more,
    )


def on_device(gradients, master_weights, first_moment, second_moment, tensor_ids):
    me = lax.axis_index("i").astype(jnp.int32).reshape(1)
    own_f32 = of((ROWS, COLS), F32)
    half = pltpu.VMEM((CHIPS, ROWS, COLS), BF16)
    copy_scratch = dict(scratch_shapes=[pltpu.SemaphoreType.DMA((2,))])

    halves = gradients.reshape(2, 2, CHIPS // 2, ROWS, COLS)
    halves = pltpu.with_memory_space_constraint(halves, pltpu.HBM)
    take = lambda other: kernel(
        functools.partial(take_kernel, other=other), [SMEM, HBM], VMEM, half, **copy_scratch
    )(me, halves)
    sent = take(True)
    arrived = lax.ppermute(sent, "i", CORE_SWAP)
    kept = take(False)
    blocks = pltpu.VMEM((GROUP, GROUP, ROWS, COLS), BF16)
    both = kernel(add_kernel, [SMEM] + [VMEM] * 2, VMEM, blocks)(me, kept, arrived)
    parts = exchange(both, WIDE)
    total = kernel(total_kernel, [VMEM], VMEM, pltpu.VMEM((GROUP, ROWS, COLS), BF16))(parts)
    parts = exchange(total, NARROW)

    new_first, new_second, update, sums = kernel(
        update_kernel, [VMEM] * 4 + [SMEM], (VMEM,) * 4, (own_f32, own_f32, own_f32, of((8, 128), F32))
    )(parts, master_weights, first_moment, second_moment, tensor_ids)

    arrived = lax.ppermute(sums, "i", CORE_SWAP)
    sums = kernel(chip_sums_kernel, [VMEM] * 2, VMEM, of((GROUP, 8, 128), F32))(sums, arrived)
    sums = exchange(sums, WIDE)
    pay = kernel(pay_kernel, [VMEM] * 3, VMEM, of((GROUP, PAY, COLS), BF16))(update, master_weights, sums)
    got = exchange(pay, NARROW)

    chunk = pltpu.VMEM((GROUP, ROWS, COLS), BF16)
    params = kernel(params_kernel, [SMEM, VMEM], VMEM, chunk)(me, got)
    new_master, scaled_update = kernel(
        own_rows_kernel, [SMEM] + [VMEM] * 3, (VMEM, VMEM), (own_f32, own_f32)
    )(me, got, update, master_weights)

    def send(value, pairs):
        return lax.ppermute(value, "i", pairs)

    join = lambda *parts: kernel(
        join_kernel, [VMEM] * len(parts), VMEM, pltpu.VMEM((len(parts), GROUP, ROWS, COLS), BF16)
    )(*parts)
    every = of((2 * CHIPS, ROWS, COLS), BF16)

    def place(arrays, chunks, before=None):
        first = before is None
        return kernel(
            functools.partial(place_kernel, chunks=chunks, first=first),
            [SMEM] + [VMEM] * len(arrays) + ([] if first else [HBM]),
            HBM,
            every,
            scratch_shapes=[pltpu.SemaphoreType.DMA],
            input_output_aliases={} if first else {1 + len(arrays): 0},
        )(me, *arrays, *(() if first else (before,)))

    own = (0, 0)
    wide = [send(params, wide_shift(offset)) for offset in OFFSETS]
    other_own = send(params, CORE_SWAP)
    other_0 = send(join(*wide[0:3]), CORE_SWAP)
    other_1 = send(join(*wide[3:5]), CORE_SWAP)
    other_2 = send(wide[5], CORE_SWAP)
    other_3 = send(wide[6], CORE_SWAP)
    gathered = place(
        [params, *wide[0:5], other_own, other_0],
        [(0, None, False, own)]
        + [(1 + k, None, False, OFFSETS[k]) for k in range(5)]
        + [(6, None, True, own)]
        + [(7, k, True, OFFSETS[k]) for k in range(3)],
    )
    gathered = place(
        [wide[5], other_1], [(0, None, False, OFFSETS[5])] + [(1, k, True, OFFSETS[3 + k]) for k in range(2)], gathered
    )
    gathered = place(
        [wide[6], other_2, other_3],
        [(0, None, False, OFFSETS[6]), (1, None, True, OFFSETS[5]), (2, None, True, OFFSETS[6])],
        gathered,
    )
    gathered = gathered.reshape(2 * CHIPS * ROWS, COLS)
    return (new_master, new_first, new_second, scaled_update, gathered)


def solution(mesh):
    flat = Mesh(mesh.devices.reshape(2 * CHIPS), ("i",))
    return jax.shard_map(
        on_device,
        mesh=flat,
        in_specs=(P("i", None, None), P("i", None), P("i", None), P("i", None), P("i")),
        out_specs=(P("i", None), P("i", None), P("i", None), P("i", None), P()),
        check_vma=False,
    )
```

profile of v0, /device:TPU:1, one launch (start us, length us, event | category | flops | bytes accessed | tf_op | source)
XLA Modules:
  0.0 89.8 jit_solution(4554510110029819820)
XLA Ops:
  0.6 1.4 %shard_map.93 = bf16[64,24,512]{2,1,0:T(8,128)(2,1)S(1)} custom-call(s32[1]{0:T(128)} %bitcast.me, bf16[2,2,32,24,512]{4,3,2,1,0:T(8,128)(2,1)} %bitcast.4), custom_call_target="tpu_custom_call" | custom-call | tf_op jit(solution)/shard_map/pallas_call | solution.py:261
  2.0 1.5 %collective-permute-start = (bf16[64,24,512]{2,1,0:T(8,128)(2,1)S(1)}, bf16[64,24,512]{2,1,0:T(8,128)(2,1)S(1)}, u32[]{:S(2)}, u32[]{:S(2)}) collective-permute-start(bf16[64,24,512]{2,1,0:T(8,128)(2,1)S(1)} %shard_map.93), channel_id=1, source_target_pairs={{0,32},{32,0},{64,96},{96,64},{1,33},{33,1},{65,97},{97,65},{8,40}... | collective-permute-start | bytes 4718600 | tf_op jit(solution)/shard_map/ppermute | solution.py:265
  3.5 1.4 %shard_map.92.kept = bf16[64,24,512]{2,1,0:T(8,128)(2,1)S(1)} custom-call(s32[1]{0:T(128)} %bitcast.me, bf16[2,2,32,24,512]{4,3,2,1,0:T(8,128)(2,1)} %bitcast.5), custom_call_target="tpu_custom_call" | custom-call | tf_op jit(solution)/shard_map/pallas_call | solution.py:261
  4.9 1.6 %collective-permute-done.arrived = bf16[64,24,512]{2,1,0:T(8,128)(2,1)S(1)} collective-permute-done((bf16[64,24,512]{2,1,0:T(8,128)(2,1)S(1)}, bf16[64,24,512]{2,1,0:T(8,128)(2,1)S(1)}, u32[]{:S(2)}, u32[]{:S(2)}) %collective-permute-start) | collective-permute-done | bytes 1572896 | tf_op jit(solution)/shard_map/ppermute | solution.py:265
  7.1 21.8 %all_to_all.20.parts = bf16[8,8,24,512]{3,2,1,0:T(8,128)(2,1)S(1)} all-to-all(bf16[8,8,24,512]{3,2,1,0:T(8,128)(2,1)S(1)} %shard_map.94), channel_id=1, replica_groups={{0,8,2,10,4,12,6,14},{24,16,26,18,28,20,30,22},{64,72,66,74,68,76,70,78..., dimensions={0} | all-to-all | bytes 3145728 | tf_op jit(solution)/shard_map/all_to_all | solution.py:79
  29.1 9.3 %all_to_all.21.parts = bf16[8,24,512]{2,1,0:T(8,128)(2,1)S(1)} all-to-all(bf16[8,24,512]{2,1,0:T(8,128)(2,1)S(1)} %shard_map.95), channel_id=1, replica_groups={{0,24,64,88,1,25,65,89},{8,16,72,80,9,17,73,81},{2,26,66,90,3,27,67,91}..., dimensions={0} | all-to-all | bytes 393216 | tf_op jit(solution)/shard_map/all_to_all | solution.py:79
  38.4 1.2 %shard_map.96 = (f32[24,512]{1,0:T(8,128)}, f32[24,512]{1,0:T(8,128)}, f32[24,512]{1,0:T(8,128)S(1)}, f32[8,128]{1,0:T(8,128)S(1)}) custom-call(bf16[8,24,512]{2,1,0:T(8,128)(2,1)S(1)} %all_to_all.21.parts, f32[24,512]{1,0:T(8,128)S(1)} %copy-done, f32[24,512]{1,0:T(8,128)S(1)} %copy-done.1, f32[24,512]{1,0:T(8,128)S(1)} %copy-done.2, s32[24]{0:T(128)S(1)} %copy-done.3), custom_call_target="tpu_custom_call" | custom-call | tf_op jit(solution)/shard_map/pallas_call | solution.py:273
  39.7 3.4 %collective-permute-start.1 = (f32[8,128]{1,0:T(8,128)S(1)}, f32[8,128]{1,0:T(8,128)S(1)}, u32[]{:S(2)}, u32[]{:S(2)}) collective-permute-start(f32[8,128]{1,0:T(8,128)S(1)} %get-tuple-element.12.sums), channel_id=1, source_target_pairs={{0,32},{32,0},{64,96},{96,64},{1,33},{33,1},{65,97},{97,65},{8,40}... | collective-permute-start | bytes 12296 | tf_op jit(solution)/shard_map/ppermute | solution.py:277
  43.0 0.8 collective-permute-done.1.arrived
  43.9 8.7 %all_to_all.22.sums = f32[8,8,128]{2,1,0:T(8,128)S(1)} all-to-all(f32[8,8,128]{2,1,0:T(8,128)S(1)} %shard_map.97), channel_id=1, replica_groups={{0,8,2,10,4,12,6,14},{24,16,26,18,28,20,30,22},{64,72,66,74,68,76,70,78..., dimensions={0} | all-to-all | bytes 65536 | tf_op jit(solution)/shard_map/all_to_all | solution.py:79
  52.6 9.6 %all_to_all.23.got = bf16[8,56,512]{2,1,0:T(8,128)(2,1)S(1)} all-to-all(bf16[8,56,512]{2,1,0:T(8,128)(2,1)S(1)} %shard_map.98), channel_id=1, replica_groups={{0,24,64,88,1,25,65,89},{8,16,72,80,9,17,73,81},{2,26,66,90,3,27,67,91}..., dimensions={0} | all-to-all | bytes 917504 | tf_op jit(solution)/shard_map/all_to_all | solution.py:79
  63.0 4.4 %collective-permute-start.10 = (bf16[8,24,512]{2,1,0:T(8,128)(2,1)S(1)}, bf16[8,24,512]{2,1,0:T(8,128)(2,1)S(1)}, u32[]{:S(2)}, u32[]{:S(2)}) collective-permute-start(bf16[8,24,512]{2,1,0:T(8,128)(2,1)S(1)} %shard_map.100.refs_0_), channel_id=1, source_target_pairs={{10,0},{2,8},{12,2},{4,10},{14,4},{6,12},{8,6},{0,14},{18,24},{26,... | collective-permute-start | bytes 589832 | tf_op jit(solution)/shard_map/ppermute | solution.py:290
  67.4 2.1 %collective-permute-start.7 = (bf16[8,24,512]{2,1,0:T(8,128)(2,1)S(1)}, bf16[8,24,512]{2,1,0:T(8,128)(2,1)S(1)}, u32[]{:S(2)}, u32[]{:S(2)}) collective-permute-start(bf16[8,24,512]{2,1,0:T(8,128)(2,1)S(1)} %shard_map.100.refs_0_), channel_id=1, source_target_pairs={{8,0},{0,8},{10,2},{2,10},{12,4},{4,12},{14,6},{6,14},{16,24},{24,... | collective-permute-start | bytes 589832 | tf_op jit(solution)/shard_map/ppermute | solution.py:290
  69.5 3.2 %collective-permute-start.6 = (bf16[8,24,512]{2,1,0:T(8,128)(2,1)S(1)}, bf16[8,24,512]{2,1,0:T(8,128)(2,1)S(1)}, u32[]{:S(2)}, u32[]{:S(2)}) collective-permute-start(bf16[8,24,512]{2,1,0:T(8,128)(2,1)S(1)} %shard_map.100.refs_0_), channel_id=1, source_target_pairs={{4,0},{12,8},{6,2},{14,10},{0,4},{8,12},{2,6},{10,14},{28,24},{20,... | collective-permute-start | bytes 589832 | tf_op jit(solution)/shard_map/ppermute | solution.py:290
  72.7 2.9 %collective-permute-done.9.refs_0_.refs_1_ = bf16[8,24,512]{2,1,0:T(8,128)(2,1)S(1)} collective-permute-done((bf16[8,24,512]{2,1,0:T(8,128)(2,1)S(1)}, bf16[8,24,512]{2,1,0:T(8,128)(2,1)S(1)}, u32[]{:S(2)}, u32[]{:S(2)}) %collective-permute-start.9) | collective-permute-done | bytes 196640 | tf_op jit(solution)/shard_map/ppermute | solution.py:290
  75.6 2.2 %collective-permute-start.13 = (bf16[3,8,24,512]{3,2,1,0:T(8,128)(2,1)S(1)}, bf16[3,8,24,512]{3,2,1,0:T(8,128)(2,1)S(1)}, u32[]{:S(2)}, u32[]{:S(2)}) collective-permute-start(bf16[3,8,24,512]{3,2,1,0:T(8,128)(2,1)S(1)} %shard_map.102), channel_id=1, source_target_pairs={{0,32},{32,0},{64,96},{96,64},{1,33},{33,1},{65,97},{97,65},{8,40}... | collective-permute-start | bytes 1769480 | tf_op jit(solution)/shard_map/ppermute | solution.py:290
  78.6 0.9 %collective-permute-start.2 = (bf16[8,24,512]{2,1,0:T(8,128)(2,1)S(1)}, bf16[8,24,512]{2,1,0:T(8,128)(2,1)S(1)}, u32[]{:S(2)}, u32[]{:S(2)}) collective-permute-start(bf16[8,24,512]{2,1,0:T(8,128)(2,1)S(1)} %shard_map.100.refs_0_), channel_id=1, source_target_pairs={{6,0},{14,8},{0,2},{8,10},{2,4},{10,12},{4,6},{12,14},{30,24},{22,... | collective-permute-start | bytes 589832 | tf_op jit(solution)/shard_map/ppermute | solution.py:290
  80.2 2.5 %collective-permute-done.3.refs_0_ = bf16[8,24,512]{2,1,0:T(8,128)(2,1)S(1)} collective-permute-done((bf16[8,24,512]{2,1,0:T(8,128)(2,1)S(1)}, bf16[8,24,512]{2,1,0:T(8,128)(2,1)S(1)}, u32[]{:S(2)}, u32[]{:S(2)}) %collective-permute-start.3) | collective-permute-done | bytes 196640 | tf_op jit(solution)/shard_map/ppermute | solution.py:290
  82.7 0.9 %collective-permute-start.4 = (bf16[8,24,512]{2,1,0:T(8,128)(2,1)S(1)}, bf16[8,24,512]{2,1,0:T(8,128)(2,1)S(1)}, u32[]{:S(2)}, u32[]{:S(2)}) collective-permute-start(bf16[8,24,512]{2,1,0:T(8,128)(2,1)S(1)} %collective-permute-done.3.refs_0_), channel_id=1, source_target_pairs={{0,32},{32,0},{64,96},{96,64},{1,33},{33,1},{65,97},{97,65},{8,40}... | collective-permute-start | bytes 589832 | tf_op jit(solution)/shard_map/ppermute | solution.py:290
  83.6 1.1 %collective-permute-done.2.refs_0_ = bf16[8,24,512]{2,1,0:T(8,128)(2,1)S(1)} collective-permute-done((bf16[8,24,512]{2,1,0:T(8,128)(2,1)S(1)}, bf16[8,24,512]{2,1,0:T(8,128)(2,1)S(1)}, u32[]{:S(2)}, u32[]{:S(2)}) %collective-permute-start.2) | collective-permute-done | bytes 196640 | tf_op jit(solution)/shard_map/ppermute | solution.py:290
  84.7 1.3 %collective-permute-start.5 = (bf16[8,24,512]{2,1,0:T(8,128)(2,1)S(1)}, bf16[8,24,512]{2,1,0:T(8,128)(2,1)S(1)}, u32[]{:S(2)}, u32[]{:S(2)}) collective-permute-start(bf16[8,24,512]{2,1,0:T(8,128)(2,1)S(1)} %collective-permute-done.2.refs_0_), channel_id=1, source_target_pairs={{0,32},{32,0},{64,96},{96,64},{1,33},{33,1},{65,97},{97,65},{8,40}... | collective-permute-start | bytes 589832 | tf_op jit(solution)/shard_map/ppermute | solution.py:290
  86.0 0.9 shard_map.99
  86.9 1.3 %shard_map.103.refs_2_ = bf16[128,24,512]{2,1,0:T(8,128)(2,1)} custom-call(s32[1]{0:T(128)} %bitcast.me, bf16[8,24,512]{2,1,0:T(8,128)(2,1)S(1)} %shard_map.100.refs_0_, bf16[8,24,512]{2,1,0:T(8,128)(2,1)S(1)} %collective-permute-done.9.refs_0_.refs_1_, bf16[8,24,512]{2,1,0:T(8,128)(2,1)S(1)} %collective-permute-done.10.refs_1_.refs_2_, ...), custom_call_target="tpu_custom_call" | custom-call | tf_op jit(solution)/shard_map/pallas_call | solution.py:299
  89.0 0.8 shard_map.105
  (30 shorter events, 3.9 us)
Async XLA Ops:
  2.0 4.5 %collective-permute-start = (bf16[64,24,512]{2,1,0:T(8,128)(2,1)S(1)}, bf16[64,24,512]{2,1,0:T(8,128)(2,1)S(1)}, u32[]{:S(2)}, u32[]{:S(2)}) collective-permute-start(bf16[64,24,512]{2,1,0:T(8,128)(2,1)S(1)} %shard_map.93), channel_id=1, source_target_pairs={{0,32},{32,0},{64,96},{96,64},{1,33},{33,1},{65,97},{97,65},{8,40}... | collective-permute-start | bytes 4718600 | tf_op jit(solution)/shard_map/ppermute | solution.py:265
  28.9 9.6 %copy-start = (f32[24,512]{1,0:T(8,128)S(1)}, f32[24,512]{1,0:T(8,128)}, u32[]{:S(2)}) copy-start(f32[24,512]{1,0:T(8,128)} %weights.5) | copy-start | bytes 147460
  28.9 9.6 %copy-start.1 = (f32[24,512]{1,0:T(8,128)S(1)}, f32[24,512]{1,0:T(8,128)}, u32[]{:S(2)}) copy-start(f32[24,512]{1,0:T(8,128)} %first.1) | copy-start | bytes 147460
  28.9 9.6 %copy-start.2 = (f32[24,512]{1,0:T(8,128)S(1)}, f32[24,512]{1,0:T(8,128)}, u32[]{:S(2)}) copy-start(f32[24,512]{1,0:T(8,128)} %second.1) | copy-start | bytes 147460
  28.9 9.6 %copy-start.3 = (s32[24]{0:T(128)S(1)}, s32[24]{0:T(128)}, u32[]{:S(2)}) copy-start(s32[24]{0:T(128)} %ids.1) | copy-start | bytes 292
  39.7 4.2 %collective-permute-start.1 = (f32[8,128]{1,0:T(8,128)S(1)}, f32[8,128]{1,0:T(8,128)S(1)}, u32[]{:S(2)}, u32[]{:S(2)}) collective-permute-start(f32[8,128]{1,0:T(8,128)S(1)} %get-tuple-element.12.sums), channel_id=1, source_target_pairs={{0,32},{32,0},{64,96},{96,64},{1,33},{33,1},{65,97},{97,65},{8,40}... | collective-permute-start | bytes 12296 | tf_op jit(solution)/shard_map/ppermute | solution.py:277
  62.5 10.2 %collective-permute-start.11 = (bf16[8,24,512]{2,1,0:T(8,128)(2,1)S(1)}, bf16[8,24,512]{2,1,0:T(8,128)(2,1)S(1)}, u32[]{:S(2)}, u32[]{:S(2)}) collective-permute-start(bf16[8,24,512]{2,1,0:T(8,128)(2,1)S(1)} %shard_map.100.refs_0_), channel_id=1, source_target_pairs={{14,0},{6,8},{8,2},{0,10},{10,4},{2,12},{12,6},{4,14},{22,24},{30,... | collective-permute-start | bytes 589832 | tf_op jit(solution)/shard_map/ppermute | solution.py:290
  63.0 9.7 %collective-permute-start.10 = (bf16[8,24,512]{2,1,0:T(8,128)(2,1)S(1)}, bf16[8,24,512]{2,1,0:T(8,128)(2,1)S(1)}, u32[]{:S(2)}, u32[]{:S(2)}) collective-permute-start(bf16[8,24,512]{2,1,0:T(8,128)(2,1)S(1)} %shard_map.100.refs_0_), channel_id=1, source_target_pairs={{10,0},{2,8},{12,2},{4,10},{14,4},{6,12},{8,6},{0,14},{18,24},{26,... | collective-permute-start | bytes 589832 | tf_op jit(solution)/shard_map/ppermute | solution.py:290
  67.4 8.2 %collective-permute-start.9 = (bf16[8,24,512]{2,1,0:T(8,128)(2,1)S(1)}, bf16[8,24,512]{2,1,0:T(8,128)(2,1)S(1)}, u32[]{:S(2)}, u32[]{:S(2)}) collective-permute-start(bf16[8,24,512]{2,1,0:T(8,128)(2,1)S(1)} %shard_map.100.refs_0_), channel_id=1, source_target_pairs={{12,0},{4,8},{14,2},{6,10},{8,4},{0,12},{10,6},{2,14},{20,24},{28,... | collective-permute-start | bytes 589832 | tf_op jit(solution)/shard_map/ppermute | solution.py:290
  67.4 11.1 %collective-permute-start.7 = (bf16[8,24,512]{2,1,0:T(8,128)(2,1)S(1)}, bf16[8,24,512]{2,1,0:T(8,128)(2,1)S(1)}, u32[]{:S(2)}, u32[]{:S(2)}) collective-permute-start(bf16[8,24,512]{2,1,0:T(8,128)(2,1)S(1)} %shard_map.100.refs_0_), channel_id=1, source_target_pairs={{8,0},{0,8},{10,2},{2,10},{12,4},{4,12},{14,6},{6,14},{16,24},{24,... | collective-permute-start | bytes 589832 | tf_op jit(solution)/shard_map/ppermute | solution.py:290
  69.5 9.0 %collective-permute-start.6 = (bf16[8,24,512]{2,1,0:T(8,128)(2,1)S(1)}, bf16[8,24,512]{2,1,0:T(8,128)(2,1)S(1)}, u32[]{:S(2)}, u32[]{:S(2)}) collective-permute-start(bf16[8,24,512]{2,1,0:T(8,128)(2,1)S(1)} %shard_map.100.refs_0_), channel_id=1, source_target_pairs={{4,0},{12,8},{6,2},{14,10},{0,4},{8,12},{2,6},{10,14},{28,24},{20,... | collective-permute-start | bytes 589832 | tf_op jit(solution)/shard_map/ppermute | solution.py:290
  75.6 11.2 %collective-permute-start.13 = (bf16[3,8,24,512]{3,2,1,0:T(8,128)(2,1)S(1)}, bf16[3,8,24,512]{3,2,1,0:T(8,128)(2,1)S(1)}, u32[]{:S(2)}, u32[]{:S(2)}) collective-permute-start(bf16[3,8,24,512]{3,2,1,0:T(8,128)(2,1)S(1)} %shard_map.102), channel_id=1, source_target_pairs={{0,32},{32,0},{64,96},{96,64},{1,33},{33,1},{65,97},{97,65},{8,40}... | collective-permute-start | bytes 1769480 | tf_op jit(solution)/shard_map/ppermute | solution.py:290
  77.9 4.8 %collective-permute-start.3 = (bf16[8,24,512]{2,1,0:T(8,128)(2,1)S(1)}, bf16[8,24,512]{2,1,0:T(8,128)(2,1)S(1)}, u32[]{:S(2)}, u32[]{:S(2)}) collective-permute-start(bf16[8,24,512]{2,1,0:T(8,128)(2,1)S(1)} %shard_map.100.refs_0_), channel_id=1, source_target_pairs={{2,0},{10,8},{4,2},{12,10},{6,4},{14,12},{0,6},{8,14},{26,24},{18,... | collective-permute-start | bytes 589832 | tf_op jit(solution)/shard_map/ppermute | solution.py:290
  78.5 9.6 %collective-permute-start.8 = (bf16[2,8,24,512]{3,2,1,0:T(8,128)(2,1)S(1)}, bf16[2,8,24,512]{3,2,1,0:T(8,128)(2,1)S(1)}, u32[]{:S(2)}, u32[]{:S(2)}) collective-permute-start(bf16[2,8,24,512]{3,2,1,0:T(8,128)(2,1)S(1)} %shard_map.101), channel_id=1, source_target_pairs={{0,32},{32,0},{64,96},{96,64},{1,33},{33,1},{65,97},{97,65},{8,40}... | collective-permute-start | bytes 1179656 | tf_op jit(solution)/shard_map/ppermute | solution.py:290
  78.6 6.1 %collective-permute-start.2 = (bf16[8,24,512]{2,1,0:T(8,128)(2,1)S(1)}, bf16[8,24,512]{2,1,0:T(8,128)(2,1)S(1)}, u32[]{:S(2)}, u32[]{:S(2)}) collective-permute-start(bf16[8,24,512]{2,1,0:T(8,128)(2,1)S(1)} %shard_map.100.refs_0_), channel_id=1, source_target_pairs={{6,0},{14,8},{0,2},{8,10},{2,4},{10,12},{4,6},{12,14},{30,24},{22,... | collective-permute-start | bytes 589832 | tf_op jit(solution)/shard_map/ppermute | solution.py:290
  79.5 7.3 %collective-permute-start.12 = (bf16[8,24,512]{2,1,0:T(8,128)(2,1)S(1)}, bf16[8,24,512]{2,1,0:T(8,128)(2,1)S(1)}, u32[]{:S(2)}, u32[]{:S(2)}) collective-permute-start(bf16[8,24,512]{2,1,0:T(8,128)(2,1)S(1)} %shard_map.100.refs_0_), channel_id=1, source_target_pairs={{0,32},{32,0},{64,96},{96,64},{1,33},{33,1},{65,97},{97,65},{8,40}... | collective-permute-start | bytes 589832 | tf_op jit(solution)/shard_map/ppermute | solution.py:290
  82.7 6.3 %collective-permute-start.4 = (bf16[8,24,512]{2,1,0:T(8,128)(2,1)S(1)}, bf16[8,24,512]{2,1,0:T(8,128)(2,1)S(1)}, u32[]{:S(2)}, u32[]{:S(2)}) collective-permute-start(bf16[8,24,512]{2,1,0:T(8,128)(2,1)S(1)} %collective-permute-done.3.refs_0_), channel_id=1, source_target_pairs={{0,32},{32,0},{64,96},{96,64},{1,33},{33,1},{65,97},{97,65},{8,40}... | collective-permute-start | bytes 589832 | tf_op jit(solution)/shard_map/ppermute | solution.py:290
  84.7 4.3 %collective-permute-start.5 = (bf16[8,24,512]{2,1,0:T(8,128)(2,1)S(1)}, bf16[8,24,512]{2,1,0:T(8,128)(2,1)S(1)}, u32[]{:S(2)}, u32[]{:S(2)}) collective-permute-start(bf16[8,24,512]{2,1,0:T(8,128)(2,1)S(1)} %collective-permute-done.2.refs_0_), channel_id=1, source_target_pairs={{0,32},{32,0},{64,96},{96,64},{1,33},{33,1},{65,97},{97,65},{8,40}... | collective-permute-start | bytes 589832 | tf_op jit(solution)/shard_map/ppermute | solution.py:290
where the time goes:
time: 91.2 us; the launch traced here: 89.8 us
  blocking collectives  49.4 us (54%)
  starting transfers between devices  21.7 us (24%)
  Pallas kernels  8.96 us (10%)
  waiting for transfers between devices  8.96 us (10%)
    all_to_all x4, blocking collectives, exchange(): lax.all_to_all(value, 'i', 0, 0, axis_index_groups=groups, tiled=True)  49.4 us
    ppermute x12, starting transfers between devices, send(): return lax.ppermute(value, 'i', pairs)  16.9 us
    ppermute x12, waiting for transfers between devices, send(): return lax.ppermute(value, 'i', pairs)  6.49 us
    ppermute x1, starting transfers between devices, on_device(): arrived = lax.ppermute(sums, 'i', CORE_SWAP)  3.35 us
    pallas_call x3, Pallas kernels, place(): kernel(functools.partial(place_kernel, chunks=chunks, first=first), [SMEM...  2.9 us
    pallas_call x2, Pallas kernels, on_device(): kernel(functools.partial(take_kernel, other=other), [SMEM, HBM], VMEM, ha...  2.78 us
  transfers between devices with their start and end apart: 14, of which 5 were waited for; matrix products, arithmetic and copies ran while one was open for 0% of the time, Pallas kernels for 5%

commit v1 on v0

v1 whole, which is shorter than its diff:
```python
import functools

import jax
import jax.numpy as jnp
import numpy as np
from jax import lax
from jax.experimental import pallas as pl
from jax.experimental.pallas import tpu as pltpu
from jax.sharding import Mesh
from jax.sharding import PartitionSpec as P


decay_first = 0.9
decay_second = 0.999
epsilon = 1e-06
weight_decay = 0.01
step_size = 0.05


ROWS = 24
COLS = 512
CHIPS = 64
GROUP = 8
F32 = jnp.float32
BF16 = jnp.bfloat16

NUMBER = np.arange(2 * CHIPS).reshape(2, 2, 4, 4, 2)
PLACE = NUMBER.transpose(3, 2, 4, 0, 1).reshape(4, 4, 4, 2)

CORE_SWAP = [(int(a), int(b)) for pair in PLACE.reshape(CHIPS, 2) for a, b in (pair, pair[::-1])]


def grouping():
    grid = np.zeros((2, GROUP, GROUP), int)
    for core in range(2):
        for a in range(GROUP):
            for b in range(GROUP):
                x, low, z, high = (a >> 1, a & 1, b >> 1, b & 1) if core == 0 else (b >> 1, b & 1, a >> 1, a & 1)
                grid[core, a, b] = PLACE[x, 2 * high + (low ^ high), z, core]
    wide = [grid[core, :, b].tolist() for core in range(2) for b in range(GROUP)]
    narrow = [grid[core, a, :].tolist() for core in range(2) for a in range(GROUP)]
    return wide, narrow


WIDE, NARROW = grouping()


def place_of(device):
    return device >> 6, (device >> 5) & 1, (device >> 3) & 3, (device >> 1) & 3, device & 1


def wide_place(device):
    z_lo, core, y, x, z_hi = place_of(device)
    return jnp.where(core == 0, 2 * x + ((y ^ (y >> 1)) & 1), 2 * (2 * z_hi + z_lo) + (y >> 1))


OFFSETS = ((2, 1), (3, 1), (1, 1), (2, 0), (0, 1), (3, 0), (1, 0))
OWN = (0, 0)


def source_place(a, offset):
    ring, pair = offset
    return ((((a >> 1) + 4 - ring) & 3) << 1) + ((a & 1) ^ pair)


def target_place(a, offset):
    ring, pair = offset
    return ((((a >> 1) + ring) & 3) << 1) + ((a & 1) ^ pair)


def wide_shift(offset):
    return [(group[source_place(a, offset)], group[a]) for group in WIDE for a in range(GROUP)]


def owner_of(core, a, b):
    first = core == 0
    p = jnp.where(first, a, b)
    q = jnp.where(first, b, a)
    x, z = p >> 1, q >> 1
    y = 2 * (q & 1) + ((p ^ q) & 1)
    return ((z & 1) << 6) + (core << 5) + (y << 3) + (x << 1) + (z >> 1)


def exchange(value, groups):
    return lax.all_to_all(value, "i", 0, 0, axis_index_groups=groups, tiled=True)


def lane_index(rows):
    return lax.broadcasted_iota(jnp.int32, (rows, 128), 1)


def before_kernel(weights, ids, tensor, sums):
    row = lax.broadcasted_iota(jnp.int32, (ROWS, 128), 0)
    of_row = jnp.zeros((ROWS, 128), jnp.int32)
    for k in range(ROWS):
        of_row = jnp.where(row == k, ids[k], of_row)
    tensor[...] = of_row
    lane = lane_index(ROWS)
    kind = lane // 4
    w = weights[...]
    w_sq = jnp.sum(w * w, axis=1, keepdims=True)
    by_kind = jnp.where(kind == 0, w_sq, jnp.where(kind == 2, float(COLS), 0.0))
    per_tensor = jnp.sum(jnp.where(of_row == lane % 4, by_kind, 0.0), axis=0, keepdims=True)
    sums[...] = jnp.broadcast_to(per_tensor, (8, 128))


def update_kernel(parts, weights, first, second, tensor, base, new_first, new_second, update, sums):
    summed = parts[0].astype(F32)
    for k in range(1, GROUP):
        summed = summed + parts[k].astype(F32)
    m = decay_first * first[...] + (1.0 - decay_first) * summed
    v = decay_second * second[...] + (1.0 - decay_second) * summed * summed
    u = m / (jnp.sqrt(v) + epsilon) + weight_decay * weights[...]
    new_first[...] = m
    new_second[...] = v
    update[...] = u
    u_sq = jnp.sum(u * u, axis=1, keepdims=True)
    here = tensor[...] + 4 == lane_index(ROWS)
    per_tensor = jnp.sum(jnp.where(here, u_sq, 0.0), axis=0, keepdims=True)
    sums[...] = base[...] + jnp.broadcast_to(per_tensor, (8, 128))


PAY = 2 * ROWS + 8


def pay_kernel(update, weights, sums, pay):
    total = sums[0, 0:1, :]
    for k in range(1, GROUP):
        total = total + sums[k, 0:1, :]
    high = total.astype(BF16)
    rest = total - high.astype(F32)
    mid = rest.astype(BF16)
    low = (rest - mid.astype(F32)).astype(BF16)
    row = lax.broadcasted_iota(jnp.int32, (8, 128), 0)
    three = jnp.where(
        row == 0, high.astype(F32), jnp.where(row == 1, mid.astype(F32), jnp.where(row == 2, low.astype(F32), 0.0))
    )
    three = jnp.concatenate([three, jnp.zeros((8, COLS - 128), F32)], axis=1)
    one = jnp.concatenate([update[...], weights[...], three], axis=0).astype(BF16)
    for k in range(GROUP):
        pay[k] = one


def trust_and_runs(got):
    total = jnp.zeros((1, 128), F32)
    for k in range(GROUP):
        three = got[k, 2 * ROWS :, 0:128].astype(F32)
        total = total + ((three[0:1] + three[1:2]) + three[2:3])
    update_sq = pltpu.roll(total, 124, 1)
    count = pltpu.roll(total, 120, 1)
    lane = lane_index(1)
    used = lane < 4
    trust = jnp.where(used, jnp.sqrt(total / (update_sq + count)), 0.0)
    rows = jnp.where(used, count * (1.0 / COLS), 0.0)
    start = jnp.zeros((1, 128), F32)
    for k in range(1, 4):
        start = start + jnp.where(lane >= k, pltpu.roll(rows, k, 1), 0.0)
    return trust, start, jnp.where(used, start + rows, -1.0)


def row_trust(first_row, trust, start, end):
    row = (lax.broadcasted_iota(jnp.int32, (ROWS, 128), 0) + first_row).astype(F32)
    here = jnp.logical_and(row >= start, row < end)
    return jnp.sum(jnp.where(here, trust, 0.0), axis=1, keepdims=True)


def params_kernel(me, got, update, weights, params, new_master, scaled_update):
    trust, start, end = trust_and_runs(got)
    core = (me[0] >> 5) & 1
    place = wide_place(me[0])
    for b in range(GROUP):
        factor = row_trust(owner_of(core, place, b) * ROWS, trust, start, end)
        block = got[b, ROWS : 2 * ROWS].astype(F32) - step_size * (factor * got[b, 0:ROWS].astype(F32))
        params[b] = block.astype(BF16)
    scaled = row_trust(me[0] * ROWS, trust, start, end) * update[...]
    scaled_update[...] = scaled
    new_master[...] = weights[...] - step_size * scaled


def take_kernel(me, gradients, taken, done, *, other, offsets):
    device = me[0] ^ (32 if other else 0)
    core = (device >> 5) & 1
    for j, offset in enumerate(offsets):
        a = target_place(wide_place(device), offset)
        for b in range(GROUP):
            pltpu.make_async_copy(gradients.at[owner_of(core, a, b)], taken.at[j, b], done).start()
    pltpu.make_async_copy(taken, taken, done).wait()


def add_kernel(kept, arrived, *both):
    for j, out in enumerate(both):
        out[...] = kept[j] + arrived[j]


def total_kernel(*refs):
    for b in range(GROUP):
        summed = refs[0][b].astype(F32)
        for part in refs[1:-1]:
            summed = summed + part[b].astype(F32)
        refs[-1][b] = summed.astype(BF16)


def chip_sums_kernel(sums, arrived, out):
    both = sums[...] + arrived[...]
    for k in range(GROUP):
        out[k] = both


def join_kernel(*refs):
    for k, part in enumerate(refs[:-1]):
        refs[-1][k] = part[...]


def place_kernel(me, *refs, arrays, chunks, rows=0):
    blocks, whole = refs[:arrays], refs[arrays : arrays + rows]
    scratch = 1 + (rows > 0)
    outs = refs[len(refs) - scratch - 1 - rows : len(refs) - scratch]
    out, done = outs[0], refs[len(refs) - scratch]
    copies = [pltpu.make_async_copy(whole[k], outs[1 + k], refs[-1].at[k]) for k in range(rows)]
    for array, index, other, offset in chunks:
        device = me[0] ^ (32 if other else 0)
        core = (device >> 5) & 1
        a = source_place(wide_place(device), offset)
        part = blocks[array] if index is None else blocks[array].at[index]
        for b in range(GROUP):
            pltpu.make_async_copy(part.at[b], out.at[owner_of(core, a, b)], done).start()
    for copy in copies:
        copy.start()
    total = len(chunks) * GROUP
    pltpu.make_async_copy(out.at[pl.ds(0, total)], out.at[pl.ds(0, total)], done).wait()
    for copy in copies:
        copy.wait()


SMEM = pl.BlockSpec(memory_space=pltpu.SMEM)
VMEM = pl.BlockSpec(memory_space=pltpu.VMEM)
HBM = pl.BlockSpec(memory_space=pltpu.HBM)


def of(shape, dtype):
    return jax.ShapeDtypeStruct(shape, dtype)


def kernel(body, ins, outs, shapes, limit=8, **more):
    return pl.pallas_call(
        body,
        out_shape=shapes,
        in_specs=ins,
        out_specs=outs,
        compiler_params=pltpu.CompilerParams(vmem_limit_bytes=limit * 2**20),
        **more,
    )


def on_device(gradients, master_weights, first_moment, second_moment, tensor_ids):
    me = lax.axis_index("i").astype(jnp.int32).reshape(1)
    own_f32 = pltpu.VMEM((ROWS, COLS), F32)
    chunk = pltpu.VMEM((GROUP, ROWS, COLS), BF16)
    copied = dict(scratch_shapes=[pltpu.SemaphoreType.DMA])

    def send(value, pairs):
        return lax.ppermute(value, "i", pairs)

    blocks = pltpu.with_memory_space_constraint(gradients.reshape(2 * CHIPS, ROWS, COLS), pltpu.HBM)
    halves = (OFFSETS[:4], OFFSETS[4:] + (OWN,))

    def take(other, offsets):
        body = functools.partial(take_kernel, other=other, offsets=offsets)
        return kernel(body, [SMEM, HBM], VMEM, pltpu.VMEM((4, GROUP, ROWS, COLS), BF16), **copied)(me, blocks)

    sent = [take(True, offsets) for offsets in halves]
    arrived = [send(sent[k], CORE_SWAP) for k in range(2)]
    kept = [take(False, offsets) for offsets in halves]
    chunks = []
    for k in range(2):
        chunks += kernel(add_kernel, [VMEM] * 2, [VMEM] * 4, [chunk] * 4)(kept[k], arrived[k])
    tensor, sums = kernel(
        before_kernel, [VMEM, SMEM], (VMEM, VMEM), (pltpu.VMEM((ROWS, 128), jnp.int32), pltpu.VMEM((8, 128), F32))
    )(master_weights, tensor_ids)
    wide = [send(chunks[k], wide_shift(offset)) for k, offset in enumerate(OFFSETS)]
    total = kernel(total_kernel, [VMEM] * 8, VMEM, chunk)(chunks[7], *wide)
    parts = exchange(total, NARROW)

    new_first, new_second, update, sums = kernel(
        update_kernel, [VMEM] * 6, (VMEM,) * 4, (own_f32, own_f32, own_f32, pltpu.VMEM((8, 128), F32))
    )(parts, master_weights, first_moment, second_moment, tensor, sums)

    arrived = lax.ppermute(sums, "i", CORE_SWAP)
    sums = kernel(chip_sums_kernel, [VMEM] * 2, VMEM, pltpu.VMEM((GROUP, 8, 128), F32))(sums, arrived)
    sums = exchange(sums, WIDE)
    pay = kernel(pay_kernel, [VMEM] * 3, VMEM, pltpu.VMEM((GROUP, PAY, COLS), BF16))(update, master_weights, sums)
    got = exchange(pay, NARROW)

    params, new_master, scaled_update = kernel(
        params_kernel, [SMEM] + [VMEM] * 3, (VMEM,) * 3, (chunk, own_f32, own_f32)
    )(me, got, update, master_weights)
    join = lambda *parts: kernel(
        join_kernel, [VMEM] * len(parts), VMEM, pltpu.VMEM((len(parts), GROUP, ROWS, COLS), BF16)
    )(*parts)
    every = of((2 * CHIPS, ROWS, COLS), BF16)

    def place(arrays, chunks, before=None, rows=()):
        first = before is None
        count = len(arrays) + len(rows)
        return kernel(
            functools.partial(place_kernel, arrays=len(arrays), chunks=chunks, rows=len(rows)),
            [SMEM] + [VMEM] * count + ([] if first else [HBM]),
            [HBM] * (1 + len(rows)),
            [every] + [of((ROWS, COLS), F32)] * len(rows),
            input_output_aliases={} if first else {1 + count: 0},
            scratch_shapes=[pltpu.SemaphoreType.DMA] + ([pltpu.SemaphoreType.DMA((len(rows),))] if rows else []),
        )(me, *arrays, *rows, *(() if first else (before,)))

    wide = [send(params, wide_shift(offset)) for offset in OFFSETS]
    other_0 = send(join(params, *wide[0:3]), CORE_SWAP)
    other_1 = send(join(*wide[3:5]), CORE_SWAP)
    other_2 = send(join(*wide[5:7]), CORE_SWAP)
    gathered, new_first, new_second, new_master, scaled_update = place(
        [params, *wide[0:5], other_0],
        [(0, None, False, OWN)]
        + [(1 + k, None, False, OFFSETS[k]) for k in range(5)]
        + [(6, 0, True, OWN)]
        + [(6, 1 + k, True, OFFSETS[k]) for k in range(3)],
        rows=(new_first, new_second, new_master, scaled_update),
    )
    (gathered,) = place(
        [*wide[5:7], other_1, other_2],
        [(k, None, False, OFFSETS[5 + k]) for k in range(2)]
        + [(2, k, True, OFFSETS[3 + k]) for k in range(2)]
        + [(3, k, True, OFFSETS[5 + k]) for k in range(2)],
        gathered,
    )
    gathered = gathered.reshape(2 * CHIPS * ROWS, COLS)
    return (new_master, new_first, new_second, scaled_update, gathered)


def solution(mesh):
    flat = Mesh(mesh.devices.reshape(2 * CHIPS), ("i",))
    return jax.shard_map(
        on_device,
        mesh=flat,
        in_specs=(P("i", None, None), P("i", None), P("i", None), P("i", None), P("i")),
        out_specs=(P("i", None), P("i", None), P("i", None), P("i", None), P()),
        check_vma=False,
    )
```

time: 91.2 us -> 91.8 us (level)
  blocking collectives: 49.4 us -> 19 us
  waiting for transfers between devices: 8.96 us -> 25.1 us
  starting transfers between devices: 21.7 us -> 37.2 us
    all_to_all x4 -> x2, blocking collectives: 49.4 us -> 19 us  [exchange(): lax.all_to_all(value, 'i', 0, 0, axis_index_groups=groups, tiled=True)]
    ppermute x12 -> x19, waiting for transfers between devices: 6.49 us -> 19.4 us  [send(): return lax.ppermute(value, 'i', pairs)]
    ppermute x12 -> x19, starting transfers between devices: 16.9 us -> 28.6 us  [send(): return lax.ppermute(value, 'i', pairs)]
    all_to_all x0 -> x1, waiting for transfers between devices: none -> 4.87 us  [exchange(): lax.all_to_all(value, 'i', 0, 0, axis_index_groups=groups, tiled=True)]
    all_to_all x0 -> x1, starting transfers between devices: none -> 4.02 us  [exchange(): lax.all_to_all(value, 'i', 0, 0, axis_index_groups=groups, tiled=True)]
    ppermute x1 -> x0, waiting for transfers between devices: 1.64 us -> none  [on_device(): arrived = lax.ppermute(sent, 'i', CORE_SWAP)]
    ppermute x1 -> x0, starting transfers between devices: 1.46 us -> none  [on_device(): arrived = lax.ppermute(sent, 'i', CORE_SWAP)]
    ppermute x1, starting transfers between devices: 3.35 us -> 4.61 us  [on_device(): arrived = lax.ppermute(sums, 'i', CORE_SWAP)]
  transfers between devices with their start and end apart: 14 -> 21, of which waited for: 5 -> 11; matrix products, arithmetic and copies ran while one was open for 0% -> 0% of each run, Pallas kernels for 5% -> 6%
where the time goes in v1:
time: 91.8 us; the launch traced here: 91.2 us
  starting transfers between devices  37.2 us (41%)
  waiting for transfers between devices  25.1 us (27%)
  blocking collectives  19 us (21%)
  Pallas kernels  9.04 us (10%)
    ppermute x19, starting transfers between devices, send(): return lax.ppermute(value, 'i', pairs)  28.6 us
    ppermute x19, waiting for transfers between devices, send(): return lax.ppermute(value, 'i', pairs)  19.4 us
    all_to_all x2, blocking collectives, exchange(): lax.all_to_all(value, 'i', 0, 0, axis_index_groups=groups, tiled=True)  19 us
    all_to_all x1, waiting for transfers between devices, exchange(): lax.all_to_all(value, 'i', 0, 0, axis_index_groups=groups, tiled=True)  4.87 us
    ppermute x1, starting transfers between devices, on_device(): arrived = lax.ppermute(sums, 'i', CORE_SWAP)  4.61 us
    pallas_call x4, Pallas kernels, take(): kernel(body, [SMEM, HBM], VMEM, pltpu.VMEM((4, GROUP, ROWS, COLS), BF16),...  4.42 us
    all_to_all x1, starting transfers between devices, exchange(): lax.all_to_all(value, 'i', 0, 0, axis_index_groups=groups, tiled=True)  4.02 us
    pallas_call x2, Pallas kernels, place(): kernel(functools.partial(place_kernel, arrays=len(arrays), chunks=chunks,...  2.35 us
  transfers between devices with their start and end apart: 21, of which 11 were waited for; matrix products, arithmetic and copies ran while one was open for 0% of the time, Pallas kernels for 6%

profile of v1, /device:TPU:1, one launch (start us, length us, event | category | flops | bytes accessed | tf_op | source)
XLA Modules:
  0.0 91.2 jit_solution(17558598071404093359)
XLA Ops:
  0.6 1.2 %shard_map.93 = bf16[4,8,24,512]{3,2,1,0:T(8,128)(2,1)S(1)} custom-call(s32[1]{0:T(128)} %bitcast.me, bf16[128,24,512]{2,1,0:T(8,128)(2,1)} %bitcast.3), custom_call_target="tpu_custom_call" | custom-call | tf_op jit(solution)/shard_map/pallas_call | solution.py:269
  1.8 1.5 %collective-permute-start = (bf16[4,8,24,512]{3,2,1,0:T(8,128)(2,1)S(1)}, bf16[4,8,24,512]{3,2,1,0:T(8,128)(2,1)S(1)}, u32[]{:S(2)}, u32[]{:S(2)}) collective-permute-start(bf16[4,8,24,512]{3,2,1,0:T(8,128)(2,1)S(1)} %shard_map.93), channel_id=1, source_target_pairs={{0,32},{32,0},{64,96},{96,64},{1,33},{33,1},{65,97},{97,65},{8,40}... | collective-permute-start | bytes 2359304 | tf_op jit(solution)/shard_map/ppermute | solution.py:262
  5.7 2.9 %collective-permute-start.6 = (bf16[8,24,512]{2,1,0:T(8,128)(2,1)S(1)}, bf16[8,24,512]{2,1,0:T(8,128)(2,1)S(1)}, u32[]{:S(2)}, u32[]{:S(2)}) collective-permute-start(bf16[8,24,512]{2,1,0:T(8,128)(2,1)S(1)} %get-tuple-element.32), channel_id=1, source_target_pairs={{8,0},{0,8},{10,2},{2,10},{12,4},{4,12},{14,6},{6,14},{16,24},{24,... | collective-permute-start | bytes 589832 | tf_op jit(solution)/shard_map/ppermute | solution.py:262
  8.7 3.8 %collective-permute-start.7 = (bf16[8,24,512]{2,1,0:T(8,128)(2,1)S(1)}, bf16[8,24,512]{2,1,0:T(8,128)(2,1)S(1)}, u32[]{:S(2)}, u32[]{:S(2)}) collective-permute-start(bf16[8,24,512]{2,1,0:T(8,128)(2,1)S(1)} %get-tuple-element.33), channel_id=1, source_target_pairs={{2,0},{10,8},{4,2},{12,10},{6,4},{14,12},{0,6},{8,14},{26,24},{18,... | collective-permute-start | bytes 589832 | tf_op jit(solution)/shard_map/ppermute | solution.py:262
  13.8 1.1 %collective-permute-start.2 = (bf16[8,24,512]{2,1,0:T(8,128)(2,1)S(1)}, bf16[8,24,512]{2,1,0:T(8,128)(2,1)S(1)}, u32[]{:S(2)}, u32[]{:S(2)}) collective-permute-start(bf16[8,24,512]{2,1,0:T(8,128)(2,1)S(1)} %get-tuple-element.28), channel_id=1, source_target_pairs={{12,0},{4,8},{14,2},{6,10},{8,4},{0,12},{10,6},{2,14},{20,24},{28,... | collective-permute-start | bytes 589832 | tf_op jit(solution)/shard_map/ppermute | solution.py:262
  14.9 3.0 %collective-permute-start.3 = (bf16[8,24,512]{2,1,0:T(8,128)(2,1)S(1)}, bf16[8,24,512]{2,1,0:T(8,128)(2,1)S(1)}, u32[]{:S(2)}, u32[]{:S(2)}) collective-permute-start(bf16[8,24,512]{2,1,0:T(8,128)(2,1)S(1)} %get-tuple-element.29), channel_id=1, source_target_pairs={{10,0},{2,8},{12,2},{4,10},{14,4},{6,12},{8,6},{0,14},{18,24},{26,... | collective-permute-start | bytes 589832 | tf_op jit(solution)/shard_map/ppermute | solution.py:262
  17.9 1.3 %collective-permute-start.4 = (bf16[8,24,512]{2,1,0:T(8,128)(2,1)S(1)}, bf16[8,24,512]{2,1,0:T(8,128)(2,1)S(1)}, u32[]{:S(2)}, u32[]{:S(2)}) collective-permute-start(bf16[8,24,512]{2,1,0:T(8,128)(2,1)S(1)} %get-tuple-element.30), channel_id=1, source_target_pairs={{14,0},{6,8},{8,2},{0,10},{10,4},{2,12},{12,6},{4,14},{22,24},{30,... | collective-permute-start | bytes 589832 | tf_op jit(solution)/shard_map/ppermute | solution.py:262
  19.2 1.9 %collective-permute-start.5 = (bf16[8,24,512]{2,1,0:T(8,128)(2,1)S(1)}, bf16[8,24,512]{2,1,0:T(8,128)(2,1)S(1)}, u32[]{:S(2)}, u32[]{:S(2)}) collective-permute-start(bf16[8,24,512]{2,1,0:T(8,128)(2,1)S(1)} %get-tuple-element.31), channel_id=1, source_target_pairs={{4,0},{12,8},{6,2},{14,10},{0,4},{8,12},{2,6},{10,14},{28,24},{20,... | collective-permute-start | bytes 589832 | tf_op jit(solution)/shard_map/ppermute | solution.py:262
  22.0 3.2 %collective-permute-done.3.refs_2_ = bf16[8,24,512]{2,1,0:T(8,128)(2,1)S(1)} collective-permute-done((bf16[8,24,512]{2,1,0:T(8,128)(2,1)S(1)}, bf16[8,24,512]{2,1,0:T(8,128)(2,1)S(1)}, u32[]{:S(2)}, u32[]{:S(2)}) %collective-permute-start.3) | collective-permute-done | bytes 196640 | tf_op jit(solution)/shard_map/ppermute | solution.py:262
  25.2 1.1 %collective-permute-done.4.refs_3_ = bf16[8,24,512]{2,1,0:T(8,128)(2,1)S(1)} collective-permute-done((bf16[8,24,512]{2,1,0:T(8,128)(2,1)S(1)}, bf16[8,24,512]{2,1,0:T(8,128)(2,1)S(1)}, u32[]{:S(2)}, u32[]{:S(2)}) %collective-permute-start.4) | collective-permute-done | bytes 196640 | tf_op jit(solution)/shard_map/ppermute | solution.py:262
  28.2 4.0 %all-to-all-start = ((bf16[8,24,512]{2,1,0:T(8,128)(2,1)}), bf16[8,24,512]{2,1,0:T(8,128)(2,1)S(1)}, u32[]{:S(2)}, u32[]{:S(2)}) async-start(bf16[8,24,512]{2,1,0:T(8,128)(2,1)} %shard_map.98), calls=%async_computation | async-start | bytes 393216 | tf_op jit(solution)/shard_map/all_to_all | solution.py:85
  32.9 4.9 %all-to-all-done.parts = bf16[8,24,512]{2,1,0:T(8,128)(2,1)S(1)} async-done(((bf16[8,24,512]{2,1,0:T(8,128)(2,1)}), bf16[8,24,512]{2,1,0:T(8,128)(2,1)S(1)}, u32[]{:S(2)}, u32[]{:S(2)}) %all-to-all-start) | async-done | bytes 196640 | tf_op jit(solution)/shard_map/all_to_all | solution.py:85
  37.9 4.6 %collective-permute-start.9 = (f32[8,128]{1,0:T(8,128)S(1)}, f32[8,128]{1,0:T(8,128)S(1)}, u32[]{:S(2)}, u32[]{:S(2)}) collective-permute-start(f32[8,128]{1,0:T(8,128)S(1)} %get-tuple-element.38.sums), channel_id=1, source_target_pairs={{0,32},{32,0},{64,96},{96,64},{1,33},{33,1},{65,97},{97,65},{8,40}... | collective-permute-start | bytes 12296 | tf_op jit(solution)/shard_map/ppermute | solution.py:288
  43.3 8.7 %all_to_all.15.sums = f32[8,8,128]{2,1,0:T(8,128)S(1)} all-to-all(f32[8,8,128]{2,1,0:T(8,128)S(1)} %shard_map.101), channel_id=1, replica_groups={{0,8,2,10,4,12,6,14},{24,16,26,18,28,20,30,22},{64,72,66,74,68,76,70,78..., dimensions={0} | all-to-all | bytes 65536 | tf_op jit(solution)/shard_map/all_to_all | solution.py:85
  52.0 10.4 %all_to_all.16.got = bf16[8,56,512]{2,1,0:T(8,128)(2,1)S(1)} all-to-all(bf16[8,56,512]{2,1,0:T(8,128)(2,1)S(1)} %shard_map.102), channel_id=1, replica_groups={{0,24,64,88,1,25,65,89},{8,16,72,80,9,17,73,81},{2,26,66,90,3,27,67,91}..., dimensions={0} | all-to-all | bytes 917504 | tf_op jit(solution)/shard_map/all_to_all | solution.py:85
  63.2 4.4 %collective-permute-start.11 = (bf16[8,24,512]{2,1,0:T(8,128)(2,1)S(1)}, bf16[8,24,512]{2,1,0:T(8,128)(2,1)S(1)}, u32[]{:S(2)}, u32[]{:S(2)}) collective-permute-start(bf16[8,24,512]{2,1,0:T(8,128)(2,1)S(1)} %get-tuple-element.39.refs_0_), channel_id=1, source_target_pairs={{10,0},{2,8},{12,2},{4,10},{14,4},{6,12},{8,6},{0,14},{18,24},{26,... | collective-permute-start | bytes 589832 | tf_op jit(solution)/shard_map/ppermute | solution.py:262
  67.6 3.1 %collective-permute-done.12.refs_3_ = bf16[8,24,512]{2,1,0:T(8,128)(2,1)S(1)} collective-permute-done((bf16[8,24,512]{2,1,0:T(8,128)(2,1)S(1)}, bf16[8,24,512]{2,1,0:T(8,128)(2,1)S(1)}, u32[]{:S(2)}, u32[]{:S(2)}) %collective-permute-start.12) | collective-permute-done | bytes 196640 | tf_op jit(solution)/shard_map/ppermute | solution.py:262
  70.6 5.1 %collective-permute-done.10.refs_1_ = bf16[8,24,512]{2,1,0:T(8,128)(2,1)S(1)} collective-permute-done((bf16[8,24,512]{2,1,0:T(8,128)(2,1)S(1)}, bf16[8,24,512]{2,1,0:T(8,128)(2,1)S(1)}, u32[]{:S(2)}, u32[]{:S(2)}) %collective-permute-start.10) | collective-permute-done | bytes 196640 | tf_op jit(solution)/shard_map/ppermute | solution.py:262
  75.8 2.4 %collective-permute-start.15 = (bf16[4,8,24,512]{3,2,1,0:T(8,128)(2,1)S(1)}, bf16[4,8,24,512]{3,2,1,0:T(8,128)(2,1)S(1)}, u32[]{:S(2)}, u32[]{:S(2)}) collective-permute-start(bf16[4,8,24,512]{3,2,1,0:T(8,128)(2,1)S(1)} %shard_map.104), channel_id=1, source_target_pairs={{0,32},{32,0},{64,96},{96,64},{1,33},{33,1},{65,97},{97,65},{8,40}... | collective-permute-start | bytes 2359304 | tf_op jit(solution)/shard_map/ppermute | solution.py:262
  78.2 2.7 %collective-permute-start.16 = (bf16[8,24,512]{2,1,0:T(8,128)(2,1)S(1)}, bf16[8,24,512]{2,1,0:T(8,128)(2,1)S(1)}, u32[]{:S(2)}, u32[]{:S(2)}) collective-permute-start(bf16[8,24,512]{2,1,0:T(8,128)(2,1)S(1)} %get-tuple-element.39.refs_0_), channel_id=1, source_target_pairs={{2,0},{10,8},{4,2},{12,10},{6,4},{14,12},{0,6},{8,14},{26,24},{18,... | collective-permute-start | bytes 589832 | tf_op jit(solution)/shard_map/ppermute | solution.py:262
  81.4 2.8 %collective-permute-done.17.refs_1_ = bf16[8,24,512]{2,1,0:T(8,128)(2,1)S(1)} collective-permute-done((bf16[8,24,512]{2,1,0:T(8,128)(2,1)S(1)}, bf16[8,24,512]{2,1,0:T(8,128)(2,1)S(1)}, u32[]{:S(2)}, u32[]{:S(2)}) %collective-permute-start.17) | collective-permute-done | bytes 196640 | tf_op jit(solution)/shard_map/ppermute | solution.py:262
  84.2 1.4 %collective-permute-done.16.refs_0_ = bf16[8,24,512]{2,1,0:T(8,128)(2,1)S(1)} collective-permute-done((bf16[8,24,512]{2,1,0:T(8,128)(2,1)S(1)}, bf16[8,24,512]{2,1,0:T(8,128)(2,1)S(1)}, u32[]{:S(2)}, u32[]{:S(2)}) %collective-permute-start.16) | collective-permute-done | bytes 196640 | tf_op jit(solution)/shard_map/ppermute | solution.py:262
  85.6 1.3 %collective-permute-start.19 = (bf16[2,8,24,512]{3,2,1,0:T(8,128)(2,1)S(1)}, bf16[2,8,24,512]{3,2,1,0:T(8,128)(2,1)S(1)}, u32[]{:S(2)}, u32[]{:S(2)}) collective-permute-start(bf16[2,8,24,512]{3,2,1,0:T(8,128)(2,1)S(1)} %shard_map.107), channel_id=1, source_target_pairs={{0,32},{32,0},{64,96},{96,64},{1,33},{33,1},{65,97},{97,65},{8,40}... | collective-permute-start | bytes 1179656 | tf_op jit(solution)/shard_map/ppermute | solution.py:262
  88.8 1.3 %shard_map.105 = (bf16[128,24,512]{2,1,0:T(8,128)(2,1)}, f32[24,512]{1,0:T(8,128)}, f32[24,512]{1,0:T(8,128)}, f32[24,512]{1,0:T(8,128)}, f32[24,512]{1,0:T(8,128)}) custom-call(s32[1]{0:T(128)} %bitcast.me, bf16[8,24,512]{2,1,0:T(8,128)(2,1)S(1)} %get-tuple-element.39.refs_0_, bf16[8,24,512]{2,1,0:T(8,128)(2,1)S(1)} %collective-permute-done.10.refs_1_, ...), custom_call_target="tpu_custom_call" | custom-call | tf_op jit(solution)/shard_map/pallas_call | solution.py:305
  (45 shorter events, 12.5 us)
Async XLA Ops:
  1.8 3.8 %collective-permute-start = (bf16[4,8,24,512]{3,2,1,0:T(8,128)(2,1)S(1)}, bf16[4,8,24,512]{3,2,1,0:T(8,128)(2,1)S(1)}, u32[]{:S(2)}, u32[]{:S(2)}) collective-permute-start(bf16[4,8,24,512]{3,2,1,0:T(8,128)(2,1)S(1)} %shard_map.93), channel_id=1, source_target_pairs={{0,32},{32,0},{64,96},{96,64},{1,33},{33,1},{65,97},{97,65},{8,40}... | collective-permute-start | bytes 2359304 | tf_op jit(solution)/shard_map/ppermute | solution.py:262
  4.4 9.3 %collective-permute-start.1 = (bf16[4,8,24,512]{3,2,1,0:T(8,128)(2,1)S(1)}, bf16[4,8,24,512]{3,2,1,0:T(8,128)(2,1)S(1)}, u32[]{:S(2)}, u32[]{:S(2)}) collective-permute-start(bf16[4,8,24,512]{3,2,1,0:T(8,128)(2,1)S(1)} %shard_map.96), channel_id=1, source_target_pairs={{0,32},{32,0},{64,96},{96,64},{1,33},{33,1},{65,97},{97,65},{8,40}... | collective-permute-start | bytes 2359304 | tf_op jit(solution)/shard_map/ppermute | solution.py:262
  5.7 12.2 %collective-permute-start.6 = (bf16[8,24,512]{2,1,0:T(8,128)(2,1)S(1)}, bf16[8,24,512]{2,1,0:T(8,128)(2,1)S(1)}, u32[]{:S(2)}, u32[]{:S(2)}) collective-permute-start(bf16[8,24,512]{2,1,0:T(8,128)(2,1)S(1)} %get-tuple-element.32), channel_id=1, source_target_pairs={{8,0},{0,8},{10,2},{2,10},{12,4},{4,12},{14,6},{6,14},{16,24},{24,... | collective-permute-start | bytes 589832 | tf_op jit(solution)/shard_map/ppermute | solution.py:262
  8.6 23.6 %copy-start.3 = (s32[24]{0:T(128)S(1)}, s32[24]{0:T(128)}, u32[]{:S(2)}) copy-start(s32[24]{0:T(128)} %ids.1) | copy-start | bytes 292
  8.6 29.1 %copy-start.1 = (f32[24,512]{1,0:T(8,128)S(1)}, f32[24,512]{1,0:T(8,128)}, u32[]{:S(2)}) copy-start(f32[24,512]{1,0:T(8,128)} %first.1) | copy-start | bytes 147460
  8.6 29.1 %copy-start.2 = (f32[24,512]{1,0:T(8,128)S(1)}, f32[24,512]{1,0:T(8,128)}, u32[]{:S(2)}) copy-start(f32[24,512]{1,0:T(8,128)} %second.1) | copy-start | bytes 147460
  8.7 10.5 %collective-permute-start.7 = (bf16[8,24,512]{2,1,0:T(8,128)(2,1)S(1)}, bf16[8,24,512]{2,1,0:T(8,128)(2,1)S(1)}, u32[]{:S(2)}, u32[]{:S(2)}) collective-permute-start(bf16[8,24,512]{2,1,0:T(8,128)(2,1)S(1)} %get-tuple-element.33), channel_id=1, source_target_pairs={{2,0},{10,8},{4,2},{12,10},{6,4},{14,12},{0,6},{8,14},{26,24},{18,... | collective-permute-start | bytes 589832 | tf_op jit(solution)/shard_map/ppermute | solution.py:262
  13.6 7.5 %collective-permute-start.8 = (bf16[8,24,512]{2,1,0:T(8,128)(2,1)S(1)}, bf16[8,24,512]{2,1,0:T(8,128)(2,1)S(1)}, u32[]{:S(2)}, u32[]{:S(2)}) collective-permute-start(bf16[8,24,512]{2,1,0:T(8,128)(2,1)S(1)} %get-tuple-element.34), channel_id=1, source_target_pairs={{6,0},{14,8},{0,2},{8,10},{2,4},{10,12},{4,6},{12,14},{30,24},{22,... | collective-permute-start | bytes 589832 | tf_op jit(solution)/shard_map/ppermute | solution.py:262
  13.8 8.2 %collective-permute-start.2 = (bf16[8,24,512]{2,1,0:T(8,128)(2,1)S(1)}, bf16[8,24,512]{2,1,0:T(8,128)(2,1)S(1)}, u32[]{:S(2)}, u32[]{:S(2)}) collective-permute-start(bf16[8,24,512]{2,1,0:T(8,128)(2,1)S(1)} %get-tuple-element.28), channel_id=1, source_target_pairs={{12,0},{4,8},{14,2},{6,10},{8,4},{0,12},{10,6},{2,14},{20,24},{28,... | collective-permute-start | bytes 589832 | tf_op jit(solution)/shard_map/ppermute | solution.py:262
  14.9 10.3 %collective-permute-start.3 = (bf16[8,24,512]{2,1,0:T(8,128)(2,1)S(1)}, bf16[8,24,512]{2,1,0:T(8,128)(2,1)S(1)}, u32[]{:S(2)}, u32[]{:S(2)}) collective-permute-start(bf16[8,24,512]{2,1,0:T(8,128)(2,1)S(1)} %get-tuple-element.29), channel_id=1, source_target_pairs={{10,0},{2,8},{12,2},{4,10},{14,4},{6,12},{8,6},{0,14},{18,24},{26,... | collective-permute-start | bytes 589832 | tf_op jit(solution)/shard_map/ppermute | solution.py:262
  17.9 8.4 %collective-permute-start.4 = (bf16[8,24,512]{2,1,0:T(8,128)(2,1)S(1)}, bf16[8,24,512]{2,1,0:T(8,128)(2,1)S(1)}, u32[]{:S(2)}, u32[]{:S(2)}) collective-permute-start(bf16[8,24,512]{2,1,0:T(8,128)(2,1)S(1)} %get-tuple-element.30), channel_id=1, source_target_pairs={{14,0},{6,8},{8,2},{0,10},{10,4},{2,12},{12,6},{4,14},{22,24},{30,... | collective-permute-start | bytes 589832 | tf_op jit(solution)/shard_map/ppermute | solution.py:262
  19.2 8.1 %collective-permute-start.5 = (bf16[8,24,512]{2,1,0:T(8,128)(2,1)S(1)}, bf16[8,24,512]{2,1,0:T(8,128)(2,1)S(1)}, u32[]{:S(2)}, u32[]{:S(2)}) collective-permute-start(bf16[8,24,512]{2,1,0:T(8,128)(2,1)S(1)} %get-tuple-element.31), channel_id=1, source_target_pairs={{4,0},{12,8},{6,2},{14,10},{0,4},{8,12},{2,6},{10,14},{28,24},{20,... | collective-permute-start | bytes 589832 | tf_op jit(solution)/shard_map/ppermute | solution.py:262
  28.2 9.5 %all-to-all-start = ((bf16[8,24,512]{2,1,0:T(8,128)(2,1)}), bf16[8,24,512]{2,1,0:T(8,128)(2,1)S(1)}, u32[]{:S(2)}, u32[]{:S(2)}) async-start(bf16[8,24,512]{2,1,0:T(8,128)(2,1)} %shard_map.98), calls=%async_computation | async-start | bytes 393216 | tf_op jit(solution)/shard_map/all_to_all | solution.py:85
  37.9 5.4 %collective-permute-start.9 = (f32[8,128]{1,0:T(8,128)S(1)}, f32[8,128]{1,0:T(8,128)S(1)}, u32[]{:S(2)}, u32[]{:S(2)}) collective-permute-start(f32[8,128]{1,0:T(8,128)S(1)} %get-tuple-element.38.sums), channel_id=1, source_target_pairs={{0,32},{32,0},{64,96},{96,64},{1,33},{33,1},{65,97},{97,65},{8,40}... | collective-permute-start | bytes 12296 | tf_op jit(solution)/shard_map/ppermute | solution.py:288
  62.7 7.9 %collective-permute-start.12 = (bf16[8,24,512]{2,1,0:T(8,128)(2,1)S(1)}, bf16[8,24,512]{2,1,0:T(8,128)(2,1)S(1)}, u32[]{:S(2)}, u32[]{:S(2)}) collective-permute-start(bf16[8,24,512]{2,1,0:T(8,128)(2,1)S(1)} %get-tuple-element.39.refs_0_), channel_id=1, source_target_pairs={{14,0},{6,8},{8,2},{0,10},{10,4},{2,12},{12,6},{4,14},{22,24},{30,... | collective-permute-start | bytes 589832 | tf_op jit(solution)/shard_map/ppermute | solution.py:262
  63.2 7.4 %collective-permute-start.11 = (bf16[8,24,512]{2,1,0:T(8,128)(2,1)S(1)}, bf16[8,24,512]{2,1,0:T(8,128)(2,1)S(1)}, u32[]{:S(2)}, u32[]{:S(2)}) collective-permute-start(bf16[8,24,512]{2,1,0:T(8,128)(2,1)S(1)} %get-tuple-element.39.refs_0_), channel_id=1, source_target_pairs={{10,0},{2,8},{12,2},{4,10},{14,4},{6,12},{8,6},{0,14},{18,24},{26,... | collective-permute-start | bytes 589832 | tf_op jit(solution)/shard_map/ppermute | solution.py:262
  67.6 8.1 %collective-permute-start.10 = (bf16[8,24,512]{2,1,0:T(8,128)(2,1)S(1)}, bf16[8,24,512]{2,1,0:T(8,128)(2,1)S(1)}, u32[]{:S(2)}, u32[]{:S(2)}) collective-permute-start(bf16[8,24,512]{2,1,0:T(8,128)(2,1)S(1)} %get-tuple-element.39.refs_0_), channel_id=1, source_target_pairs={{12,0},{4,8},{14,2},{6,10},{8,4},{0,12},{10,6},{2,14},{20,24},{28,... | collective-permute-start | bytes 589832 | tf_op jit(solution)/shard_map/ppermute | solution.py:262
  75.8 13.0 %collective-permute-start.15 = (bf16[4,8,24,512]{3,2,1,0:T(8,128)(2,1)S(1)}, bf16[4,8,24,512]{3,2,1,0:T(8,128)(2,1)S(1)}, u32[]{:S(2)}, u32[]{:S(2)}) collective-permute-start(bf16[4,8,24,512]{3,2,1,0:T(8,128)(2,1)S(1)} %shard_map.104), channel_id=1, source_target_pairs={{0,32},{32,0},{64,96},{96,64},{1,33},{33,1},{65,97},{97,65},{8,40}... | collective-permute-start | bytes 2359304 | tf_op jit(solution)/shard_map/ppermute | solution.py:262
  78.2 6.0 %collective-permute-start.17 = (bf16[8,24,512]{2,1,0:T(8,128)(2,1)S(1)}, bf16[8,24,512]{2,1,0:T(8,128)(2,1)S(1)}, u32[]{:S(2)}, u32[]{:S(2)}) collective-permute-start(bf16[8,24,512]{2,1,0:T(8,128)(2,1)S(1)} %get-tuple-element.39.refs_0_), channel_id=1, source_target_pairs={{6,0},{14,8},{0,2},{8,10},{2,4},{10,12},{4,6},{12,14},{30,24},{22,... | collective-permute-start | bytes 589832 | tf_op jit(solution)/shard_map/ppermute | solution.py:262
  78.2 7.4 %collective-permute-start.16 = (bf16[8,24,512]{2,1,0:T(8,128)(2,1)S(1)}, bf16[8,24,512]{2,1,0:T(8,128)(2,1)S(1)}, u32[]{:S(2)}, u32[]{:S(2)}) collective-permute-start(bf16[8,24,512]{2,1,0:T(8,128)(2,1)S(1)} %get-tuple-element.39.refs_0_), channel_id=1, source_target_pairs={{2,0},{10,8},{4,2},{12,10},{6,4},{14,12},{0,6},{8,14},{26,24},{18,... | collective-permute-start | bytes 589832 | tf_op jit(solution)/shard_map/ppermute | solution.py:262
  80.8 6.1 %collective-permute-start.14 = (bf16[8,24,512]{2,1,0:T(8,128)(2,1)S(1)}, bf16[8,24,512]{2,1,0:T(8,128)(2,1)S(1)}, u32[]{:S(2)}, u32[]{:S(2)}) collective-permute-start(bf16[8,24,512]{2,1,0:T(8,128)(2,1)S(1)} %get-tuple-element.39.refs_0_), channel_id=1, source_target_pairs={{8,0},{0,8},{10,2},{2,10},{12,4},{4,12},{14,6},{6,14},{16,24},{24,... | collective-permute-start | bytes 589832 | tf_op jit(solution)/shard_map/ppermute | solution.py:262
  81.4 6.3 %collective-permute-start.13 = (bf16[8,24,512]{2,1,0:T(8,128)(2,1)S(1)}, bf16[8,24,512]{2,1,0:T(8,128)(2,1)S(1)}, u32[]{:S(2)}, u32[]{:S(2)}) collective-permute-start(bf16[8,24,512]{2,1,0:T(8,128)(2,1)S(1)} %get-tuple-element.39.refs_0_), channel_id=1, source_target_pairs={{4,0},{12,8},{6,2},{14,10},{0,4},{8,12},{2,6},{10,14},{28,24},{20,... | collective-permute-start | bytes 589832 | tf_op jit(solution)/shard_map/ppermute | solution.py:262
  85.6 4.5 %collective-permute-start.19 = (bf16[2,8,24,512]{3,2,1,0:T(8,128)(2,1)S(1)}, bf16[2,8,24,512]{3,2,1,0:T(8,128)(2,1)S(1)}, u32[]{:S(2)}, u32[]{:S(2)}) collective-permute-start(bf16[2,8,24,512]{3,2,1,0:T(8,128)(2,1)S(1)} %shard_map.107), channel_id=1, source_target_pairs={{0,32},{32,0},{64,96},{96,64},{1,33},{33,1},{65,97},{97,65},{8,40}... | collective-permute-start | bytes 1179656 | tf_op jit(solution)/shard_map/ppermute | solution.py:262
  87.7 2.4 %collective-permute-start.18 = (bf16[2,8,24,512]{3,2,1,0:T(8,128)(2,1)S(1)}, bf16[2,8,24,512]{3,2,1,0:T(8,128)(2,1)S(1)}, u32[]{:S(2)}, u32[]{:S(2)}) collective-permute-start(bf16[2,8,24,512]{3,2,1,0:T(8,128)(2,1)S(1)} %shard_map.106), channel_id=1, source_target_pairs={{0,32},{32,0},{64,96},{96,64},{1,33},{33,1},{65,97},{97,65},{8,40}... | collective-permute-start | bytes 1179656 | tf_op jit(solution)/shard_map/ppermute | solution.py:262
  (1 other events, 23.6 us)

commit v2 on v1

--- a/solution.py
+++ b/solution.py
@@ -56,6 +56,7 @@
 
 OFFSETS = ((2, 1), (3, 1), (1, 1), (2, 0), (0, 1), (3, 0), (1, 0))
 OWN = (0, 0)
+HALVES = (OFFSETS[:4], OFFSETS[4:] + (OWN,))
 
 
 def source_place(a, offset):
@@ -177,14 +178,17 @@
     new_master[...] = weights[...] - step_size * scaled
 
 
-def take_kernel(me, gradients, taken, done, *, other, offsets):
+def take_kernel(me, gradients, *refs, other):
+    halves, done = refs[:2], refs[2]
     device = me[0] ^ (32 if other else 0)
     core = (device >> 5) & 1
-    for j, offset in enumerate(offsets):
-        a = target_place(wide_place(device), offset)
-        for b in range(GROUP):
-            pltpu.make_async_copy(gradients.at[owner_of(core, a, b)], taken.at[j, b], done).start()
-    pltpu.make_async_copy(taken, taken, done).wait()
+    for k, offsets in enumerate(HALVES):
+        for j, offset in enumerate(offsets):
+            a = target_place(wide_place(device), offset)
+            for b in range(GROUP):
+                pltpu.make_async_copy(gradients.at[owner_of(core, a, b)], halves[k].at[j, b], done.at[k]).start()
+    for k in range(2):
+        pltpu.make_async_copy(halves[k], halves[k], done.at[k]).wait()
 
 
 def add_kernel(kept, arrived, *both):
@@ -256,21 +260,22 @@
     me = lax.axis_index("i").astype(jnp.int32).reshape(1)
     own_f32 = pltpu.VMEM((ROWS, COLS), F32)
     chunk = pltpu.VMEM((GROUP, ROWS, COLS), BF16)
-    copied = dict(scratch_shapes=[pltpu.SemaphoreType.DMA])
 
     def send(value, pairs):
         return lax.ppermute(value, "i", pairs)
 
     blocks = pltpu.with_memory_space_constraint(gradients.reshape(2 * CHIPS, ROWS, COLS), pltpu.HBM)
-    halves = (OFFSETS[:4], OFFSETS[4:] + (OWN,))
-
-    def take(other, offsets):
-        body = functools.partial(take_kernel, other=other, offsets=offsets)
-        return kernel(body, [SMEM, HBM], VMEM, pltpu.VMEM((4, GROUP, ROWS, COLS), BF16), **copied)(me, blocks)
-
-    sent = [take(True, offsets) for offsets in halves]
+    half = pltpu.VMEM((4, GROUP, ROWS, COLS), BF16)
+
+    def take(other):
+        body = functools.partial(take_kernel, other=other)
+        return kernel(
+            body, [SMEM, HBM], [VMEM] * 2, [half] * 2, scratch_shapes=[pltpu.SemaphoreType.DMA((2,))]
+        )(me, blocks)
+
+    sent = take(True)
     arrived = [send(sent[k], CORE_SWAP) for k in range(2)]
-    kept = [take(False, offsets) for offsets in halves]
+    kept = take(False)
     chunks = []
     for k in range(2):
         chunks += kernel(add_kernel, [VMEM] * 2, [VMEM] * 4, [chunk] * 4)(kept[k], arrived[k])
@@ -316,18 +321,20 @@
     other_1 = send(join(*wide[3:5]), CORE_SWAP)
     other_2 = send(join(*wide[5:7]), CORE_SWAP)
     gathered, new_first, new_second, new_master, scaled_update = place(
-        [params, *wide[0:5], other_0],
-        [(0, None, False, OWN)]
-        + [(1 + k, None, False, OFFSETS[k]) for k in range(5)]
-        + [(6, 0, True, OWN)]
-        + [(6, 1 + k, True, OFFSETS[k]) for k in range(3)],
+        [params, *wide[0:3]],
+        [(0, None, False, OWN)] + [(1 + k, None, False, OFFSETS[k]) for k in range(3)],
         rows=(new_first, new_second, new_master, scaled_update),
     )
     (gathered,) = place(
-        [*wide[5:7], other_1, other_2],
-        [(k, None, False, OFFSETS[5 + k]) for k in range(2)]
-        + [(2, k, True, OFFSETS[3 + k]) for k in range(2)]
-        + [(3, k, True, OFFSETS[5 + k]) for k in range(2)],
+        [*wide[3:7], other_0],
+        [(k, None, False, OFFSETS[3 + k]) for k in range(4)]
+        + [(4, 0, True, OWN)]
+        + [(4, 1 + k, True, OFFSETS[k]) for k in range(3)],
+        gathered,
+    )
+    (gathered,) = place(
+        [other_1, other_2],
+        [(0, k, True, OFFSETS[3 + k]) for k in range(2)] + [(1, k, True, OFFSETS[5 + k]) for k in range(2)],
         gathered,
     )
     gathered = gathered.reshape(2 * CHIPS * ROWS, COLS)

time: 91.8 us -> 91.3 us (level)
  waiting for transfers between devices: 25.1 us -> 26.2 us
  Pallas kernels: 9.04 us -> 8.09 us
    pallas_call x4 -> x2, Pallas kernels: 4.42 us -> 2.83 us  [take(): kernel(body, [SMEM, HBM], [VMEM] * 2, [half] * 2, scratch_shapes=[pltpu.S...]
    ppermute x1, starting transfers between devices: 4.61 us -> 5.97 us  [on_device(): arrived = lax.ppermute(sums, 'i', CORE_SWAP)]
    ppermute x19, starting transfers between devices: 28.6 us -> 27.3 us  [send(): return lax.ppermute(value, 'i', pairs)]
    ppermute x19, waiting for transfers between devices: 19.4 us -> 20.5 us  [send(): return lax.ppermute(value, 'i', pairs)]
    pallas_call x2 -> x3, Pallas kernels: 2.35 us -> 2.98 us  [place(): kernel(functools.partial(place_kernel, arrays=len(arrays), chunks=chunks,...]
  transfers between devices with their start and end apart: 21 -> 21, of which waited for: 11 -> 11; matrix products, arithmetic and copies ran while one was open for 0% -> 0% of each run, Pallas kernels for 6% -> 5%
where the time goes in v2:
time: 91.3 us; the launch traced here: 90.8 us
  starting transfers between devices  37.3 us (41%)
  waiting for transfers between devices  26.2 us (29%)
  blocking collectives  18.4 us (20%)
  Pallas kernels  8.09 us (9%)
    ppermute x19, starting transfers between devices, send(): return lax.ppermute(value, 'i', pairs)  27.3 us
    ppermute x19, waiting for transfers between devices, send(): return lax.ppermute(value, 'i', pairs)  20.5 us
    all_to_all x2, blocking collectives, exchange(): lax.all_to_all(value, 'i', 0, 0, axis_index_groups=groups, tiled=True)  18.4 us
    ppermute x1, starting transfers between devices, on_device(): arrived = lax.ppermute(sums, 'i', CORE_SWAP)  5.97 us
    all_to_all x1, waiting for transfers between devices, exchange(): lax.all_to_all(value, 'i', 0, 0, axis_index_groups=groups, tiled=True)  4.87 us
    all_to_all x1, starting transfers between devices, exchange(): lax.all_to_all(value, 'i', 0, 0, axis_index_groups=groups, tiled=True)  4.02 us
    pallas_call x3, Pallas kernels, place(): kernel(functools.partial(place_kernel, arrays=len(arrays), chunks=chunks,...  2.98 us
    pallas_call x2, Pallas kernels, take(): kernel(body, [SMEM, HBM], [VMEM] * 2, [half] * 2, scratch_shapes=[pltpu.S...  2.83 us
  transfers between devices with their start and end apart: 21, of which 11 were waited for; matrix products, arithmetic and copies ran while one was open for 0% of the time, Pallas kernels for 5%

profile of v2, /device:TPU:1, one launch (start us, length us, event | category | flops | bytes accessed | tf_op | source)
XLA Modules:
  0.0 90.8 jit_solution(17394274069944689795)
XLA Ops:
  0.6 1.4 %shard_map.93 = (bf16[4,8,24,512]{3,2,1,0:T(8,128)(2,1)S(1)}, bf16[4,8,24,512]{3,2,1,0:T(8,128)(2,1)S(1)}) custom-call(s32[1]{0:T(128)} %bitcast.me, bf16[128,24,512]{2,1,0:T(8,128)(2,1)} %bitcast.4), custom_call_target="tpu_custom_call" | custom-call | tf_op jit(solution)/shard_map/pallas_call | solution.py:272
  2.1 1.5 %collective-permute-start.1 = (bf16[4,8,24,512]{3,2,1,0:T(8,128)(2,1)S(1)}, bf16[4,8,24,512]{3,2,1,0:T(8,128)(2,1)S(1)}, u32[]{:S(2)}, u32[]{:S(2)}) collective-permute-start(bf16[4,8,24,512]{3,2,1,0:T(8,128)(2,1)S(1)} %get-tuple-element.35), channel_id=1, source_target_pairs={{0,32},{32,0},{64,96},{96,64},{1,33},{33,1},{65,97},{97,65},{8,40}... | collective-permute-start | bytes 2359304 | tf_op jit(solution)/shard_map/ppermute | solution.py:265
  3.6 1.4 %shard_map.92 = (bf16[4,8,24,512]{3,2,1,0:T(8,128)(2,1)S(1)}, bf16[4,8,24,512]{3,2,1,0:T(8,128)(2,1)S(1)}) custom-call(s32[1]{0:T(128)} %bitcast.me, bf16[128,24,512]{2,1,0:T(8,128)(2,1)} %bitcast.5), custom_call_target="tpu_custom_call" | custom-call | tf_op jit(solution)/shard_map/pallas_call | solution.py:272
  5.5 6.2 %collective-permute-start.2 = (bf16[8,24,512]{2,1,0:T(8,128)(2,1)S(1)}, bf16[8,24,512]{2,1,0:T(8,128)(2,1)S(1)}, u32[]{:S(2)}, u32[]{:S(2)}) collective-permute-start(bf16[8,24,512]{2,1,0:T(8,128)(2,1)S(1)} %get-tuple-element.36), channel_id=1, source_target_pairs={{12,0},{4,8},{14,2},{6,10},{8,4},{0,12},{10,6},{2,14},{20,24},{28,... | collective-permute-start | bytes 589832 | tf_op jit(solution)/shard_map/ppermute | solution.py:265
  12.0 3.3 %collective-permute-start.4 = (bf16[8,24,512]{2,1,0:T(8,128)(2,1)S(1)}, bf16[8,24,512]{2,1,0:T(8,128)(2,1)S(1)}, u32[]{:S(2)}, u32[]{:S(2)}) collective-permute-start(bf16[8,24,512]{2,1,0:T(8,128)(2,1)S(1)} %get-tuple-element.38), channel_id=1, source_target_pairs={{14,0},{6,8},{8,2},{0,10},{10,4},{2,12},{12,6},{4,14},{22,24},{30,... | collective-permute-start | bytes 589832 | tf_op jit(solution)/shard_map/ppermute | solution.py:265
  15.5 1.4 %collective-permute-start.6 = (bf16[8,24,512]{2,1,0:T(8,128)(2,1)S(1)}, bf16[8,24,512]{2,1,0:T(8,128)(2,1)S(1)}, u32[]{:S(2)}, u32[]{:S(2)}) collective-permute-start(bf16[8,24,512]{2,1,0:T(8,128)(2,1)S(1)} %get-tuple-element.40), channel_id=1, source_target_pairs={{8,0},{0,8},{10,2},{2,10},{12,4},{4,12},{14,6},{6,14},{16,24},{24,... | collective-permute-start | bytes 589832 | tf_op jit(solution)/shard_map/ppermute | solution.py:265
  16.9 1.9 %collective-permute-start.7 = (bf16[8,24,512]{2,1,0:T(8,128)(2,1)S(1)}, bf16[8,24,512]{2,1,0:T(8,128)(2,1)S(1)}, u32[]{:S(2)}, u32[]{:S(2)}) collective-permute-start(bf16[8,24,512]{2,1,0:T(8,128)(2,1)S(1)} %get-tuple-element.41), channel_id=1, source_target_pairs={{2,0},{10,8},{4,2},{12,10},{6,4},{14,12},{0,6},{8,14},{26,24},{18,... | collective-permute-start | bytes 589832 | tf_op jit(solution)/shard_map/ppermute | solution.py:265
  20.2 3.4 %collective-permute-done.5.refs_4_ = bf16[8,24,512]{2,1,0:T(8,128)(2,1)S(1)} collective-permute-done((bf16[8,24,512]{2,1,0:T(8,128)(2,1)S(1)}, bf16[8,24,512]{2,1,0:T(8,128)(2,1)S(1)}, u32[]{:S(2)}, u32[]{:S(2)}) %collective-permute-start.5) | collective-permute-done | bytes 196640 | tf_op jit(solution)/shard_map/ppermute | solution.py:265
  23.6 2.0 %collective-permute-done.8.refs_7_ = bf16[8,24,512]{2,1,0:T(8,128)(2,1)S(1)} collective-permute-done((bf16[8,24,512]{2,1,0:T(8,128)(2,1)S(1)}, bf16[8,24,512]{2,1,0:T(8,128)(2,1)S(1)}, u32[]{:S(2)}, u32[]{:S(2)}) %collective-permute-start.8) | collective-permute-done | bytes 196640 | tf_op jit(solution)/shard_map/ppermute | solution.py:265
  26.5 4.0 %all-to-all-start = ((bf16[8,24,512]{2,1,0:T(8,128)(2,1)}), bf16[8,24,512]{2,1,0:T(8,128)(2,1)S(1)}, u32[]{:S(2)}, u32[]{:S(2)}) async-start(bf16[8,24,512]{2,1,0:T(8,128)(2,1)} %shard_map.96), calls=%async_computation | async-start | bytes 393216 | tf_op jit(solution)/shard_map/all_to_all | solution.py:86
  31.2 4.9 %all-to-all-done.parts = bf16[8,24,512]{2,1,0:T(8,128)(2,1)S(1)} async-done(((bf16[8,24,512]{2,1,0:T(8,128)(2,1)}), bf16[8,24,512]{2,1,0:T(8,128)(2,1)S(1)}, u32[]{:S(2)}, u32[]{:S(2)}) %all-to-all-start) | async-done | bytes 196640 | tf_op jit(solution)/shard_map/all_to_all | solution.py:86
  36.2 6.0 %collective-permute-start.9 = (f32[8,128]{1,0:T(8,128)S(1)}, f32[8,128]{1,0:T(8,128)S(1)}, u32[]{:S(2)}, u32[]{:S(2)}) collective-permute-start(f32[8,128]{1,0:T(8,128)S(1)} %get-tuple-element.46.sums), channel_id=1, source_target_pairs={{0,32},{32,0},{64,96},{96,64},{1,33},{33,1},{65,97},{97,65},{8,40}... | collective-permute-start | bytes 12296 | tf_op jit(solution)/shard_map/ppermute | solution.py:293
  43.0 8.7 %all_to_all.15.sums = f32[8,8,128]{2,1,0:T(8,128)S(1)} all-to-all(f32[8,8,128]{2,1,0:T(8,128)S(1)} %shard_map.99), channel_id=1, replica_groups={{0,8,2,10,4,12,6,14},{24,16,26,18,28,20,30,22},{64,72,66,74,68,76,70,78..., dimensions={0} | all-to-all | bytes 65536 | tf_op jit(solution)/shard_map/all_to_all | solution.py:86
  51.7 9.8 %all_to_all.16.got = bf16[8,56,512]{2,1,0:T(8,128)(2,1)S(1)} all-to-all(bf16[8,56,512]{2,1,0:T(8,128)(2,1)S(1)} %shard_map.100), channel_id=1, replica_groups={{0,24,64,88,1,25,65,89},{8,16,72,80,9,17,73,81},{2,26,66,90,3,27,67,91}..., dimensions={0} | all-to-all | bytes 917504 | tf_op jit(solution)/shard_map/all_to_all | solution.py:86
  61.8 1.0 %collective-permute-start.10 = (bf16[8,24,512]{2,1,0:T(8,128)(2,1)S(1)}, bf16[8,24,512]{2,1,0:T(8,128)(2,1)S(1)}, u32[]{:S(2)}, u32[]{:S(2)}) collective-permute-start(bf16[8,24,512]{2,1,0:T(8,128)(2,1)S(1)} %get-tuple-element.47.refs_0_), channel_id=1, source_target_pairs={{12,0},{4,8},{14,2},{6,10},{8,4},{0,12},{10,6},{2,14},{20,24},{28,... | collective-permute-start | bytes 589832 | tf_op jit(solution)/shard_map/ppermute | solution.py:265
  62.8 3.9 %collective-permute-start.11 = (bf16[8,24,512]{2,1,0:T(8,128)(2,1)S(1)}, bf16[8,24,512]{2,1,0:T(8,128)(2,1)S(1)}, u32[]{:S(2)}, u32[]{:S(2)}) collective-permute-start(bf16[8,24,512]{2,1,0:T(8,128)(2,1)S(1)} %get-tuple-element.47.refs_0_), channel_id=1, source_target_pairs={{10,0},{2,8},{12,2},{4,10},{14,4},{6,12},{8,6},{0,14},{18,24},{26,... | collective-permute-start | bytes 589832 | tf_op jit(solution)/shard_map/ppermute | solution.py:265
  66.7 3.3 %collective-permute-done.10.refs_1_ = bf16[8,24,512]{2,1,0:T(8,128)(2,1)S(1)} collective-permute-done((bf16[8,24,512]{2,1,0:T(8,128)(2,1)S(1)}, bf16[8,24,512]{2,1,0:T(8,128)(2,1)S(1)}, u32[]{:S(2)}, u32[]{:S(2)}) %collective-permute-start.10) | collective-permute-done | bytes 196640 | tf_op jit(solution)/shard_map/ppermute | solution.py:265
  70.9 3.6 %collective-permute-done.12.refs_3_ = bf16[8,24,512]{2,1,0:T(8,128)(2,1)S(1)} collective-permute-done((bf16[8,24,512]{2,1,0:T(8,128)(2,1)S(1)}, bf16[8,24,512]{2,1,0:T(8,128)(2,1)S(1)}, u32[]{:S(2)}, u32[]{:S(2)}) %collective-permute-start.12) | collective-permute-done | bytes 196640 | tf_op jit(solution)/shard_map/ppermute | solution.py:265
  74.6 2.7 %collective-permute-start.19 = (bf16[4,8,24,512]{3,2,1,0:T(8,128)(2,1)S(1)}, bf16[4,8,24,512]{3,2,1,0:T(8,128)(2,1)S(1)}, u32[]{:S(2)}, u32[]{:S(2)}) collective-permute-start(bf16[4,8,24,512]{3,2,1,0:T(8,128)(2,1)S(1)} %shard_map.105), channel_id=1, source_target_pairs={{0,32},{32,0},{64,96},{96,64},{1,33},{33,1},{65,97},{97,65},{8,40}... | collective-permute-start | bytes 2359304 | tf_op jit(solution)/shard_map/ppermute | solution.py:265
  79.9 2.2 %collective-permute-done.16.refs_0_.refs_2_ = bf16[8,24,512]{2,1,0:T(8,128)(2,1)S(1)} collective-permute-done((bf16[8,24,512]{2,1,0:T(8,128)(2,1)S(1)}, bf16[8,24,512]{2,1,0:T(8,128)(2,1)S(1)}, u32[]{:S(2)}, u32[]{:S(2)}) %collective-permute-start.16) | collective-permute-done | bytes 196640 | tf_op jit(solution)/shard_map/ppermute | solution.py:265
  82.1 3.9 %collective-permute-done.17.refs_1_.refs_3_ = bf16[8,24,512]{2,1,0:T(8,128)(2,1)S(1)} collective-permute-done((bf16[8,24,512]{2,1,0:T(8,128)(2,1)S(1)}, bf16[8,24,512]{2,1,0:T(8,128)(2,1)S(1)}, u32[]{:S(2)}, u32[]{:S(2)}) %collective-permute-start.17) | collective-permute-done | bytes 196640 | tf_op jit(solution)/shard_map/ppermute | solution.py:265
  86.1 1.6 %collective-permute-start.18 = (bf16[2,8,24,512]{3,2,1,0:T(8,128)(2,1)S(1)}, bf16[2,8,24,512]{3,2,1,0:T(8,128)(2,1)S(1)}, u32[]{:S(2)}, u32[]{:S(2)}) collective-permute-start(bf16[2,8,24,512]{3,2,1,0:T(8,128)(2,1)S(1)} %shard_map.104), channel_id=1, source_target_pairs={{0,32},{32,0},{64,96},{96,64},{1,33},{33,1},{65,97},{97,65},{8,40}... | collective-permute-start | bytes 1179656 | tf_op jit(solution)/shard_map/ppermute | solution.py:265
  87.8 1.0 %shard_map.102 = (bf16[128,24,512]{2,1,0:T(8,128)(2,1)}, f32[24,512]{1,0:T(8,128)}, f32[24,512]{1,0:T(8,128)}, f32[24,512]{1,0:T(8,128)}, f32[24,512]{1,0:T(8,128)}) custom-call(s32[1]{0:T(128)} %bitcast.me, bf16[8,24,512]{2,1,0:T(8,128)(2,1)S(1)} %get-tuple-element.47.refs_0_, bf16[8,24,512]{2,1,0:T(8,128)(2,1)S(1)} %collective-permute-done.10.refs_1_, ...), custom_call_target="tpu_custom_call" | custom-call | tf_op jit(solution)/shard_map/pallas_call | solution.py:310
  88.8 1.1 %shard_map.106.refs_2_ = bf16[128,24,512]{2,1,0:T(8,128)(2,1)} custom-call(s32[1]{0:T(128)} %bitcast.me, bf16[8,24,512]{2,1,0:T(8,128)(2,1)S(1)} %collective-permute-done.13.refs_0_, bf16[8,24,512]{2,1,0:T(8,128)(2,1)S(1)} %collective-permute-done.14.refs_1_, ...), custom_call_target="tpu_custom_call", output_to_operand_aliasing={{}: (6, {})} | custom-call | tf_op jit(solution)/shard_map/pallas_call | solution.py:310
  (44 shorter events, 9.8 us)
Async XLA Ops:
  2.1 3.4 %collective-permute-start.1 = (bf16[4,8,24,512]{3,2,1,0:T(8,128)(2,1)S(1)}, bf16[4,8,24,512]{3,2,1,0:T(8,128)(2,1)S(1)}, u32[]{:S(2)}, u32[]{:S(2)}) collective-permute-start(bf16[4,8,24,512]{3,2,1,0:T(8,128)(2,1)S(1)} %get-tuple-element.35), channel_id=1, source_target_pairs={{0,32},{32,0},{64,96},{96,64},{1,33},{33,1},{65,97},{97,65},{8,40}... | collective-permute-start | bytes 2359304 | tf_op jit(solution)/shard_map/ppermute | solution.py:265
  3.6 11.8 %collective-permute-start = (bf16[4,8,24,512]{3,2,1,0:T(8,128)(2,1)S(1)}, bf16[4,8,24,512]{3,2,1,0:T(8,128)(2,1)S(1)}, u32[]{:S(2)}, u32[]{:S(2)}) collective-permute-start(bf16[4,8,24,512]{3,2,1,0:T(8,128)(2,1)S(1)} %get-tuple-element.32), channel_id=1, source_target_pairs={{0,32},{32,0},{64,96},{96,64},{1,33},{33,1},{65,97},{97,65},{8,40}... | collective-permute-start | bytes 2359304 | tf_op jit(solution)/shard_map/ppermute | solution.py:265
  5.0 25.5 %copy-start = (f32[24,512]{1,0:T(8,128)S(1)}, f32[24,512]{1,0:T(8,128)}, u32[]{:S(2)}) copy-start(f32[24,512]{1,0:T(8,128)} %weights.7) | copy-start | bytes 147460
  5.1 31.0 %copy-start.1 = (f32[24,512]{1,0:T(8,128)S(1)}, f32[24,512]{1,0:T(8,128)}, u32[]{:S(2)}) copy-start(f32[24,512]{1,0:T(8,128)} %first.1) | copy-start | bytes 147460
  5.1 31.0 %copy-start.2 = (f32[24,512]{1,0:T(8,128)S(1)}, f32[24,512]{1,0:T(8,128)}, u32[]{:S(2)}) copy-start(f32[24,512]{1,0:T(8,128)} %second.1) | copy-start | bytes 147460
  5.5 11.3 %collective-permute-start.2 = (bf16[8,24,512]{2,1,0:T(8,128)(2,1)S(1)}, bf16[8,24,512]{2,1,0:T(8,128)(2,1)S(1)}, u32[]{:S(2)}, u32[]{:S(2)}) collective-permute-start(bf16[8,24,512]{2,1,0:T(8,128)(2,1)S(1)} %get-tuple-element.36), channel_id=1, source_target_pairs={{12,0},{4,8},{14,2},{6,10},{8,4},{0,12},{10,6},{2,14},{20,24},{28,... | collective-permute-start | bytes 589832 | tf_op jit(solution)/shard_map/ppermute | solution.py:265
  11.8 7.0 %collective-permute-start.3 = (bf16[8,24,512]{2,1,0:T(8,128)(2,1)S(1)}, bf16[8,24,512]{2,1,0:T(8,128)(2,1)S(1)}, u32[]{:S(2)}, u32[]{:S(2)}) collective-permute-start(bf16[8,24,512]{2,1,0:T(8,128)(2,1)S(1)} %get-tuple-element.37), channel_id=1, source_target_pairs={{10,0},{2,8},{12,2},{4,10},{14,4},{6,12},{8,6},{0,14},{18,24},{26,... | collective-permute-start | bytes 589832 | tf_op jit(solution)/shard_map/ppermute | solution.py:265
  12.0 8.1 %collective-permute-start.4 = (bf16[8,24,512]{2,1,0:T(8,128)(2,1)S(1)}, bf16[8,24,512]{2,1,0:T(8,128)(2,1)S(1)}, u32[]{:S(2)}, u32[]{:S(2)}) collective-permute-start(bf16[8,24,512]{2,1,0:T(8,128)(2,1)S(1)} %get-tuple-element.38), channel_id=1, source_target_pairs={{14,0},{6,8},{8,2},{0,10},{10,4},{2,12},{12,6},{4,14},{22,24},{30,... | collective-permute-start | bytes 589832 | tf_op jit(solution)/shard_map/ppermute | solution.py:265
  15.4 8.2 %collective-permute-start.5 = (bf16[8,24,512]{2,1,0:T(8,128)(2,1)S(1)}, bf16[8,24,512]{2,1,0:T(8,128)(2,1)S(1)}, u32[]{:S(2)}, u32[]{:S(2)}) collective-permute-start(bf16[8,24,512]{2,1,0:T(8,128)(2,1)S(1)} %get-tuple-element.39), channel_id=1, source_target_pairs={{4,0},{12,8},{6,2},{14,10},{0,4},{8,12},{2,6},{10,14},{28,24},{20,... | collective-permute-start | bytes 589832 | tf_op jit(solution)/shard_map/ppermute | solution.py:265
  15.5 8.1 %collective-permute-start.6 = (bf16[8,24,512]{2,1,0:T(8,128)(2,1)S(1)}, bf16[8,24,512]{2,1,0:T(8,128)(2,1)S(1)}, u32[]{:S(2)}, u32[]{:S(2)}) collective-permute-start(bf16[8,24,512]{2,1,0:T(8,128)(2,1)S(1)} %get-tuple-element.40), channel_id=1, source_target_pairs={{8,0},{0,8},{10,2},{2,10},{12,4},{4,12},{14,6},{6,14},{16,24},{24,... | collective-permute-start | bytes 589832 | tf_op jit(solution)/shard_map/ppermute | solution.py:265
  16.9 6.7 %collective-permute-start.7 = (bf16[8,24,512]{2,1,0:T(8,128)(2,1)S(1)}, bf16[8,24,512]{2,1,0:T(8,128)(2,1)S(1)}, u32[]{:S(2)}, u32[]{:S(2)}) collective-permute-start(bf16[8,24,512]{2,1,0:T(8,128)(2,1)S(1)} %get-tuple-element.41), channel_id=1, source_target_pairs={{2,0},{10,8},{4,2},{12,10},{6,4},{14,12},{0,6},{8,14},{26,24},{18,... | collective-permute-start | bytes 589832 | tf_op jit(solution)/shard_map/ppermute | solution.py:265
  18.8 6.8 %collective-permute-start.8 = (bf16[8,24,512]{2,1,0:T(8,128)(2,1)S(1)}, bf16[8,24,512]{2,1,0:T(8,128)(2,1)S(1)}, u32[]{:S(2)}, u32[]{:S(2)}) collective-permute-start(bf16[8,24,512]{2,1,0:T(8,128)(2,1)S(1)} %get-tuple-element.42), channel_id=1, source_target_pairs={{6,0},{14,8},{0,2},{8,10},{2,4},{10,12},{4,6},{12,14},{30,24},{22,... | collective-permute-start | bytes 589832 | tf_op jit(solution)/shard_map/ppermute | solution.py:265
  26.5 9.5 %all-to-all-start = ((bf16[8,24,512]{2,1,0:T(8,128)(2,1)}), bf16[8,24,512]{2,1,0:T(8,128)(2,1)S(1)}, u32[]{:S(2)}, u32[]{:S(2)}) async-start(bf16[8,24,512]{2,1,0:T(8,128)(2,1)} %shard_map.96), calls=%async_computation | async-start | bytes 393216 | tf_op jit(solution)/shard_map/all_to_all | solution.py:86
  36.2 6.8 %collective-permute-start.9 = (f32[8,128]{1,0:T(8,128)S(1)}, f32[8,128]{1,0:T(8,128)S(1)}, u32[]{:S(2)}, u32[]{:S(2)}) collective-permute-start(f32[8,128]{1,0:T(8,128)S(1)} %get-tuple-element.46.sums), channel_id=1, source_target_pairs={{0,32},{32,0},{64,96},{96,64},{1,33},{33,1},{65,97},{97,65},{8,40}... | collective-permute-start | bytes 12296 | tf_op jit(solution)/shard_map/ppermute | solution.py:293
  61.8 8.2 %collective-permute-start.10 = (bf16[8,24,512]{2,1,0:T(8,128)(2,1)S(1)}, bf16[8,24,512]{2,1,0:T(8,128)(2,1)S(1)}, u32[]{:S(2)}, u32[]{:S(2)}) collective-permute-start(bf16[8,24,512]{2,1,0:T(8,128)(2,1)S(1)} %get-tuple-element.47.refs_0_), channel_id=1, source_target_pairs={{12,0},{4,8},{14,2},{6,10},{8,4},{0,12},{10,6},{2,14},{20,24},{28,... | collective-permute-start | bytes 589832 | tf_op jit(solution)/shard_map/ppermute | solution.py:265
  62.8 8.1 %collective-permute-start.11 = (bf16[8,24,512]{2,1,0:T(8,128)(2,1)S(1)}, bf16[8,24,512]{2,1,0:T(8,128)(2,1)S(1)}, u32[]{:S(2)}, u32[]{:S(2)}) collective-permute-start(bf16[8,24,512]{2,1,0:T(8,128)(2,1)S(1)} %get-tuple-element.47.refs_0_), channel_id=1, source_target_pairs={{10,0},{2,8},{12,2},{4,10},{14,4},{6,12},{8,6},{0,14},{18,24},{26,... | collective-permute-start | bytes 589832 | tf_op jit(solution)/shard_map/ppermute | solution.py:265
  66.7 7.8 %collective-permute-start.12 = (bf16[8,24,512]{2,1,0:T(8,128)(2,1)S(1)}, bf16[8,24,512]{2,1,0:T(8,128)(2,1)S(1)}, u32[]{:S(2)}, u32[]{:S(2)}) collective-permute-start(bf16[8,24,512]{2,1,0:T(8,128)(2,1)S(1)} %get-tuple-element.47.refs_0_), channel_id=1, source_target_pairs={{14,0},{6,8},{8,2},{0,10},{10,4},{2,12},{12,6},{4,14},{22,24},{30,... | collective-permute-start | bytes 589832 | tf_op jit(solution)/shard_map/ppermute | solution.py:265
  74.6 14.2 %collective-permute-start.19 = (bf16[4,8,24,512]{3,2,1,0:T(8,128)(2,1)S(1)}, bf16[4,8,24,512]{3,2,1,0:T(8,128)(2,1)S(1)}, u32[]{:S(2)}, u32[]{:S(2)}) collective-permute-start(bf16[4,8,24,512]{3,2,1,0:T(8,128)(2,1)S(1)} %shard_map.105), channel_id=1, source_target_pairs={{0,32},{32,0},{64,96},{96,64},{1,33},{33,1},{65,97},{97,65},{8,40}... | collective-permute-start | bytes 2359304 | tf_op jit(solution)/shard_map/ppermute | solution.py:265
  77.3 4.8 %collective-permute-start.16 = (bf16[8,24,512]{2,1,0:T(8,128)(2,1)S(1)}, bf16[8,24,512]{2,1,0:T(8,128)(2,1)S(1)}, u32[]{:S(2)}, u32[]{:S(2)}) collective-permute-start(bf16[8,24,512]{2,1,0:T(8,128)(2,1)S(1)} %get-tuple-element.47.refs_0_), channel_id=1, source_target_pairs={{2,0},{10,8},{4,2},{12,10},{6,4},{14,12},{0,6},{8,14},{26,24},{18,... | collective-permute-start | bytes 589832 | tf_op jit(solution)/shard_map/ppermute | solution.py:265
  77.9 8.1 %collective-permute-start.17 = (bf16[8,24,512]{2,1,0:T(8,128)(2,1)S(1)}, bf16[8,24,512]{2,1,0:T(8,128)(2,1)S(1)}, u32[]{:S(2)}, u32[]{:S(2)}) collective-permute-start(bf16[8,24,512]{2,1,0:T(8,128)(2,1)S(1)} %get-tuple-element.47.refs_0_), channel_id=1, source_target_pairs={{6,0},{14,8},{0,2},{8,10},{2,4},{10,12},{4,6},{12,14},{30,24},{22,... | collective-permute-start | bytes 589832 | tf_op jit(solution)/shard_map/ppermute | solution.py:265
  78.8 8.9 %collective-permute-start.13 = (bf16[8,24,512]{2,1,0:T(8,128)(2,1)S(1)}, bf16[8,24,512]{2,1,0:T(8,128)(2,1)S(1)}, u32[]{:S(2)}, u32[]{:S(2)}) collective-permute-start(bf16[8,24,512]{2,1,0:T(8,128)(2,1)S(1)} %get-tuple-element.47.refs_0_), channel_id=1, source_target_pairs={{4,0},{12,8},{6,2},{14,10},{0,4},{8,12},{2,6},{10,14},{28,24},{20,... | collective-permute-start | bytes 589832 | tf_op jit(solution)/shard_map/ppermute | solution.py:265
  79.7 8.0 %collective-permute-start.14 = (bf16[8,24,512]{2,1,0:T(8,128)(2,1)S(1)}, bf16[8,24,512]{2,1,0:T(8,128)(2,1)S(1)}, u32[]{:S(2)}, u32[]{:S(2)}) collective-permute-start(bf16[8,24,512]{2,1,0:T(8,128)(2,1)S(1)} %get-tuple-element.47.refs_0_), channel_id=1, source_target_pairs={{8,0},{0,8},{10,2},{2,10},{12,4},{4,12},{14,6},{6,14},{16,24},{24,... | collective-permute-start | bytes 589832 | tf_op jit(solution)/shard_map/ppermute | solution.py:265
  86.1 3.8 %collective-permute-start.18 = (bf16[2,8,24,512]{3,2,1,0:T(8,128)(2,1)S(1)}, bf16[2,8,24,512]{3,2,1,0:T(8,128)(2,1)S(1)}, u32[]{:S(2)}, u32[]{:S(2)}) collective-permute-start(bf16[2,8,24,512]{3,2,1,0:T(8,128)(2,1)S(1)} %shard_map.104), channel_id=1, source_target_pairs={{0,32},{32,0},{64,96},{96,64},{1,33},{33,1},{65,97},{97,65},{8,40}... | collective-permute-start | bytes 1179656 | tf_op jit(solution)/shard_map/ppermute | solution.py:265
  87.7 2.3 %collective-permute-start.15 = (bf16[2,8,24,512]{3,2,1,0:T(8,128)(2,1)S(1)}, bf16[2,8,24,512]{3,2,1,0:T(8,128)(2,1)S(1)}, u32[]{:S(2)}, u32[]{:S(2)}) collective-permute-start(bf16[2,8,24,512]{3,2,1,0:T(8,128)(2,1)S(1)} %shard_map.103), channel_id=1, source_target_pairs={{0,32},{32,0},{64,96},{96,64},{1,33},{33,1},{65,97},{97,65},{8,40}... | collective-permute-start | bytes 1179656 | tf_op jit(solution)/shard_map/ppermute | solution.py:265
  (1 other events, 25.5 us)

commit v3 on v2

--- a/solution.py
+++ b/solution.py
@@ -317,26 +317,19 @@
         )(me, *arrays, *rows, *(() if first else (before,)))
 
     wide = [send(params, wide_shift(offset)) for offset in OFFSETS]
-    other_0 = send(join(params, *wide[0:3]), CORE_SWAP)
-    other_1 = send(join(*wide[3:5]), CORE_SWAP)
-    other_2 = send(join(*wide[5:7]), CORE_SWAP)
+    split = 4
+    other_0 = send(join(params, *wide[:split]), CORE_SWAP)
+    other_1 = send(join(*wide[split:]), CORE_SWAP)
     gathered, new_first, new_second, new_master, scaled_update = place(
-        [params, *wide[0:3]],
-        [(0, None, False, OWN)] + [(1 + k, None, False, OFFSETS[k]) for k in range(3)],
-        rows=(new_first, new_second, new_master, scaled_update),
+        [params], [(0, None, False, OWN)], rows=(new_first, new_second, new_master, scaled_update)
     )
     (gathered,) = place(
-        [*wide[3:7], other_0],
-        [(k, None, False, OFFSETS[3 + k]) for k in range(4)]
-        + [(4, 0, True, OWN)]
-        + [(4, 1 + k, True, OFFSETS[k]) for k in range(3)],
+        [*wide, other_0],
+        [(k, None, False, offset) for k, offset in enumerate(OFFSETS)]
+        + [(7, k, True, offset) for k, offset in enumerate((OWN,) + OFFSETS[:split])],
         gathered,
     )
-    (gathered,) = place(
-        [other_1, other_2],
-        [(0, k, True, OFFSETS[3 + k]) for k in range(2)] + [(1, k, True, OFFSETS[5 + k]) for k in range(2)],
-        gathered,
-    )
+    (gathered,) = place([other_1], [(0, k, True, offset) for k, offset in enumerate(OFFSETS[split:])], gathered)
     gathered = gathered.reshape(2 * CHIPS * ROWS, COLS)
     return (new_master, new_first, new_second, scaled_update, gathered)
 

time: 91.3 us -> 91.6 us (level)
  starting transfers between devices: 37.3 us -> 39.6 us
  waiting for transfers between devices: 26.2 us -> 24.2 us
    ppermute x19 -> x18, starting transfers between devices: 27.3 us -> 29.6 us  [send(): return lax.ppermute(value, 'i', pairs)]
    ppermute x19 -> x18, waiting for transfers between devices: 20.5 us -> 18.5 us  [send(): return lax.ppermute(value, 'i', pairs)]
  transfers between devices with their start and end apart: 21 -> 20, of which waited for: 11 -> 12; matrix products, arithmetic and copies ran while one was open for 0% -> 0% of each run, Pallas kernels for 5% -> 5%
where the time goes in v3:
time: 91.6 us; the launch traced here: 91.2 us
  starting transfers between devices  39.6 us (43%)
  waiting for transfers between devices  24.2 us (26%)
  blocking collectives  18.4 us (20%)
  Pallas kernels  8.08 us (9%)
    ppermute x18, starting transfers between devices, send(): return lax.ppermute(value, 'i', pairs)  29.6 us
    ppermute x18, waiting for transfers between devices, send(): return lax.ppermute(value, 'i', pairs)  18.5 us
    all_to_all x2, blocking collectives, exchange(): lax.all_to_all(value, 'i', 0, 0, axis_index_groups=groups, tiled=True)  18.4 us
    ppermute x1, starting transfers between devices, on_device(): arrived = lax.ppermute(sums, 'i', CORE_SWAP)  5.97 us
    all_to_all x1, waiting for transfers between devices, exchange(): lax.all_to_all(value, 'i', 0, 0, axis_index_groups=groups, tiled=True)  4.87 us
    all_to_all x1, starting transfers between devices, exchange(): lax.all_to_all(value, 'i', 0, 0, axis_index_groups=groups, tiled=True)  4.02 us
    pallas_call x3, Pallas kernels, place(): kernel(functools.partial(place_kernel, arrays=len(arrays), chunks=chunks,...  2.98 us
    pallas_call x2, Pallas kernels, take(): kernel(body, [SMEM, HBM], [VMEM] * 2, [half] * 2, scratch_shapes=[pltpu.S...  2.83 us
  transfers between devices with their start and end apart: 20, of which 12 were waited for; matrix products, arithmetic and copies ran while one was open for 0% of the time, Pallas kernels for 5%

profile of v3, /device:TPU:1, one launch (start us, length us, event | category | flops | bytes accessed | tf_op | source)
XLA Modules:
  0.0 91.2 jit_solution(1496866151931370905)
XLA Ops:
  0.6 1.4 %shard_map.93 = (bf16[4,8,24,512]{3,2,1,0:T(8,128)(2,1)S(1)}, bf16[4,8,24,512]{3,2,1,0:T(8,128)(2,1)S(1)}) custom-call(s32[1]{0:T(128)} %bitcast.me, bf16[128,24,512]{2,1,0:T(8,128)(2,1)} %bitcast.4), custom_call_target="tpu_custom_call" | custom-call | tf_op jit(solution)/shard_map/pallas_call | solution.py:272
  2.1 1.5 %collective-permute-start.1 = (bf16[4,8,24,512]{3,2,1,0:T(8,128)(2,1)S(1)}, bf16[4,8,24,512]{3,2,1,0:T(8,128)(2,1)S(1)}, u32[]{:S(2)}, u32[]{:S(2)}) collective-permute-start(bf16[4,8,24,512]{3,2,1,0:T(8,128)(2,1)S(1)} %get-tuple-element.35), channel_id=1, source_target_pairs={{0,32},{32,0},{64,96},{96,64},{1,33},{33,1},{65,97},{97,65},{8,40}... | collective-permute-start | bytes 2359304 | tf_op jit(solution)/shard_map/ppermute | solution.py:265
  3.6 1.4 %shard_map.92 = (bf16[4,8,24,512]{3,2,1,0:T(8,128)(2,1)S(1)}, bf16[4,8,24,512]{3,2,1,0:T(8,128)(2,1)S(1)}) custom-call(s32[1]{0:T(128)} %bitcast.me, bf16[128,24,512]{2,1,0:T(8,128)(2,1)} %bitcast.5), custom_call_target="tpu_custom_call" | custom-call | tf_op jit(solution)/shard_map/pallas_call | solution.py:272
  5.5 6.2 %collective-permute-start.2 = (bf16[8,24,512]{2,1,0:T(8,128)(2,1)S(1)}, bf16[8,24,512]{2,1,0:T(8,128)(2,1)S(1)}, u32[]{:S(2)}, u32[]{:S(2)}) collective-permute-start(bf16[8,24,512]{2,1,0:T(8,128)(2,1)S(1)} %get-tuple-element.36), channel_id=1, source_target_pairs={{12,0},{4,8},{14,2},{6,10},{8,4},{0,12},{10,6},{2,14},{20,24},{28,... | collective-permute-start | bytes 589832 | tf_op jit(solution)/shard_map/ppermute | solution.py:265
  12.0 3.3 %collective-permute-start.4 = (bf16[8,24,512]{2,1,0:T(8,128)(2,1)S(1)}, bf16[8,24,512]{2,1,0:T(8,128)(2,1)S(1)}, u32[]{:S(2)}, u32[]{:S(2)}) collective-permute-start(bf16[8,24,512]{2,1,0:T(8,128)(2,1)S(1)} %get-tuple-element.38), channel_id=1, source_target_pairs={{14,0},{6,8},{8,2},{0,10},{10,4},{2,12},{12,6},{4,14},{22,24},{30,... | collective-permute-start | bytes 589832 | tf_op jit(solution)/shard_map/ppermute | solution.py:265
  15.5 1.4 %collective-permute-start.6 = (bf16[8,24,512]{2,1,0:T(8,128)(2,1)S(1)}, bf16[8,24,512]{2,1,0:T(8,128)(2,1)S(1)}, u32[]{:S(2)}, u32[]{:S(2)}) collective-permute-start(bf16[8,24,512]{2,1,0:T(8,128)(2,1)S(1)} %get-tuple-element.40), channel_id=1, source_target_pairs={{8,0},{0,8},{10,2},{2,10},{12,4},{4,12},{14,6},{6,14},{16,24},{24,... | collective-permute-start | bytes 589832 | tf_op jit(solution)/shard_map/ppermute | solution.py:265
  16.9 1.9 %collective-permute-start.7 = (bf16[8,24,512]{2,1,0:T(8,128)(2,1)S(1)}, bf16[8,24,512]{2,1,0:T(8,128)(2,1)S(1)}, u32[]{:S(2)}, u32[]{:S(2)}) collective-permute-start(bf16[8,24,512]{2,1,0:T(8,128)(2,1)S(1)} %get-tuple-element.41), channel_id=1, source_target_pairs={{2,0},{10,8},{4,2},{12,10},{6,4},{14,12},{0,6},{8,14},{26,24},{18,... | collective-permute-start | bytes 589832 | tf_op jit(solution)/shard_map/ppermute | solution.py:265
  20.2 3.4 %collective-permute-done.5.refs_4_ = bf16[8,24,512]{2,1,0:T(8,128)(2,1)S(1)} collective-permute-done((bf16[8,24,512]{2,1,0:T(8,128)(2,1)S(1)}, bf16[8,24,512]{2,1,0:T(8,128)(2,1)S(1)}, u32[]{:S(2)}, u32[]{:S(2)}) %collective-permute-start.5) | collective-permute-done | bytes 196640 | tf_op jit(solution)/shard_map/ppermute | solution.py:265
  23.6 2.0 %collective-permute-done.8.refs_7_ = bf16[8,24,512]{2,1,0:T(8,128)(2,1)S(1)} collective-permute-done((bf16[8,24,512]{2,1,0:T(8,128)(2,1)S(1)}, bf16[8,24,512]{2,1,0:T(8,128)(2,1)S(1)}, u32[]{:S(2)}, u32[]{:S(2)}) %collective-permute-start.8) | collective-permute-done | bytes 196640 | tf_op jit(solution)/shard_map/ppermute | solution.py:265
  26.5 4.0 %all-to-all-start = ((bf16[8,24,512]{2,1,0:T(8,128)(2,1)}), bf16[8,24,512]{2,1,0:T(8,128)(2,1)S(1)}, u32[]{:S(2)}, u32[]{:S(2)}) async-start(bf16[8,24,512]{2,1,0:T(8,128)(2,1)} %shard_map.96), calls=%async_computation | async-start | bytes 393216 | tf_op jit(solution)/shard_map/all_to_all | solution.py:86
  31.2 4.9 %all-to-all-done.parts = bf16[8,24,512]{2,1,0:T(8,128)(2,1)S(1)} async-done(((bf16[8,24,512]{2,1,0:T(8,128)(2,1)}), bf16[8,24,512]{2,1,0:T(8,128)(2,1)S(1)}, u32[]{:S(2)}, u32[]{:S(2)}) %all-to-all-start) | async-done | bytes 196640 | tf_op jit(solution)/shard_map/all_to_all | solution.py:86
  36.2 6.0 %collective-permute-start.9 = (f32[8,128]{1,0:T(8,128)S(1)}, f32[8,128]{1,0:T(8,128)S(1)}, u32[]{:S(2)}, u32[]{:S(2)}) collective-permute-start(f32[8,128]{1,0:T(8,128)S(1)} %get-tuple-element.46.sums), channel_id=1, source_target_pairs={{0,32},{32,0},{64,96},{96,64},{1,33},{33,1},{65,97},{97,65},{8,40}... | collective-permute-start | bytes 12296 | tf_op jit(solution)/shard_map/ppermute | solution.py:293
  43.0 8.7 %all_to_all.15.sums = f32[8,8,128]{2,1,0:T(8,128)S(1)} all-to-all(f32[8,8,128]{2,1,0:T(8,128)S(1)} %shard_map.99), channel_id=1, replica_groups={{0,8,2,10,4,12,6,14},{24,16,26,18,28,20,30,22},{64,72,66,74,68,76,70,78..., dimensions={0} | all-to-all | bytes 65536 | tf_op jit(solution)/shard_map/all_to_all | solution.py:86
  51.7 9.8 %all_to_all.16.got = bf16[8,56,512]{2,1,0:T(8,128)(2,1)S(1)} all-to-all(bf16[8,56,512]{2,1,0:T(8,128)(2,1)S(1)} %shard_map.100), channel_id=1, replica_groups={{0,24,64,88,1,25,65,89},{8,16,72,80,9,17,73,81},{2,26,66,90,3,27,67,91}..., dimensions={0} | all-to-all | bytes 917504 | tf_op jit(solution)/shard_map/all_to_all | solution.py:86
  61.8 1.0 %collective-permute-start.14 = (bf16[8,24,512]{2,1,0:T(8,128)(2,1)S(1)}, bf16[8,24,512]{2,1,0:T(8,128)(2,1)S(1)}, u32[]{:S(2)}, u32[]{:S(2)}) collective-permute-start(bf16[8,24,512]{2,1,0:T(8,128)(2,1)S(1)} %get-tuple-element.47.refs_0_), channel_id=1, source_target_pairs={{12,0},{4,8},{14,2},{6,10},{8,4},{0,12},{10,6},{2,14},{20,24},{28,... | collective-permute-start | bytes 589832 | tf_op jit(solution)/shard_map/ppermute | solution.py:265
  62.8 3.9 %collective-permute-start.15 = (bf16[8,24,512]{2,1,0:T(8,128)(2,1)S(1)}, bf16[8,24,512]{2,1,0:T(8,128)(2,1)S(1)}, u32[]{:S(2)}, u32[]{:S(2)}) collective-permute-start(bf16[8,24,512]{2,1,0:T(8,128)(2,1)S(1)} %get-tuple-element.47.refs_0_), channel_id=1, source_target_pairs={{10,0},{2,8},{12,2},{4,10},{14,4},{6,12},{8,6},{0,14},{18,24},{26,... | collective-permute-start | bytes 589832 | tf_op jit(solution)/shard_map/ppermute | solution.py:265
  66.7 1.6 %collective-permute-start.17 = (bf16[8,24,512]{2,1,0:T(8,128)(2,1)S(1)}, bf16[8,24,512]{2,1,0:T(8,128)(2,1)S(1)}, u32[]{:S(2)}, u32[]{:S(2)}) collective-permute-start(bf16[8,24,512]{2,1,0:T(8,128)(2,1)S(1)} %get-tuple-element.47.refs_0_), channel_id=1, source_target_pairs={{4,0},{12,8},{6,2},{14,10},{0,4},{8,12},{2,6},{10,14},{28,24},{20,... | collective-permute-start | bytes 589832 | tf_op jit(solution)/shard_map/ppermute | solution.py:265
  68.3 1.7 %collective-permute-done.14.refs_1_.refs_0_ = bf16[8,24,512]{2,1,0:T(8,128)(2,1)S(1)} collective-permute-done((bf16[8,24,512]{2,1,0:T(8,128)(2,1)S(1)}, bf16[8,24,512]{2,1,0:T(8,128)(2,1)S(1)}, u32[]{:S(2)}, u32[]{:S(2)}) %collective-permute-start.14) | collective-permute-done | bytes 196640 | tf_op jit(solution)/shard_map/ppermute | solution.py:265
  70.9 3.8 %collective-permute-done.16.refs_3_.refs_2_ = bf16[8,24,512]{2,1,0:T(8,128)(2,1)S(1)} collective-permute-done((bf16[8,24,512]{2,1,0:T(8,128)(2,1)S(1)}, bf16[8,24,512]{2,1,0:T(8,128)(2,1)S(1)}, u32[]{:S(2)}, u32[]{:S(2)}) %collective-permute-start.16) | collective-permute-done | bytes 196640 | tf_op jit(solution)/shard_map/ppermute | solution.py:265
  75.2 2.2 %collective-permute-start.18 = (bf16[5,8,24,512]{3,2,1,0:T(8,128)(2,1)S(1)}, bf16[5,8,24,512]{3,2,1,0:T(8,128)(2,1)S(1)}, u32[]{:S(2)}, u32[]{:S(2)}) collective-permute-start(bf16[5,8,24,512]{3,2,1,0:T(8,128)(2,1)S(1)} %shard_map.104), channel_id=1, source_target_pairs={{0,32},{32,0},{64,96},{96,64},{1,33},{33,1},{65,97},{97,65},{8,40}... | collective-permute-start | bytes 2949128 | tf_op jit(solution)/shard_map/ppermute | solution.py:265
  79.3 3.7 %collective-permute-done.10.refs_0_.refs_4_ = bf16[8,24,512]{2,1,0:T(8,128)(2,1)S(1)} collective-permute-done((bf16[8,24,512]{2,1,0:T(8,128)(2,1)S(1)}, bf16[8,24,512]{2,1,0:T(8,128)(2,1)S(1)}, u32[]{:S(2)}, u32[]{:S(2)}) %collective-permute-start.10) | collective-permute-done | bytes 196640 | tf_op jit(solution)/shard_map/ppermute | solution.py:265
  83.1 1.4 %collective-permute-done.12.refs_2_.refs_6_ = bf16[8,24,512]{2,1,0:T(8,128)(2,1)S(1)} collective-permute-done((bf16[8,24,512]{2,1,0:T(8,128)(2,1)S(1)}, bf16[8,24,512]{2,1,0:T(8,128)(2,1)S(1)}, u32[]{:S(2)}, u32[]{:S(2)}) %collective-permute-start.12) | collective-permute-done | bytes 196640 | tf_op jit(solution)/shard_map/ppermute | solution.py:265
  84.5 3.6 %collective-permute-start.13 = (bf16[3,8,24,512]{3,2,1,0:T(8,128)(2,1)S(1)}, bf16[3,8,24,512]{3,2,1,0:T(8,128)(2,1)S(1)}, u32[]{:S(2)}, u32[]{:S(2)}) collective-permute-start(bf16[3,8,24,512]{3,2,1,0:T(8,128)(2,1)S(1)} %shard_map.103), channel_id=1, source_target_pairs={{0,32},{32,0},{64,96},{96,64},{1,33},{33,1},{65,97},{97,65},{8,40}... | collective-permute-start | bytes 1769480 | tf_op jit(solution)/shard_map/ppermute | solution.py:265
  88.9 1.4 %shard_map.105.refs_1_ = bf16[128,24,512]{2,1,0:T(8,128)(2,1)} custom-call(s32[1]{0:T(128)} %bitcast.me, bf16[8,24,512]{2,1,0:T(8,128)(2,1)S(1)} %collective-permute-done.14.refs_1_.refs_0_, bf16[8,24,512]{2,1,0:T(8,128)(2,1)S(1)} %collective-permute-done.15.refs_2_.refs_1_, ...), custom_call_target="tpu_custom_call", output_to_operand_aliasing={{}: (9, {})} | custom-call | tf_op jit(solution)/shard_map/pallas_call | solution.py:310
  (41 shorter events, 10.2 us)
Async XLA Ops:
  2.1 3.4 %collective-permute-start.1 = (bf16[4,8,24,512]{3,2,1,0:T(8,128)(2,1)S(1)}, bf16[4,8,24,512]{3,2,1,0:T(8,128)(2,1)S(1)}, u32[]{:S(2)}, u32[]{:S(2)}) collective-permute-start(bf16[4,8,24,512]{3,2,1,0:T(8,128)(2,1)S(1)} %get-tuple-element.35), channel_id=1, source_target_pairs={{0,32},{32,0},{64,96},{96,64},{1,33},{33,1},{65,97},{97,65},{8,40}... | collective-permute-start | bytes 2359304 | tf_op jit(solution)/shard_map/ppermute | solution.py:265
  3.6 11.8 %collective-permute-start = (bf16[4,8,24,512]{3,2,1,0:T(8,128)(2,1)S(1)}, bf16[4,8,24,512]{3,2,1,0:T(8,128)(2,1)S(1)}, u32[]{:S(2)}, u32[]{:S(2)}) collective-permute-start(bf16[4,8,24,512]{3,2,1,0:T(8,128)(2,1)S(1)} %get-tuple-element.32), channel_id=1, source_target_pairs={{0,32},{32,0},{64,96},{96,64},{1,33},{33,1},{65,97},{97,65},{8,40}... | collective-permute-start | bytes 2359304 | tf_op jit(solution)/shard_map/ppermute | solution.py:265
  5.0 25.5 %copy-start = (f32[24,512]{1,0:T(8,128)S(1)}, f32[24,512]{1,0:T(8,128)}, u32[]{:S(2)}) copy-start(f32[24,512]{1,0:T(8,128)} %weights.7) | copy-start | bytes 147460
  5.0 25.5 %copy-start.3 = (s32[24]{0:T(128)S(1)}, s32[24]{0:T(128)}, u32[]{:S(2)}) copy-start(s32[24]{0:T(128)} %ids.1) | copy-start | bytes 292
  5.1 31.0 %copy-start.1 = (f32[24,512]{1,0:T(8,128)S(1)}, f32[24,512]{1,0:T(8,128)}, u32[]{:S(2)}) copy-start(f32[24,512]{1,0:T(8,128)} %first.1) | copy-start | bytes 147460
  5.1 31.0 %copy-start.2 = (f32[24,512]{1,0:T(8,128)S(1)}, f32[24,512]{1,0:T(8,128)}, u32[]{:S(2)}) copy-start(f32[24,512]{1,0:T(8,128)} %second.1) | copy-start | bytes 147460
  5.5 11.3 %collective-permute-start.2 = (bf16[8,24,512]{2,1,0:T(8,128)(2,1)S(1)}, bf16[8,24,512]{2,1,0:T(8,128)(2,1)S(1)}, u32[]{:S(2)}, u32[]{:S(2)}) collective-permute-start(bf16[8,24,512]{2,1,0:T(8,128)(2,1)S(1)} %get-tuple-element.36), channel_id=1, source_target_pairs={{12,0},{4,8},{14,2},{6,10},{8,4},{0,12},{10,6},{2,14},{20,24},{28,... | collective-permute-start | bytes 589832 | tf_op jit(solution)/shard_map/ppermute | solution.py:265
  11.8 7.0 %collective-permute-start.3 = (bf16[8,24,512]{2,1,0:T(8,128)(2,1)S(1)}, bf16[8,24,512]{2,1,0:T(8,128)(2,1)S(1)}, u32[]{:S(2)}, u32[]{:S(2)}) collective-permute-start(bf16[8,24,512]{2,1,0:T(8,128)(2,1)S(1)} %get-tuple-element.37), channel_id=1, source_target_pairs={{10,0},{2,8},{12,2},{4,10},{14,4},{6,12},{8,6},{0,14},{18,24},{26,... | collective-permute-start | bytes 589832 | tf_op jit(solution)/shard_map/ppermute | solution.py:265
  12.0 8.1 %collective-permute-start.4 = (bf16[8,24,512]{2,1,0:T(8,128)(2,1)S(1)}, bf16[8,24,512]{2,1,0:T(8,128)(2,1)S(1)}, u32[]{:S(2)}, u32[]{:S(2)}) collective-permute-start(bf16[8,24,512]{2,1,0:T(8,128)(2,1)S(1)} %get-tuple-element.38), channel_id=1, source_target_pairs={{14,0},{6,8},{8,2},{0,10},{10,4},{2,12},{12,6},{4,14},{22,24},{30,... | collective-permute-start | bytes 589832 | tf_op jit(solution)/shard_map/ppermute | solution.py:265
  15.4 8.2 %collective-permute-start.5 = (bf16[8,24,512]{2,1,0:T(8,128)(2,1)S(1)}, bf16[8,24,512]{2,1,0:T(8,128)(2,1)S(1)}, u32[]{:S(2)}, u32[]{:S(2)}) collective-permute-start(bf16[8,24,512]{2,1,0:T(8,128)(2,1)S(1)} %get-tuple-element.39), channel_id=1, source_target_pairs={{4,0},{12,8},{6,2},{14,10},{0,4},{8,12},{2,6},{10,14},{28,24},{20,... | collective-permute-start | bytes 589832 | tf_op jit(solution)/shard_map/ppermute | solution.py:265
  15.5 8.1 %collective-permute-start.6 = (bf16[8,24,512]{2,1,0:T(8,128)(2,1)S(1)}, bf16[8,24,512]{2,1,0:T(8,128)(2,1)S(1)}, u32[]{:S(2)}, u32[]{:S(2)}) collective-permute-start(bf16[8,24,512]{2,1,0:T(8,128)(2,1)S(1)} %get-tuple-element.40), channel_id=1, source_target_pairs={{8,0},{0,8},{10,2},{2,10},{12,4},{4,12},{14,6},{6,14},{16,24},{24,... | collective-permute-start | bytes 589832 | tf_op jit(solution)/shard_map/ppermute | solution.py:265
  16.9 6.7 %collective-permute-start.7 = (bf16[8,24,512]{2,1,0:T(8,128)(2,1)S(1)}, bf16[8,24,512]{2,1,0:T(8,128)(2,1)S(1)}, u32[]{:S(2)}, u32[]{:S(2)}) collective-permute-start(bf16[8,24,512]{2,1,0:T(8,128)(2,1)S(1)} %get-tuple-element.41), channel_id=1, source_target_pairs={{2,0},{10,8},{4,2},{12,10},{6,4},{14,12},{0,6},{8,14},{26,24},{18,... | collective-permute-start | bytes 589832 | tf_op jit(solution)/shard_map/ppermute | solution.py:265
  18.8 6.8 %collective-permute-start.8 = (bf16[8,24,512]{2,1,0:T(8,128)(2,1)S(1)}, bf16[8,24,512]{2,1,0:T(8,128)(2,1)S(1)}, u32[]{:S(2)}, u32[]{:S(2)}) collective-permute-start(bf16[8,24,512]{2,1,0:T(8,128)(2,1)S(1)} %get-tuple-element.42), channel_id=1, source_target_pairs={{6,0},{14,8},{0,2},{8,10},{2,4},{10,12},{4,6},{12,14},{30,24},{22,... | collective-permute-start | bytes 589832 | tf_op jit(solution)/shard_map/ppermute | solution.py:265
  26.5 9.5 %all-to-all-start = ((bf16[8,24,512]{2,1,0:T(8,128)(2,1)}), bf16[8,24,512]{2,1,0:T(8,128)(2,1)S(1)}, u32[]{:S(2)}, u32[]{:S(2)}) async-start(bf16[8,24,512]{2,1,0:T(8,128)(2,1)} %shard_map.96), calls=%async_computation | async-start | bytes 393216 | tf_op jit(solution)/shard_map/all_to_all | solution.py:86
  36.2 6.8 %collective-permute-start.9 = (f32[8,128]{1,0:T(8,128)S(1)}, f32[8,128]{1,0:T(8,128)S(1)}, u32[]{:S(2)}, u32[]{:S(2)}) collective-permute-start(f32[8,128]{1,0:T(8,128)S(1)} %get-tuple-element.46.sums), channel_id=1, source_target_pairs={{0,32},{32,0},{64,96},{96,64},{1,33},{33,1},{65,97},{97,65},{8,40}... | collective-permute-start | bytes 12296 | tf_op jit(solution)/shard_map/ppermute | solution.py:293
  61.8 8.2 %collective-permute-start.14 = (bf16[8,24,512]{2,1,0:T(8,128)(2,1)S(1)}, bf16[8,24,512]{2,1,0:T(8,128)(2,1)S(1)}, u32[]{:S(2)}, u32[]{:S(2)}) collective-permute-start(bf16[8,24,512]{2,1,0:T(8,128)(2,1)S(1)} %get-tuple-element.47.refs_0_), channel_id=1, source_target_pairs={{12,0},{4,8},{14,2},{6,10},{8,4},{0,12},{10,6},{2,14},{20,24},{28,... | collective-permute-start | bytes 589832 | tf_op jit(solution)/shard_map/ppermute | solution.py:265
  62.8 8.1 %collective-permute-start.15 = (bf16[8,24,512]{2,1,0:T(8,128)(2,1)S(1)}, bf16[8,24,512]{2,1,0:T(8,128)(2,1)S(1)}, u32[]{:S(2)}, u32[]{:S(2)}) collective-permute-start(bf16[8,24,512]{2,1,0:T(8,128)(2,1)S(1)} %get-tuple-element.47.refs_0_), channel_id=1, source_target_pairs={{10,0},{2,8},{12,2},{4,10},{14,4},{6,12},{8,6},{0,14},{18,24},{26,... | collective-permute-start | bytes 589832 | tf_op jit(solution)/shard_map/ppermute | solution.py:265
  66.7 8.1 %collective-permute-start.16 = (bf16[8,24,512]{2,1,0:T(8,128)(2,1)S(1)}, bf16[8,24,512]{2,1,0:T(8,128)(2,1)S(1)}, u32[]{:S(2)}, u32[]{:S(2)}) collective-permute-start(bf16[8,24,512]{2,1,0:T(8,128)(2,1)S(1)} %get-tuple-element.47.refs_0_), channel_id=1, source_target_pairs={{14,0},{6,8},{8,2},{0,10},{10,4},{2,12},{12,6},{4,14},{22,24},{30,... | collective-permute-start | bytes 589832 | tf_op jit(solution)/shard_map/ppermute | solution.py:265
  66.7 8.4 %collective-permute-start.17 = (bf16[8,24,512]{2,1,0:T(8,128)(2,1)S(1)}, bf16[8,24,512]{2,1,0:T(8,128)(2,1)S(1)}, u32[]{:S(2)}, u32[]{:S(2)}) collective-permute-start(bf16[8,24,512]{2,1,0:T(8,128)(2,1)S(1)} %get-tuple-element.47.refs_0_), channel_id=1, source_target_pairs={{4,0},{12,8},{6,2},{14,10},{0,4},{8,12},{2,6},{10,14},{28,24},{20,... | collective-permute-start | bytes 589832 | tf_op jit(solution)/shard_map/ppermute | solution.py:265
  75.2 13.8 %collective-permute-start.18 = (bf16[5,8,24,512]{3,2,1,0:T(8,128)(2,1)S(1)}, bf16[5,8,24,512]{3,2,1,0:T(8,128)(2,1)S(1)}, u32[]{:S(2)}, u32[]{:S(2)}) collective-permute-start(bf16[5,8,24,512]{3,2,1,0:T(8,128)(2,1)S(1)} %shard_map.104), channel_id=1, source_target_pairs={{0,32},{32,0},{64,96},{96,64},{1,33},{33,1},{65,97},{97,65},{8,40}... | collective-permute-start | bytes 2949128 | tf_op jit(solution)/shard_map/ppermute | solution.py:265
  77.3 5.7 %collective-permute-start.10 = (bf16[8,24,512]{2,1,0:T(8,128)(2,1)S(1)}, bf16[8,24,512]{2,1,0:T(8,128)(2,1)S(1)}, u32[]{:S(2)}, u32[]{:S(2)}) collective-permute-start(bf16[8,24,512]{2,1,0:T(8,128)(2,1)S(1)} %get-tuple-element.47.refs_0_), channel_id=1, source_target_pairs={{8,0},{0,8},{10,2},{2,10},{12,4},{4,12},{14,6},{6,14},{16,24},{24,... | collective-permute-start | bytes 589832 | tf_op jit(solution)/shard_map/ppermute | solution.py:265
  77.9 5.2 %collective-permute-start.11 = (bf16[8,24,512]{2,1,0:T(8,128)(2,1)S(1)}, bf16[8,24,512]{2,1,0:T(8,128)(2,1)S(1)}, u32[]{:S(2)}, u32[]{:S(2)}) collective-permute-start(bf16[8,24,512]{2,1,0:T(8,128)(2,1)S(1)} %get-tuple-element.47.refs_0_), channel_id=1, source_target_pairs={{2,0},{10,8},{4,2},{12,10},{6,4},{14,12},{0,6},{8,14},{26,24},{18,... | collective-permute-start | bytes 589832 | tf_op jit(solution)/shard_map/ppermute | solution.py:265
  78.8 5.7 %collective-permute-start.12 = (bf16[8,24,512]{2,1,0:T(8,128)(2,1)S(1)}, bf16[8,24,512]{2,1,0:T(8,128)(2,1)S(1)}, u32[]{:S(2)}, u32[]{:S(2)}) collective-permute-start(bf16[8,24,512]{2,1,0:T(8,128)(2,1)S(1)} %get-tuple-element.47.refs_0_), channel_id=1, source_target_pairs={{6,0},{14,8},{0,2},{8,10},{2,4},{10,12},{4,6},{12,14},{30,24},{22,... | collective-permute-start | bytes 589832 | tf_op jit(solution)/shard_map/ppermute | solution.py:265
  84.5 5.8 %collective-permute-start.13 = (bf16[3,8,24,512]{3,2,1,0:T(8,128)(2,1)S(1)}, bf16[3,8,24,512]{3,2,1,0:T(8,128)(2,1)S(1)}, u32[]{:S(2)}, u32[]{:S(2)}) collective-permute-start(bf16[3,8,24,512]{3,2,1,0:T(8,128)(2,1)S(1)} %shard_map.103), channel_id=1, source_target_pairs={{0,32},{32,0},{64,96},{96,64},{1,33},{33,1},{65,97},{97,65},{8,40}... | collective-permute-start | bytes 1769480 | tf_op jit(solution)/shard_map/ppermute | solution.py:265

commit v4 on v3

--- a/solution.py
+++ b/solution.py
@@ -49,14 +49,17 @@
     return device >> 6, (device >> 5) & 1, (device >> 3) & 3, (device >> 1) & 3, device & 1
 
 
-def wide_place(device):
+def group_places(device):
     z_lo, core, y, x, z_hi = place_of(device)
-    return jnp.where(core == 0, 2 * x + ((y ^ (y >> 1)) & 1), 2 * (2 * z_hi + z_lo) + (y >> 1))
+    p = 2 * x + ((y ^ (y >> 1)) & 1)
+    q = 2 * (2 * z_hi + z_lo) + (y >> 1)
+    return jnp.where(core == 0, p, q), jnp.where(core == 0, q, p)
 
 
 OFFSETS = ((2, 1), (3, 1), (1, 1), (2, 0), (0, 1), (3, 0), (1, 0))
 OWN = (0, 0)
 HALVES = (OFFSETS[:4], OFFSETS[4:] + (OWN,))
+RINGS = (0, 2, 3, 1)
 
 
 def source_place(a, offset):
@@ -69,8 +72,8 @@
     return ((((a >> 1) + ring) & 3) << 1) + ((a & 1) ^ pair)
 
 
-def wide_shift(offset):
-    return [(group[source_place(a, offset)], group[a]) for group in WIDE for a in range(GROUP)]
+def shift(groups, offset):
+    return [(group[source_place(a, offset)], group[a]) for group in groups for a in range(GROUP)]
 
 
 def owner_of(core, a, b):
@@ -121,32 +124,35 @@
     sums[...] = base[...] + jnp.broadcast_to(per_tensor, (8, 128))
 
 
-PAY = 2 * ROWS + 8
-
-
-def pay_kernel(update, weights, sums, pay):
-    total = sums[0, 0:1, :]
-    for k in range(1, GROUP):
-        total = total + sums[k, 0:1, :]
-    high = total.astype(BF16)
-    rest = total - high.astype(F32)
-    mid = rest.astype(BF16)
-    low = (rest - mid.astype(F32)).astype(BF16)
+PAY = ROWS + 8
+
+
+def in_three(total):
+    high = total.astype(BF16).astype(F32)
+    rest = total - high
+    mid = rest.astype(BF16).astype(F32)
+    low = (rest - mid).astype(BF16).astype(F32)
     row = lax.broadcasted_iota(jnp.int32, (8, 128), 0)
-    three = jnp.where(
-        row == 0, high.astype(F32), jnp.where(row == 1, mid.astype(F32), jnp.where(row == 2, low.astype(F32), 0.0))
-    )
-    three = jnp.concatenate([three, jnp.zeros((8, COLS - 128), F32)], axis=1)
-    one = jnp.concatenate([update[...], weights[...], three], axis=0).astype(BF16)
+    three = jnp.where(row == 0, high, jnp.where(row == 1, mid, jnp.where(row == 2, low, 0.0)))
+    return jnp.concatenate([three, jnp.zeros((8, COLS - 128), F32)], axis=1)
+
+
+def pay_kernel(update, sums, pay):
+    one = jnp.concatenate([update[...], in_three(sums[0:1, :])], axis=0).astype(BF16)
     for k in range(GROUP):
         pay[k] = one
 
 
-def trust_and_runs(got):
+def open_kernel(got, updates):
     total = jnp.zeros((1, 128), F32)
     for k in range(GROUP):
-        three = got[k, 2 * ROWS :, 0:128].astype(F32)
+        updates[k] = got[k, 0:ROWS]
+        three = got[k, ROWS:, 0:128].astype(F32)
         total = total + ((three[0:1] + three[1:2]) + three[2:3])
+    updates[GROUP] = jnp.concatenate([in_three(total), jnp.zeros((ROWS - 8, COLS), F32)], axis=0).astype(BF16)
+
+
+def trust_and_runs(total):
     update_sq = pltpu.roll(total, 124, 1)
     count = pltpu.roll(total, 120, 1)
     lane = lane_index(1)
@@ -165,17 +171,41 @@
     return jnp.sum(jnp.where(here, trust, 0.0), axis=1, keepdims=True)
 
 
-def params_kernel(me, got, update, weights, params, new_master, scaled_update):
-    trust, start, end = trust_and_runs(got)
-    core = (me[0] >> 5) & 1
-    place = wide_place(me[0])
-    for b in range(GROUP):
-        factor = row_trust(owner_of(core, place, b) * ROWS, trust, start, end)
-        block = got[b, ROWS : 2 * ROWS].astype(F32) - step_size * (factor * got[b, 0:ROWS].astype(F32))
-        params[b] = block.astype(BF16)
-    scaled = row_trust(me[0] * ROWS, trust, start, end) * update[...]
+def core_total_kernel(me, *refs):
+    parts, (out, totals) = refs[:GROUP], refs[GROUP:]
+    place = group_places(me[0])[0]
+    for part, offset in zip(parts, OFFSETS + (OWN,)):
+        three = part[GROUP, 0:8, 0:128].astype(F32)
+        total = (three[0:1] + three[1:2]) + three[2:3]
+        totals[source_place(place, offset)] = jnp.broadcast_to(total, (8, 128))
+    total = totals[0]
+    for k in range(1, GROUP):
+        total = total + totals[k]
+    out[...] = total
+
+
+def trust_kernel(me, total, arrived, update, weights, out, new_master, scaled_update):
+    three = trust_and_runs(total[0:1, :] + arrived[0:1, :])
+    for k in range(3):
+        out[k] = jnp.broadcast_to(three[k], (8, 128))
+    scaled = row_trust(me[0] * ROWS, *three) * update[...]
     scaled_update[...] = scaled
     new_master[...] = weights[...] - step_size * scaled
+
+
+def params_kernel(me, trust, *refs, offsets):
+    updates, held, params = refs[: len(offsets)], refs[len(offsets) : -1], refs[-1]
+    three = trust[0, 0:1, :], trust[1, 0:1, :], trust[2, 0:1, :]
+    core = (me[0] >> 5) & 1
+    place, place_b = group_places(me[0])
+    for ring, weights in zip(RINGS, held):
+        for pair in range(2):
+            b = source_place(place_b, (ring, pair))
+            for j, offset in enumerate(offsets):
+                factor = row_trust(owner_of(core, source_place(place, offset), b) * ROWS, *three)
+                member = (OFFSETS + (OWN,)).index(offset)
+                block = weights[pair, member].astype(F32) - step_size * (factor * updates[j][b].astype(F32))
+                params[j, b] = block.astype(BF16)
 
 
 def take_kernel(me, gradients, *refs, other):
@@ -184,30 +214,28 @@
     core = (device >> 5) & 1
     for k, offsets in enumerate(HALVES):
         for j, offset in enumerate(offsets):
-            a = target_place(wide_place(device), offset)
+            a = target_place(group_places(device)[0], offset)
             for b in range(GROUP):
                 pltpu.make_async_copy(gradients.at[owner_of(core, a, b)], halves[k].at[j, b], done.at[k]).start()
     for k in range(2):
         pltpu.make_async_copy(halves[k], halves[k], done.at[k]).wait()
 
 
-def add_kernel(kept, arrived, *both):
+def add_kernel(kept, arrived, weights, *both):
     for j, out in enumerate(both):
-        out[...] = kept[j] + arrived[j]
+        out[0:GROUP] = kept[j] + arrived[j]
+        out[GROUP] = weights[...].astype(BF16)
 
 
 def total_kernel(*refs):
+    parts, (total, members) = refs[:-2], refs[-2:]
     for b in range(GROUP):
-        summed = refs[0][b].astype(F32)
-        for part in refs[1:-1]:
+        summed = parts[GROUP - 1][b].astype(F32)
+        for part in parts[: GROUP - 1]:
             summed = summed + part[b].astype(F32)
-        refs[-1][b] = summed.astype(BF16)
-
-
-def chip_sums_kernel(sums, arrived, out):
-    both = sums[...] + arrived[...]
-    for k in range(GROUP):
-        out[k] = both
+        total[b] = summed.astype(BF16)
+    for j, part in enumerate(parts):
+        members[j] = part[GROUP]
 
 
 def join_kernel(*refs):
@@ -224,7 +252,7 @@
     for array, index, other, offset in chunks:
         device = me[0] ^ (32 if other else 0)
         core = (device >> 5) & 1
-        a = source_place(wide_place(device), offset)
+        a = source_place(group_places(device)[0], offset)
         part = blocks[array] if index is None else blocks[array].at[index]
         for b in range(GROUP):
             pltpu.make_async_copy(part.at[b], out.at[owner_of(core, a, b)], done).start()
@@ -245,7 +273,7 @@
     return jax.ShapeDtypeStruct(shape, dtype)
 
 
-def kernel(body, ins, outs, shapes, limit=8, **more):
+def kernel(body, ins, outs, shapes, limit=4, **more):
     return pl.pallas_call(
         body,
         out_shape=shapes,
@@ -277,31 +305,49 @@
     arrived = [send(sent[k], CORE_SWAP) for k in range(2)]
     kept = take(False)
     chunks = []
+    more = pltpu.VMEM((GROUP + 1, ROWS, COLS), BF16)
     for k in range(2):
-        chunks += kernel(add_kernel, [VMEM] * 2, [VMEM] * 4, [chunk] * 4)(kept[k], arrived[k])
+        chunks += kernel(add_kernel, [VMEM] * 3, [VMEM] * 4, [more] * 4)(kept[k], arrived[k], master_weights)
     tensor, sums = kernel(
         before_kernel, [VMEM, SMEM], (VMEM, VMEM), (pltpu.VMEM((ROWS, 128), jnp.int32), pltpu.VMEM((8, 128), F32))
     )(master_weights, tensor_ids)
-    wide = [send(chunks[k], wide_shift(offset)) for k, offset in enumerate(OFFSETS)]
-    total = kernel(total_kernel, [VMEM] * 8, VMEM, chunk)(chunks[7], *wide)
+    wide = [send(chunks[k], shift(WIDE, offset)) for k, offset in enumerate(OFFSETS)]
+    total, members = kernel(total_kernel, [VMEM] * 8, [VMEM] * 2, [chunk] * 2)(*wide, chunks[7])
     parts = exchange(total, NARROW)
+    pair = send(members, shift(NARROW, (0, 1)))
+    pair = kernel(join_kernel, [VMEM] * 2, VMEM, pltpu.VMEM((2, GROUP, ROWS, COLS), BF16))(members, pair)
+    held = [pair] + [send(pair, shift(NARROW, (ring, 0))) for ring in RINGS[1:]]
 
     new_first, new_second, update, sums = kernel(
         update_kernel, [VMEM] * 6, (VMEM,) * 4, (own_f32, own_f32, own_f32, pltpu.VMEM((8, 128), F32))
     )(parts, master_weights, first_moment, second_moment, tensor, sums)
 
-    arrived = lax.ppermute(sums, "i", CORE_SWAP)
-    sums = kernel(chip_sums_kernel, [VMEM] * 2, VMEM, pltpu.VMEM((GROUP, 8, 128), F32))(sums, arrived)
-    sums = exchange(sums, WIDE)
-    pay = kernel(pay_kernel, [VMEM] * 3, VMEM, pltpu.VMEM((GROUP, PAY, COLS), BF16))(update, master_weights, sums)
+    pay = kernel(pay_kernel, [VMEM] * 2, VMEM, of((GROUP, PAY, COLS), BF16))(update, sums)
     got = exchange(pay, NARROW)
-
-    params, new_master, scaled_update = kernel(
-        params_kernel, [SMEM] + [VMEM] * 3, (VMEM,) * 3, (chunk, own_f32, own_f32)
-    )(me, got, update, master_weights)
-    join = lambda *parts: kernel(
-        join_kernel, [VMEM] * len(parts), VMEM, pltpu.VMEM((len(parts), GROUP, ROWS, COLS), BF16)
-    )(*parts)
+    updates = kernel(open_kernel, [VMEM], VMEM, more)(got)
+    wide = [send(updates, shift(WIDE, offset)) for offset in OFFSETS]
+    total = kernel(
+        core_total_kernel,
+        [SMEM] + [VMEM] * GROUP,
+        VMEM,
+        pltpu.VMEM((8, 128), F32),
+        scratch_shapes=[pltpu.VMEM((GROUP, 8, 128), F32)],
+    )(me, *wide, updates)
+    arrived = send(total, CORE_SWAP)
+    trust, new_master, scaled_update = kernel(
+        trust_kernel, [SMEM] + [VMEM] * 4, (VMEM,) * 3, (pltpu.VMEM((3, 8, 128), F32), own_f32, own_f32)
+    )(me, total, arrived, update, master_weights)
+
+    def params_of(offsets, values):
+        body = functools.partial(params_kernel, offsets=offsets)
+        shape = pltpu.VMEM((len(offsets), GROUP, ROWS, COLS), BF16)
+        return kernel(body, [SMEM] + [VMEM] * (5 + len(values)), VMEM, shape)(me, trust, *values, *held)
+
+    first, last = (OWN,) + OFFSETS[:3], OFFSETS[3:]
+    params_0 = params_of(first, (updates, *wide[:3]))
+    params_1 = params_of(last, wide[3:])
+    other_0 = send(params_0, CORE_SWAP)
+    other_1 = send(params_1, CORE_SWAP)
     every = of((2 * CHIPS, ROWS, COLS), BF16)
 
     def place(arrays, chunks, before=None, rows=()):
@@ -316,20 +362,14 @@
             scratch_shapes=[pltpu.SemaphoreType.DMA] + ([pltpu.SemaphoreType.DMA((len(rows),))] if rows else []),
         )(me, *arrays, *rows, *(() if first else (before,)))
 
-    wide = [send(params, wide_shift(offset)) for offset in OFFSETS]
-    split = 4
-    other_0 = send(join(params, *wide[:split]), CORE_SWAP)
-    other_1 = send(join(*wide[split:]), CORE_SWAP)
+    listed = lambda array, other, offsets: [(array, k, other, offset) for k, offset in enumerate(offsets)]
     gathered, new_first, new_second, new_master, scaled_update = place(
-        [params], [(0, None, False, OWN)], rows=(new_first, new_second, new_master, scaled_update)
+        [params_0, params_1],
+        listed(0, False, first) + listed(1, False, last),
+        rows=(new_first, new_second, new_master, scaled_update),
     )
-    (gathered,) = place(
-        [*wide, other_0],
-        [(k, None, False, offset) for k, offset in enumerate(OFFSETS)]
-        + [(7, k, True, offset) for k, offset in enumerate((OWN,) + OFFSETS[:split])],
-        gathered,
-    )
-    (gathered,) = place([other_1], [(0, k, True, offset) for k, offset in enumerate(OFFSETS[split:])], gathered)
+    (gathered,) = place([other_0], listed(0, True, first), gathered)
+    (gathered,) = place([other_1], listed(0, True, last), gathered)
     gathered = gathered.reshape(2 * CHIPS * ROWS, COLS)
     return (new_master, new_first, new_second, scaled_update, gathered)
 

time: 91.6 us -> 89.3 us (0.975)
  the two profiles are of different devices: /device:TPU:1 before, /device:TPU:9 now
where the time goes in v4:
time: 89.3 us; the launch traced here: 88.8 us
  starting transfers between devices  49.3 us (55%)
  waiting for transfers between devices  29.2 us (33%)
  Pallas kernels  9.55 us (11%)
    ppermute x23, starting transfers between devices, send(): return lax.ppermute(value, 'i', pairs)  38.9 us
    ppermute x23, waiting for transfers between devices, send(): return lax.ppermute(value, 'i', pairs)  19.8 us
    all_to_all x2, starting transfers between devices, exchange(): lax.all_to_all(value, 'i', 0, 0, axis_index_groups=groups, tiled=True)  10.3 us
    all_to_all x2, waiting for transfers between devices, exchange(): lax.all_to_all(value, 'i', 0, 0, axis_index_groups=groups, tiled=True)  9.35 us
    pallas_call x3, Pallas kernels, place(): kernel(functools.partial(place_kernel, arrays=len(arrays), chunks=chunks,...  2.94 us
    pallas_call x2, Pallas kernels, take(): kernel(body, [SMEM, HBM], [VMEM] * 2, [half] * 2, scratch_shapes=[pltpu.S...  2.83 us
  transfers between devices with their start and end apart: 25, of which 10 were waited for; matrix products, arithmetic and copies ran while one was open for 0% of the time, Pallas kernels for 6%

profile of v4, /device:TPU:9, one launch (start us, length us, event | category | flops | bytes accessed | tf_op | source)
XLA Modules:
  0.0 88.8 jit_solution(549267974463697398)
XLA Ops:
  0.6 1.5 %shard_map.93 = (bf16[4,8,24,512]{3,2,1,0:T(8,128)(2,1)S(1)}, bf16[4,8,24,512]{3,2,1,0:T(8,128)(2,1)S(1)}) custom-call(s32[1]{0:T(128)} %bitcast.me, bf16[128,24,512]{2,1,0:T(8,128)(2,1)} %bitcast.4), custom_call_target="tpu_custom_call" | custom-call | tf_op jit(solution)/shard_map/pallas_call | solution.py:300
  3.0 1.4 %shard_map.92 = (bf16[4,8,24,512]{3,2,1,0:T(8,128)(2,1)S(1)}, bf16[4,8,24,512]{3,2,1,0:T(8,128)(2,1)S(1)}) custom-call(s32[1]{0:T(128)} %bitcast.me, bf16[128,24,512]{2,1,0:T(8,128)(2,1)} %bitcast.5), custom_call_target="tpu_custom_call" | custom-call | tf_op jit(solution)/shard_map/pallas_call | solution.py:300
  4.9 1.4 %collective-permute-start.6 = (bf16[9,24,512]{2,1,0:T(8,128)(2,1)S(1)}, bf16[9,24,512]{2,1,0:T(8,128)(2,1)S(1)}, u32[]{:S(2)}, u32[]{:S(2)}) collective-permute-start(bf16[9,24,512]{2,1,0:T(8,128)(2,1)S(1)} %get-tuple-element.41), channel_id=1, source_target_pairs={{8,0},{0,8},{10,2},{2,10},{12,4},{4,12},{14,6},{6,14},{16,24},{24,... | collective-permute-start | bytes 663560 | tf_op jit(solution)/shard_map/ppermute | solution.py:293
  6.2 3.8 %collective-permute-start.7 = (bf16[9,24,512]{2,1,0:T(8,128)(2,1)S(1)}, bf16[9,24,512]{2,1,0:T(8,128)(2,1)S(1)}, u32[]{:S(2)}, u32[]{:S(2)}) collective-permute-start(bf16[9,24,512]{2,1,0:T(8,128)(2,1)S(1)} %get-tuple-element.42), channel_id=1, source_target_pairs={{2,0},{10,8},{4,2},{12,10},{6,4},{14,12},{0,6},{8,14},{26,24},{18,... | collective-permute-start | bytes 663560 | tf_op jit(solution)/shard_map/ppermute | solution.py:293
  10.1 1.3 %collective-permute-start.1 = (bf16[9,24,512]{2,1,0:T(8,128)(2,1)S(1)}, bf16[9,24,512]{2,1,0:T(8,128)(2,1)S(1)}, u32[]{:S(2)}, u32[]{:S(2)}) collective-permute-start(bf16[9,24,512]{2,1,0:T(8,128)(2,1)S(1)} %get-tuple-element.35), channel_id=1, source_target_pairs={{12,0},{4,8},{14,2},{6,10},{8,4},{0,12},{10,6},{2,14},{20,24},{28,... | collective-permute-start | bytes 663560 | tf_op jit(solution)/shard_map/ppermute | solution.py:293
  11.4 1.6 %collective-permute-start.2 = (bf16[9,24,512]{2,1,0:T(8,128)(2,1)S(1)}, bf16[9,24,512]{2,1,0:T(8,128)(2,1)S(1)}, u32[]{:S(2)}, u32[]{:S(2)}) collective-permute-start(bf16[9,24,512]{2,1,0:T(8,128)(2,1)S(1)} %get-tuple-element.36), channel_id=1, source_target_pairs={{10,0},{2,8},{12,2},{4,10},{14,4},{6,12},{8,6},{0,14},{18,24},{26,... | collective-permute-start | bytes 663560 | tf_op jit(solution)/shard_map/ppermute | solution.py:293
  13.0 1.3 %collective-permute-start.3 = (bf16[9,24,512]{2,1,0:T(8,128)(2,1)S(1)}, bf16[9,24,512]{2,1,0:T(8,128)(2,1)S(1)}, u32[]{:S(2)}, u32[]{:S(2)}) collective-permute-start(bf16[9,24,512]{2,1,0:T(8,128)(2,1)S(1)} %get-tuple-element.37), channel_id=1, source_target_pairs={{14,0},{6,8},{8,2},{0,10},{10,4},{2,12},{12,6},{4,14},{22,24},{30,... | collective-permute-start | bytes 663560 | tf_op jit(solution)/shard_map/ppermute | solution.py:293
  14.3 1.9 %collective-permute-start.4 = (bf16[9,24,512]{2,1,0:T(8,128)(2,1)S(1)}, bf16[9,24,512]{2,1,0:T(8,128)(2,1)S(1)}, u32[]{:S(2)}, u32[]{:S(2)}) collective-permute-start(bf16[9,24,512]{2,1,0:T(8,128)(2,1)S(1)} %get-tuple-element.38), channel_id=1, source_target_pairs={{4,0},{12,8},{6,2},{14,10},{0,4},{8,12},{2,6},{10,14},{28,24},{20,... | collective-permute-start | bytes 663560 | tf_op jit(solution)/shard_map/ppermute | solution.py:293
  16.2 7.2 %collective-permute-done.8.refs_6_ = bf16[9,24,512]{2,1,0:T(8,128)(2,1)S(1)} collective-permute-done((bf16[9,24,512]{2,1,0:T(8,128)(2,1)S(1)}, bf16[9,24,512]{2,1,0:T(8,128)(2,1)S(1)}, u32[]{:S(2)}, u32[]{:S(2)}) %collective-permute-start.8) | collective-permute-done | bytes 221216 | tf_op jit(solution)/shard_map/ppermute | solution.py:293
  23.4 0.9 shard_map.96
  24.3 6.4 %all-to-all-start = ((bf16[8,24,512]{2,1,0:T(8,128)(2,1)}), bf16[8,24,512]{2,1,0:T(8,128)(2,1)S(1)}, u32[]{:S(2)}, u32[]{:S(2)}) async-start(bf16[8,24,512]{2,1,0:T(8,128)(2,1)} %get-tuple-element.45), calls=%async_computation | async-start | bytes 393216 | tf_op jit(solution)/shard_map/all_to_all | solution.py:89
  31.3 4.3 %all-to-all-done.parts = bf16[8,24,512]{2,1,0:T(8,128)(2,1)S(1)} async-done(((bf16[8,24,512]{2,1,0:T(8,128)(2,1)}), bf16[8,24,512]{2,1,0:T(8,128)(2,1)S(1)}, u32[]{:S(2)}, u32[]{:S(2)}) %all-to-all-start) | async-done | bytes 196640 | tf_op jit(solution)/shard_map/all_to_all | solution.py:89
  36.5 3.9 %all-to-all-start.1 = ((bf16[8,32,512]{2,1,0:T(8,128)(2,1)}), bf16[8,32,512]{2,1,0:T(8,128)(2,1)S(1)}, u32[]{:S(2)}, u32[]{:S(2)}) async-start(bf16[8,32,512]{2,1,0:T(8,128)(2,1)} %shard_map.99), calls=%async_computation.1 | async-start | bytes 524288 | tf_op jit(solution)/shard_map/all_to_all | solution.py:89
  40.6 5.1 %all-to-all-done.1.got = bf16[8,32,512]{2,1,0:T(8,128)(2,1)S(1)} async-done(((bf16[8,32,512]{2,1,0:T(8,128)(2,1)}), bf16[8,32,512]{2,1,0:T(8,128)(2,1)S(1)}, u32[]{:S(2)}, u32[]{:S(2)}) %all-to-all-start.1) | async-done | bytes 262176 | tf_op jit(solution)/shard_map/all_to_all | solution.py:89
  45.8 2.7 %collective-permute-start.14 = (bf16[9,24,512]{2,1,0:T(8,128)(2,1)S(1)}, bf16[9,24,512]{2,1,0:T(8,128)(2,1)S(1)}, u32[]{:S(2)}, u32[]{:S(2)}) collective-permute-start(bf16[9,24,512]{2,1,0:T(8,128)(2,1)S(1)} %shard_map.100.refs_7_.refs_0_), channel_id=1, source_target_pairs={{2,0},{10,8},{4,2},{12,10},{6,4},{14,12},{0,6},{8,14},{26,24},{18,... | collective-permute-start | bytes 663560 | tf_op jit(solution)/shard_map/ppermute | solution.py:293
  48.5 1.6 %collective-permute-start.13 = (bf16[9,24,512]{2,1,0:T(8,128)(2,1)S(1)}, bf16[9,24,512]{2,1,0:T(8,128)(2,1)S(1)}, u32[]{:S(2)}, u32[]{:S(2)}) collective-permute-start(bf16[9,24,512]{2,1,0:T(8,128)(2,1)S(1)} %shard_map.100.refs_7_.refs_0_), channel_id=1, source_target_pairs={{8,0},{0,8},{10,2},{2,10},{12,4},{4,12},{14,6},{6,14},{16,24},{24,... | collective-permute-start | bytes 663560 | tf_op jit(solution)/shard_map/ppermute | solution.py:293
  52.2 2.5 %collective-permute-start.19 = (bf16[2,8,24,512]{3,2,1,0:T(8,128)(2,1)S(1)}, bf16[2,8,24,512]{3,2,1,0:T(8,128)(2,1)S(1)}, u32[]{:S(2)}, u32[]{:S(2)}) collective-permute-start(bf16[2,8,24,512]{3,2,1,0:T(8,128)(2,1)S(1)} %shard_map.103.refs_4_), channel_id=1, source_target_pairs={{64,0},{88,24},{1,64},{25,88},{65,1},{89,25},{0,65},{24,89},{72,8}... | collective-permute-start | bytes 1179656 | tf_op jit(solution)/shard_map/ppermute | solution.py:293
  54.7 1.3 %collective-permute-start.18 = (bf16[2,8,24,512]{3,2,1,0:T(8,128)(2,1)S(1)}, bf16[2,8,24,512]{3,2,1,0:T(8,128)(2,1)S(1)}, u32[]{:S(2)}, u32[]{:S(2)}) collective-permute-start(bf16[2,8,24,512]{3,2,1,0:T(8,128)(2,1)S(1)} %shard_map.103.refs_4_), channel_id=1, source_target_pairs={{1,0},{25,24},{65,64},{89,88},{0,1},{24,25},{64,65},{88,89},{9,8},... | collective-permute-start | bytes 1179656 | tf_op jit(solution)/shard_map/ppermute | solution.py:293
  56.0 3.3 %collective-permute-done.12.refs_3_.refs_0_ = bf16[9,24,512]{2,1,0:T(8,128)(2,1)S(1)} collective-permute-done((bf16[9,24,512]{2,1,0:T(8,128)(2,1)S(1)}, bf16[9,24,512]{2,1,0:T(8,128)(2,1)S(1)}, u32[]{:S(2)}, u32[]{:S(2)}) %collective-permute-start.12) | collective-permute-done | bytes 221216 | tf_op jit(solution)/shard_map/ppermute | solution.py:293
  59.3 1.0 %collective-permute-start.10 = (bf16[9,24,512]{2,1,0:T(8,128)(2,1)S(1)}, bf16[9,24,512]{2,1,0:T(8,128)(2,1)S(1)}, u32[]{:S(2)}, u32[]{:S(2)}) collective-permute-start(bf16[9,24,512]{2,1,0:T(8,128)(2,1)S(1)} %shard_map.100.refs_7_.refs_0_), channel_id=1, source_target_pairs={{10,0},{2,8},{12,2},{4,10},{14,4},{6,12},{8,6},{0,14},{18,24},{26,... | collective-permute-start | bytes 663560 | tf_op jit(solution)/shard_map/ppermute | solution.py:293
  60.3 5.0 %collective-permute-done.10.refs_1_.refs_2_ = bf16[9,24,512]{2,1,0:T(8,128)(2,1)S(1)} collective-permute-done((bf16[9,24,512]{2,1,0:T(8,128)(2,1)S(1)}, bf16[9,24,512]{2,1,0:T(8,128)(2,1)S(1)}, u32[]{:S(2)}, u32[]{:S(2)}) %collective-permute-start.10) | collective-permute-done | bytes 221216 | tf_op jit(solution)/shard_map/ppermute | solution.py:293
  65.3 2.3 %collective-permute-done.9.refs_0_.refs_1_ = bf16[9,24,512]{2,1,0:T(8,128)(2,1)S(1)} collective-permute-done((bf16[9,24,512]{2,1,0:T(8,128)(2,1)S(1)}, bf16[9,24,512]{2,1,0:T(8,128)(2,1)S(1)}, u32[]{:S(2)}, u32[]{:S(2)}) %collective-permute-start.9) | collective-permute-done | bytes 221216 | tf_op jit(solution)/shard_map/ppermute | solution.py:293
  67.6 15.3 %collective-permute-start.16 = (f32[8,128]{1,0:T(8,128)S(1)}, f32[8,128]{1,0:T(8,128)S(1)}, u32[]{:S(2)}, u32[]{:S(2)}) collective-permute-start(f32[8,128]{1,0:T(8,128)S(1)} %shard_map.101.total), channel_id=1, source_target_pairs={{0,32},{32,0},{64,96},{96,64},{1,33},{33,1},{65,97},{97,65},{8,40}... | collective-permute-start | bytes 12296 | tf_op jit(solution)/shard_map/ppermute | solution.py:293
  85.6 1.2 %shard_map.106 = (bf16[128,24,512]{2,1,0:T(8,128)(2,1)}, f32[24,512]{1,0:T(8,128)}, f32[24,512]{1,0:T(8,128)}, f32[24,512]{1,0:T(8,128)}, f32[24,512]{1,0:T(8,128)}) custom-call(s32[1]{0:T(128)} %bitcast.me, bf16[4,8,24,512]{3,2,1,0:T(8,128)(2,1)S(1)} %shard_map.104.refs_0_, bf16[4,8,24,512]{3,2,1,0:T(8,128)(2,1)S(1)} %shard_map.105.refs_1_, ...), custom_call_target="tpu_custom_call" | custom-call | tf_op jit(solution)/shard_map/pallas_call | solution.py:356
  (51 shorter events, 10.0 us)
Async XLA Ops:
  2.1 2.7 %collective-permute-start.5 = (bf16[4,8,24,512]{3,2,1,0:T(8,128)(2,1)S(1)}, bf16[4,8,24,512]{3,2,1,0:T(8,128)(2,1)S(1)}, u32[]{:S(2)}, u32[]{:S(2)}) collective-permute-start(bf16[4,8,24,512]{3,2,1,0:T(8,128)(2,1)S(1)} %get-tuple-element.40), channel_id=1, source_target_pairs={{0,32},{32,0},{64,96},{96,64},{1,33},{33,1},{65,97},{97,65},{8,40}... | collective-permute-start | bytes 2359304 | tf_op jit(solution)/shard_map/ppermute | solution.py:293
  2.9 7.1 %collective-permute-start = (bf16[4,8,24,512]{3,2,1,0:T(8,128)(2,1)S(1)}, bf16[4,8,24,512]{3,2,1,0:T(8,128)(2,1)S(1)}, u32[]{:S(2)}, u32[]{:S(2)}) collective-permute-start(bf16[4,8,24,512]{3,2,1,0:T(8,128)(2,1)S(1)} %get-tuple-element.34), channel_id=1, source_target_pairs={{0,32},{32,0},{64,96},{96,64},{1,33},{33,1},{65,97},{97,65},{8,40}... | collective-permute-start | bytes 2359304 | tf_op jit(solution)/shard_map/ppermute | solution.py:293
  4.9 8.1 %collective-permute-start.6 = (bf16[9,24,512]{2,1,0:T(8,128)(2,1)S(1)}, bf16[9,24,512]{2,1,0:T(8,128)(2,1)S(1)}, u32[]{:S(2)}, u32[]{:S(2)}) collective-permute-start(bf16[9,24,512]{2,1,0:T(8,128)(2,1)S(1)} %get-tuple-element.41), channel_id=1, source_target_pairs={{8,0},{0,8},{10,2},{2,10},{12,4},{4,12},{14,6},{6,14},{16,24},{24,... | collective-permute-start | bytes 663560 | tf_op jit(solution)/shard_map/ppermute | solution.py:293
  6.2 8.1 %collective-permute-start.7 = (bf16[9,24,512]{2,1,0:T(8,128)(2,1)S(1)}, bf16[9,24,512]{2,1,0:T(8,128)(2,1)S(1)}, u32[]{:S(2)}, u32[]{:S(2)}) collective-permute-start(bf16[9,24,512]{2,1,0:T(8,128)(2,1)S(1)} %get-tuple-element.42), channel_id=1, source_target_pairs={{2,0},{10,8},{4,2},{12,10},{6,4},{14,12},{0,6},{8,14},{26,24},{18,... | collective-permute-start | bytes 663560 | tf_op jit(solution)/shard_map/ppermute | solution.py:293
  10.0 13.4 %collective-permute-start.8 = (bf16[9,24,512]{2,1,0:T(8,128)(2,1)S(1)}, bf16[9,24,512]{2,1,0:T(8,128)(2,1)S(1)}, u32[]{:S(2)}, u32[]{:S(2)}) collective-permute-start(bf16[9,24,512]{2,1,0:T(8,128)(2,1)S(1)} %get-tuple-element.43), channel_id=1, source_target_pairs={{6,0},{14,8},{0,2},{8,10},{2,4},{10,12},{4,6},{12,14},{30,24},{22,... | collective-permute-start | bytes 663560 | tf_op jit(solution)/shard_map/ppermute | solution.py:293
  10.1 13.3 %collective-permute-start.1 = (bf16[9,24,512]{2,1,0:T(8,128)(2,1)S(1)}, bf16[9,24,512]{2,1,0:T(8,128)(2,1)S(1)}, u32[]{:S(2)}, u32[]{:S(2)}) collective-permute-start(bf16[9,24,512]{2,1,0:T(8,128)(2,1)S(1)} %get-tuple-element.35), channel_id=1, source_target_pairs={{12,0},{4,8},{14,2},{6,10},{8,4},{0,12},{10,6},{2,14},{20,24},{28,... | collective-permute-start | bytes 663560 | tf_op jit(solution)/shard_map/ppermute | solution.py:293
  11.4 12.0 %collective-permute-start.2 = (bf16[9,24,512]{2,1,0:T(8,128)(2,1)S(1)}, bf16[9,24,512]{2,1,0:T(8,128)(2,1)S(1)}, u32[]{:S(2)}, u32[]{:S(2)}) collective-permute-start(bf16[9,24,512]{2,1,0:T(8,128)(2,1)S(1)} %get-tuple-element.36), channel_id=1, source_target_pairs={{10,0},{2,8},{12,2},{4,10},{14,4},{6,12},{8,6},{0,14},{18,24},{26,... | collective-permute-start | bytes 663560 | tf_op jit(solution)/shard_map/ppermute | solution.py:293
  13.0 10.4 %collective-permute-start.3 = (bf16[9,24,512]{2,1,0:T(8,128)(2,1)S(1)}, bf16[9,24,512]{2,1,0:T(8,128)(2,1)S(1)}, u32[]{:S(2)}, u32[]{:S(2)}) collective-permute-start(bf16[9,24,512]{2,1,0:T(8,128)(2,1)S(1)} %get-tuple-element.37), channel_id=1, source_target_pairs={{14,0},{6,8},{8,2},{0,10},{10,4},{2,12},{12,6},{4,14},{22,24},{30,... | collective-permute-start | bytes 663560 | tf_op jit(solution)/shard_map/ppermute | solution.py:293
  14.3 9.1 %collective-permute-start.4 = (bf16[9,24,512]{2,1,0:T(8,128)(2,1)S(1)}, bf16[9,24,512]{2,1,0:T(8,128)(2,1)S(1)}, u32[]{:S(2)}, u32[]{:S(2)}) collective-permute-start(bf16[9,24,512]{2,1,0:T(8,128)(2,1)S(1)} %get-tuple-element.38), channel_id=1, source_target_pairs={{4,0},{12,8},{6,2},{14,10},{0,4},{8,12},{2,6},{10,14},{28,24},{20,... | collective-permute-start | bytes 663560 | tf_op jit(solution)/shard_map/ppermute | solution.py:293
  24.3 11.3 %all-to-all-start = ((bf16[8,24,512]{2,1,0:T(8,128)(2,1)}), bf16[8,24,512]{2,1,0:T(8,128)(2,1)S(1)}, u32[]{:S(2)}, u32[]{:S(2)}) async-start(bf16[8,24,512]{2,1,0:T(8,128)(2,1)} %get-tuple-element.45), calls=%async_computation | async-start | bytes 393216 | tf_op jit(solution)/shard_map/all_to_all | solution.py:89
  36.5 9.2 %all-to-all-start.1 = ((bf16[8,32,512]{2,1,0:T(8,128)(2,1)}), bf16[8,32,512]{2,1,0:T(8,128)(2,1)S(1)}, u32[]{:S(2)}, u32[]{:S(2)}) async-start(bf16[8,32,512]{2,1,0:T(8,128)(2,1)} %shard_map.99), calls=%async_computation.1 | async-start | bytes 524288 | tf_op jit(solution)/shard_map/all_to_all | solution.py:89
  40.4 10.4 %collective-permute-start.17 = (bf16[8,24,512]{2,1,0:T(8,128)(2,1)S(1)}, bf16[8,24,512]{2,1,0:T(8,128)(2,1)S(1)}, u32[]{:S(2)}, u32[]{:S(2)}) collective-permute-start(bf16[8,24,512]{2,1,0:T(8,128)(2,1)S(1)} %get-tuple-element.51.refs_0_), channel_id=1, source_target_pairs={{24,0},{0,24},{88,64},{64,88},{25,1},{1,25},{89,65},{65,89},{16,8}... | collective-permute-start | bytes 589832 | tf_op jit(solution)/shard_map/ppermute | solution.py:293
  45.8 6.3 %collective-permute-start.15 = (bf16[9,24,512]{2,1,0:T(8,128)(2,1)S(1)}, bf16[9,24,512]{2,1,0:T(8,128)(2,1)S(1)}, u32[]{:S(2)}, u32[]{:S(2)}) collective-permute-start(bf16[9,24,512]{2,1,0:T(8,128)(2,1)S(1)} %shard_map.100.refs_7_.refs_0_), channel_id=1, source_target_pairs={{6,0},{14,8},{0,2},{8,10},{2,4},{10,12},{4,6},{12,14},{30,24},{22,... | collective-permute-start | bytes 663560 | tf_op jit(solution)/shard_map/ppermute | solution.py:293
  45.8 6.4 %collective-permute-start.14 = (bf16[9,24,512]{2,1,0:T(8,128)(2,1)S(1)}, bf16[9,24,512]{2,1,0:T(8,128)(2,1)S(1)}, u32[]{:S(2)}, u32[]{:S(2)}) collective-permute-start(bf16[9,24,512]{2,1,0:T(8,128)(2,1)S(1)} %shard_map.100.refs_7_.refs_0_), channel_id=1, source_target_pairs={{2,0},{10,8},{4,2},{12,10},{6,4},{14,12},{0,6},{8,14},{26,24},{18,... | collective-permute-start | bytes 663560 | tf_op jit(solution)/shard_map/ppermute | solution.py:293
  48.5 6.2 %collective-permute-start.13 = (bf16[9,24,512]{2,1,0:T(8,128)(2,1)S(1)}, bf16[9,24,512]{2,1,0:T(8,128)(2,1)S(1)}, u32[]{:S(2)}, u32[]{:S(2)}) collective-permute-start(bf16[9,24,512]{2,1,0:T(8,128)(2,1)S(1)} %shard_map.100.refs_7_.refs_0_), channel_id=1, source_target_pairs={{8,0},{0,8},{10,2},{2,10},{12,4},{4,12},{14,6},{6,14},{16,24},{24,... | collective-permute-start | bytes 663560 | tf_op jit(solution)/shard_map/ppermute | solution.py:293
  50.1 9.2 %collective-permute-start.12 = (bf16[9,24,512]{2,1,0:T(8,128)(2,1)S(1)}, bf16[9,24,512]{2,1,0:T(8,128)(2,1)S(1)}, u32[]{:S(2)}, u32[]{:S(2)}) collective-permute-start(bf16[9,24,512]{2,1,0:T(8,128)(2,1)S(1)} %shard_map.100.refs_7_.refs_0_), channel_id=1, source_target_pairs={{4,0},{12,8},{6,2},{14,10},{0,4},{8,12},{2,6},{10,14},{28,24},{20,... | collective-permute-start | bytes 663560 | tf_op jit(solution)/shard_map/ppermute | solution.py:293
  50.9 9.4 %collective-permute-start.11 = (bf16[9,24,512]{2,1,0:T(8,128)(2,1)S(1)}, bf16[9,24,512]{2,1,0:T(8,128)(2,1)S(1)}, u32[]{:S(2)}, u32[]{:S(2)}) collective-permute-start(bf16[9,24,512]{2,1,0:T(8,128)(2,1)S(1)} %shard_map.100.refs_7_.refs_0_), channel_id=1, source_target_pairs={{14,0},{6,8},{8,2},{0,10},{10,4},{2,12},{12,6},{4,14},{22,24},{30,... | collective-permute-start | bytes 663560 | tf_op jit(solution)/shard_map/ppermute | solution.py:293
  52.0 31.9 %collective-permute-start.20 = (bf16[2,8,24,512]{3,2,1,0:T(8,128)(2,1)S(1)}, bf16[2,8,24,512]{3,2,1,0:T(8,128)(2,1)S(1)}, u32[]{:S(2)}, u32[]{:S(2)}) collective-permute-start(bf16[2,8,24,512]{3,2,1,0:T(8,128)(2,1)S(1)} %shard_map.103.refs_4_), channel_id=1, source_target_pairs={{65,0},{89,24},{0,64},{24,88},{64,1},{88,25},{1,65},{25,89},{73,8}... | collective-permute-start | bytes 1179656 | tf_op jit(solution)/shard_map/ppermute | solution.py:293
  52.2 31.8 %collective-permute-start.19 = (bf16[2,8,24,512]{3,2,1,0:T(8,128)(2,1)S(1)}, bf16[2,8,24,512]{3,2,1,0:T(8,128)(2,1)S(1)}, u32[]{:S(2)}, u32[]{:S(2)}) collective-permute-start(bf16[2,8,24,512]{3,2,1,0:T(8,128)(2,1)S(1)} %shard_map.103.refs_4_), channel_id=1, source_target_pairs={{64,0},{88,24},{1,64},{25,88},{65,1},{89,25},{0,65},{24,89},{72,8}... | collective-permute-start | bytes 1179656 | tf_op jit(solution)/shard_map/ppermute | solution.py:293
  54.7 29.3 %collective-permute-start.18 = (bf16[2,8,24,512]{3,2,1,0:T(8,128)(2,1)S(1)}, bf16[2,8,24,512]{3,2,1,0:T(8,128)(2,1)S(1)}, u32[]{:S(2)}, u32[]{:S(2)}) collective-permute-start(bf16[2,8,24,512]{3,2,1,0:T(8,128)(2,1)S(1)} %shard_map.103.refs_4_), channel_id=1, source_target_pairs={{1,0},{25,24},{65,64},{89,88},{0,1},{24,25},{64,65},{88,89},{9,8},... | collective-permute-start | bytes 1179656 | tf_op jit(solution)/shard_map/ppermute | solution.py:293
  59.3 6.0 %collective-permute-start.10 = (bf16[9,24,512]{2,1,0:T(8,128)(2,1)S(1)}, bf16[9,24,512]{2,1,0:T(8,128)(2,1)S(1)}, u32[]{:S(2)}, u32[]{:S(2)}) collective-permute-start(bf16[9,24,512]{2,1,0:T(8,128)(2,1)S(1)} %shard_map.100.refs_7_.refs_0_), channel_id=1, source_target_pairs={{10,0},{2,8},{12,2},{4,10},{14,4},{6,12},{8,6},{0,14},{18,24},{26,... | collective-permute-start | bytes 663560 | tf_op jit(solution)/shard_map/ppermute | solution.py:293
  60.3 7.3 %collective-permute-start.9 = (bf16[9,24,512]{2,1,0:T(8,128)(2,1)S(1)}, bf16[9,24,512]{2,1,0:T(8,128)(2,1)S(1)}, u32[]{:S(2)}, u32[]{:S(2)}) collective-permute-start(bf16[9,24,512]{2,1,0:T(8,128)(2,1)S(1)} %shard_map.100.refs_7_.refs_0_), channel_id=1, source_target_pairs={{12,0},{4,8},{14,2},{6,10},{8,4},{0,12},{10,6},{2,14},{20,24},{28,... | collective-permute-start | bytes 663560 | tf_op jit(solution)/shard_map/ppermute | solution.py:293
  67.6 16.1 %collective-permute-start.16 = (f32[8,128]{1,0:T(8,128)S(1)}, f32[8,128]{1,0:T(8,128)S(1)}, u32[]{:S(2)}, u32[]{:S(2)}) collective-permute-start(f32[8,128]{1,0:T(8,128)S(1)} %shard_map.101.total), channel_id=1, source_target_pairs={{0,32},{32,0},{64,96},{96,64},{1,33},{33,1},{65,97},{97,65},{8,40}... | collective-permute-start | bytes 12296 | tf_op jit(solution)/shard_map/ppermute | solution.py:293
  85.3 2.6 %collective-permute-start.21 = (bf16[4,8,24,512]{3,2,1,0:T(8,128)(2,1)S(1)}, bf16[4,8,24,512]{3,2,1,0:T(8,128)(2,1)S(1)}, u32[]{:S(2)}, u32[]{:S(2)}) collective-permute-start(bf16[4,8,24,512]{3,2,1,0:T(8,128)(2,1)S(1)} %shard_map.105.refs_1_), channel_id=1, source_target_pairs={{0,32},{32,0},{64,96},{96,64},{1,33},{33,1},{65,97},{97,65},{8,40}... | collective-permute-start | bytes 2359304 | tf_op jit(solution)/shard_map/ppermute | solution.py:293
  (5 other events, 95.4 us)

commit v5 on v4

--- a/solution.py
+++ b/solution.py
@@ -59,7 +59,7 @@
 OFFSETS = ((2, 1), (3, 1), (1, 1), (2, 0), (0, 1), (3, 0), (1, 0))
 OWN = (0, 0)
 HALVES = (OFFSETS[:4], OFFSETS[4:] + (OWN,))
-RINGS = (0, 2, 3, 1)
+RINGS = (0, 1, 3, 2)
 
 
 def source_place(a, offset):
@@ -325,14 +325,18 @@
     pay = kernel(pay_kernel, [VMEM] * 2, VMEM, of((GROUP, PAY, COLS), BF16))(update, sums)
     got = exchange(pay, NARROW)
     updates = kernel(open_kernel, [VMEM], VMEM, more)(got)
-    wide = [send(updates, shift(WIDE, offset)) for offset in OFFSETS]
+    beside = send(updates, shift(WIDE, (0, 1)))
+    wide = {OWN: updates, (0, 1): beside}
+    for pair, value in enumerate((updates, beside)):
+        for ring in RINGS[1:]:
+            wide[ring, pair] = send(value, shift(WIDE, (ring, 0)))
     total = kernel(
         core_total_kernel,
         [SMEM] + [VMEM] * GROUP,
         VMEM,
         pltpu.VMEM((8, 128), F32),
         scratch_shapes=[pltpu.VMEM((GROUP, 8, 128), F32)],
-    )(me, *wide, updates)
+    )(me, *(wide[offset] for offset in OFFSETS + (OWN,)))
     arrived = send(total, CORE_SWAP)
     trust, new_master, scaled_update = kernel(
         trust_kernel, [SMEM] + [VMEM] * 4, (VMEM,) * 3, (pltpu.VMEM((3, 8, 128), F32), own_f32, own_f32)
@@ -344,8 +348,8 @@
         return kernel(body, [SMEM] + [VMEM] * (5 + len(values)), VMEM, shape)(me, trust, *values, *held)
 
     first, last = (OWN,) + OFFSETS[:3], OFFSETS[3:]
-    params_0 = params_of(first, (updates, *wide[:3]))
-    params_1 = params_of(last, wide[3:])
+    params_0 = params_of(first, [wide[offset] for offset in first])
+    params_1 = params_of(last, [wide[offset] for offset in last])
     other_0 = send(params_0, CORE_SWAP)
     other_1 = send(params_1, CORE_SWAP)
     every = of((2 * CHIPS, ROWS, COLS), BF16)

time: 89.3 us -> 87.7 us (0.982)
  the two profiles are of different devices: /device:TPU:9 before, /device:TPU:1 now
where the time goes in v5:
time: 87.7 us; the launch traced here: 87.3 us
  starting transfers between devices  45.9 us (52%)
  waiting for transfers between devices  23.5 us (27%)
  Pallas kernels  8.84 us (10%)
  blocking collectives  8.3 us (9%)
    ppermute x23, starting transfers between devices, send(): return lax.ppermute(value, 'i', pairs)  41.9 us
    ppermute x23, waiting for transfers between devices, send(): return lax.ppermute(value, 'i', pairs)  18.6 us
    all_to_all x1, blocking collectives, exchange(): lax.all_to_all(value, 'i', 0, 0, axis_index_groups=groups, tiled=True)  8.3 us
    all_to_all x1, waiting for transfers between devices, exchange(): lax.all_to_all(value, 'i', 0, 0, axis_index_groups=groups, tiled=True)  4.88 us
    all_to_all x1, starting transfers between devices, exchange(): lax.all_to_all(value, 'i', 0, 0, axis_index_groups=groups, tiled=True)  4.02 us
    pallas_call x3, Pallas kernels, place(): kernel(functools.partial(place_kernel, arrays=len(arrays), chunks=chunks,...  2.94 us
    pallas_call x2, Pallas kernels, take(): kernel(body, [SMEM, HBM], [VMEM] * 2, [half] * 2, scratch_shapes=[pltpu.S...  2.83 us
  transfers between devices with their start and end apart: 24, of which 13 were waited for; matrix products, arithmetic and copies ran while one was open for 0% of the time, Pallas kernels for 6%

profile of v5, /device:TPU:1, one launch (start us, length us, event | category | flops | bytes accessed | tf_op | source)
XLA Modules:
  0.0 87.3 jit_solution(7766237082399927179)
XLA Ops:
  0.6 1.5 %shard_map.93 = (bf16[4,8,24,512]{3,2,1,0:T(8,128)(2,1)S(1)}, bf16[4,8,24,512]{3,2,1,0:T(8,128)(2,1)S(1)}) custom-call(s32[1]{0:T(128)} %bitcast.me, bf16[128,24,512]{2,1,0:T(8,128)(2,1)} %bitcast.4), custom_call_target="tpu_custom_call" | custom-call | tf_op jit(solution)/shard_map/pallas_call | solution.py:300
  2.1 1.5 %collective-permute-start.5 = (bf16[4,8,24,512]{3,2,1,0:T(8,128)(2,1)S(1)}, bf16[4,8,24,512]{3,2,1,0:T(8,128)(2,1)S(1)}, u32[]{:S(2)}, u32[]{:S(2)}) collective-permute-start(bf16[4,8,24,512]{3,2,1,0:T(8,128)(2,1)S(1)} %get-tuple-element.40), channel_id=1, source_target_pairs={{0,32},{32,0},{64,96},{96,64},{1,33},{33,1},{65,97},{97,65},{8,40}... | collective-permute-start | bytes 2359304 | tf_op jit(solution)/shard_map/ppermute | solution.py:293
  3.7 1.4 %shard_map.92 = (bf16[4,8,24,512]{3,2,1,0:T(8,128)(2,1)S(1)}, bf16[4,8,24,512]{3,2,1,0:T(8,128)(2,1)S(1)}) custom-call(s32[1]{0:T(128)} %bitcast.me, bf16[128,24,512]{2,1,0:T(8,128)(2,1)} %bitcast.5), custom_call_target="tpu_custom_call" | custom-call | tf_op jit(solution)/shard_map/pallas_call | solution.py:300
  5.6 2.9 %collective-permute-start.6 = (bf16[9,24,512]{2,1,0:T(8,128)(2,1)S(1)}, bf16[9,24,512]{2,1,0:T(8,128)(2,1)S(1)}, u32[]{:S(2)}, u32[]{:S(2)}) collective-permute-start(bf16[9,24,512]{2,1,0:T(8,128)(2,1)S(1)} %get-tuple-element.41), channel_id=1, source_target_pairs={{8,0},{0,8},{10,2},{2,10},{12,4},{4,12},{14,6},{6,14},{16,24},{24,... | collective-permute-start | bytes 663560 | tf_op jit(solution)/shard_map/ppermute | solution.py:293
  8.5 3.8 %collective-permute-start.7 = (bf16[9,24,512]{2,1,0:T(8,128)(2,1)S(1)}, bf16[9,24,512]{2,1,0:T(8,128)(2,1)S(1)}, u32[]{:S(2)}, u32[]{:S(2)}) collective-permute-start(bf16[9,24,512]{2,1,0:T(8,128)(2,1)S(1)} %get-tuple-element.42), channel_id=1, source_target_pairs={{2,0},{10,8},{4,2},{12,10},{6,4},{14,12},{0,6},{8,14},{26,24},{18,... | collective-permute-start | bytes 663560 | tf_op jit(solution)/shard_map/ppermute | solution.py:293
  12.4 1.2 %collective-permute-start.1 = (bf16[9,24,512]{2,1,0:T(8,128)(2,1)S(1)}, bf16[9,24,512]{2,1,0:T(8,128)(2,1)S(1)}, u32[]{:S(2)}, u32[]{:S(2)}) collective-permute-start(bf16[9,24,512]{2,1,0:T(8,128)(2,1)S(1)} %get-tuple-element.35), channel_id=1, source_target_pairs={{12,0},{4,8},{14,2},{6,10},{8,4},{0,12},{10,6},{2,14},{20,24},{28,... | collective-permute-start | bytes 663560 | tf_op jit(solution)/shard_map/ppermute | solution.py:293
  13.5 2.9 %collective-permute-start.2 = (bf16[9,24,512]{2,1,0:T(8,128)(2,1)S(1)}, bf16[9,24,512]{2,1,0:T(8,128)(2,1)S(1)}, u32[]{:S(2)}, u32[]{:S(2)}) collective-permute-start(bf16[9,24,512]{2,1,0:T(8,128)(2,1)S(1)} %get-tuple-element.36), channel_id=1, source_target_pairs={{10,0},{2,8},{12,2},{4,10},{14,4},{6,12},{8,6},{0,14},{18,24},{26,... | collective-permute-start | bytes 663560 | tf_op jit(solution)/shard_map/ppermute | solution.py:293
  16.5 1.3 %collective-permute-start.3 = (bf16[9,24,512]{2,1,0:T(8,128)(2,1)S(1)}, bf16[9,24,512]{2,1,0:T(8,128)(2,1)S(1)}, u32[]{:S(2)}, u32[]{:S(2)}) collective-permute-start(bf16[9,24,512]{2,1,0:T(8,128)(2,1)S(1)} %get-tuple-element.37), channel_id=1, source_target_pairs={{14,0},{6,8},{8,2},{0,10},{10,4},{2,12},{12,6},{4,14},{22,24},{30,... | collective-permute-start | bytes 663560 | tf_op jit(solution)/shard_map/ppermute | solution.py:293
  17.8 1.9 %collective-permute-start.4 = (bf16[9,24,512]{2,1,0:T(8,128)(2,1)S(1)}, bf16[9,24,512]{2,1,0:T(8,128)(2,1)S(1)}, u32[]{:S(2)}, u32[]{:S(2)}) collective-permute-start(bf16[9,24,512]{2,1,0:T(8,128)(2,1)S(1)} %get-tuple-element.38), channel_id=1, source_target_pairs={{4,0},{12,8},{6,2},{14,10},{0,4},{8,12},{2,6},{10,14},{28,24},{20,... | collective-permute-start | bytes 663560 | tf_op jit(solution)/shard_map/ppermute | solution.py:293
  19.7 1.2 %collective-permute-done.1.refs_0_ = bf16[9,24,512]{2,1,0:T(8,128)(2,1)S(1)} collective-permute-done((bf16[9,24,512]{2,1,0:T(8,128)(2,1)S(1)}, bf16[9,24,512]{2,1,0:T(8,128)(2,1)S(1)}, u32[]{:S(2)}, u32[]{:S(2)}) %collective-permute-start.1) | collective-permute-done | bytes 221216 | tf_op jit(solution)/shard_map/ppermute | solution.py:293
  20.8 3.6 %collective-permute-done.2.refs_1_ = bf16[9,24,512]{2,1,0:T(8,128)(2,1)S(1)} collective-permute-done((bf16[9,24,512]{2,1,0:T(8,128)(2,1)S(1)}, bf16[9,24,512]{2,1,0:T(8,128)(2,1)S(1)}, u32[]{:S(2)}, u32[]{:S(2)}) %collective-permute-start.2) | collective-permute-done | bytes 221216 | tf_op jit(solution)/shard_map/ppermute | solution.py:293
  24.4 1.3 %collective-permute-done.3.refs_2_ = bf16[9,24,512]{2,1,0:T(8,128)(2,1)S(1)} collective-permute-done((bf16[9,24,512]{2,1,0:T(8,128)(2,1)S(1)}, bf16[9,24,512]{2,1,0:T(8,128)(2,1)S(1)}, u32[]{:S(2)}, u32[]{:S(2)}) %collective-permute-start.3) | collective-permute-done | bytes 221216 | tf_op jit(solution)/shard_map/ppermute | solution.py:293
  27.3 4.0 %all-to-all-start = ((bf16[8,24,512]{2,1,0:T(8,128)(2,1)}), bf16[8,24,512]{2,1,0:T(8,128)(2,1)S(1)}, u32[]{:S(2)}, u32[]{:S(2)}) async-start(bf16[8,24,512]{2,1,0:T(8,128)(2,1)} %get-tuple-element.45), calls=%async_computation | async-start | bytes 393216 | tf_op jit(solution)/shard_map/all_to_all | solution.py:89
  32.0 4.9 %all-to-all-done.parts = bf16[8,24,512]{2,1,0:T(8,128)(2,1)S(1)} async-done(((bf16[8,24,512]{2,1,0:T(8,128)(2,1)}), bf16[8,24,512]{2,1,0:T(8,128)(2,1)S(1)}, u32[]{:S(2)}, u32[]{:S(2)}) %all-to-all-start) | async-done | bytes 196640 | tf_op jit(solution)/shard_map/all_to_all | solution.py:89
  37.1 8.3 %all_to_all.10.got = bf16[8,32,512]{2,1,0:T(8,128)(2,1)S(1)} all-to-all(bf16[8,32,512]{2,1,0:T(8,128)(2,1)S(1)} %shard_map.99), channel_id=1, replica_groups={{0,24,64,88,1,25,65,89},{8,16,72,80,9,17,73,81},{2,26,66,90,3,27,67,91}..., dimensions={0} | all-to-all | bytes 524288 | tf_op jit(solution)/shard_map/all_to_all | solution.py:89
  45.4 2.3 %collective-permute-start.9 = (bf16[9,24,512]{2,1,0:T(8,128)(2,1)S(1)}, bf16[9,24,512]{2,1,0:T(8,128)(2,1)S(1)}, u32[]{:S(2)}, u32[]{:S(2)}) collective-permute-start(bf16[9,24,512]{2,1,0:T(8,128)(2,1)S(1)} %shard_map.100.refs_7_.refs_0_), channel_id=1, source_target_pairs={{8,0},{0,8},{10,2},{2,10},{12,4},{4,12},{14,6},{6,14},{16,24},{24,... | collective-permute-start | bytes 663560 | tf_op jit(solution)/shard_map/ppermute | solution.py:293
  47.7 2.7 %collective-permute-start.14 = (bf16[9,24,512]{2,1,0:T(8,128)(2,1)S(1)}, bf16[9,24,512]{2,1,0:T(8,128)(2,1)S(1)}, u32[]{:S(2)}, u32[]{:S(2)}) collective-permute-start(bf16[9,24,512]{2,1,0:T(8,128)(2,1)S(1)} %shard_map.100.refs_7_.refs_0_), channel_id=1, source_target_pairs={{2,0},{10,8},{4,2},{12,10},{6,4},{14,12},{0,6},{8,14},{26,24},{18,... | collective-permute-start | bytes 663560 | tf_op jit(solution)/shard_map/ppermute | solution.py:293
  51.4 1.6 %collective-permute-done.9.refs_4_.refs_1_ = bf16[9,24,512]{2,1,0:T(8,128)(2,1)S(1)} collective-permute-done((bf16[9,24,512]{2,1,0:T(8,128)(2,1)S(1)}, bf16[9,24,512]{2,1,0:T(8,128)(2,1)S(1)}, u32[]{:S(2)}, u32[]{:S(2)}) %collective-permute-start.9) | collective-permute-done | bytes 221216 | tf_op jit(solution)/shard_map/ppermute | solution.py:293
  53.0 2.0 %collective-permute-done.17.refs_1_ = bf16[8,24,512]{2,1,0:T(8,128)(2,1)S(1)} collective-permute-done((bf16[8,24,512]{2,1,0:T(8,128)(2,1)S(1)}, bf16[8,24,512]{2,1,0:T(8,128)(2,1)S(1)}, u32[]{:S(2)}, u32[]{:S(2)}) %collective-permute-start.17) | collective-permute-done | bytes 196640 | tf_op jit(solution)/shard_map/ppermute | solution.py:293
  55.0 1.4 %collective-permute-start.20 = (bf16[2,8,24,512]{3,2,1,0:T(8,128)(2,1)S(1)}, bf16[2,8,24,512]{3,2,1,0:T(8,128)(2,1)S(1)}, u32[]{:S(2)}, u32[]{:S(2)}) collective-permute-start(bf16[2,8,24,512]{3,2,1,0:T(8,128)(2,1)S(1)} %shard_map.103.refs_4_), channel_id=1, source_target_pairs={{1,0},{25,24},{65,64},{89,88},{0,1},{24,25},{64,65},{88,89},{9,8},... | collective-permute-start | bytes 1179656 | tf_op jit(solution)/shard_map/ppermute | solution.py:293
  60.4 2.5 %collective-permute-done.11.refs_1_.refs_2_ = bf16[9,24,512]{2,1,0:T(8,128)(2,1)S(1)} collective-permute-done((bf16[9,24,512]{2,1,0:T(8,128)(2,1)S(1)}, bf16[9,24,512]{2,1,0:T(8,128)(2,1)S(1)}, u32[]{:S(2)}, u32[]{:S(2)}) %collective-permute-start.11) | collective-permute-done | bytes 221216 | tf_op jit(solution)/shard_map/ppermute | solution.py:293
  62.9 3.4 %collective-permute-done.10.refs_0_.refs_1_ = bf16[9,24,512]{2,1,0:T(8,128)(2,1)S(1)} collective-permute-done((bf16[9,24,512]{2,1,0:T(8,128)(2,1)S(1)}, bf16[9,24,512]{2,1,0:T(8,128)(2,1)S(1)}, u32[]{:S(2)}, u32[]{:S(2)}) %collective-permute-start.10) | collective-permute-done | bytes 221216 | tf_op jit(solution)/shard_map/ppermute | solution.py:293
  66.3 15.1 %collective-permute-start.16 = (f32[8,128]{1,0:T(8,128)S(1)}, f32[8,128]{1,0:T(8,128)S(1)}, u32[]{:S(2)}, u32[]{:S(2)}) collective-permute-start(f32[8,128]{1,0:T(8,128)S(1)} %shard_map.101.total), channel_id=1, source_target_pairs={{0,32},{32,0},{64,96},{96,64},{1,33},{33,1},{65,97},{97,65},{8,40}... | collective-permute-start | bytes 12296 | tf_op jit(solution)/shard_map/ppermute | solution.py:293
  84.0 1.2 %shard_map.106 = (bf16[128,24,512]{2,1,0:T(8,128)(2,1)}, f32[24,512]{1,0:T(8,128)}, f32[24,512]{1,0:T(8,128)}, f32[24,512]{1,0:T(8,128)}, f32[24,512]{1,0:T(8,128)}) custom-call(s32[1]{0:T(128)} %bitcast.me, bf16[4,8,24,512]{3,2,1,0:T(8,128)(2,1)S(1)} %shard_map.104.refs_0_, bf16[4,8,24,512]{3,2,1,0:T(8,128)(2,1)S(1)} %shard_map.105.refs_1_, ...), custom_call_target="tpu_custom_call" | custom-call | tf_op jit(solution)/shard_map/pallas_call | solution.py:360
  (50 shorter events, 12.9 us)
Async XLA Ops:
  2.1 3.4 %collective-permute-start.5 = (bf16[4,8,24,512]{3,2,1,0:T(8,128)(2,1)S(1)}, bf16[4,8,24,512]{3,2,1,0:T(8,128)(2,1)S(1)}, u32[]{:S(2)}, u32[]{:S(2)}) collective-permute-start(bf16[4,8,24,512]{3,2,1,0:T(8,128)(2,1)S(1)} %get-tuple-element.40), channel_id=1, source_target_pairs={{0,32},{32,0},{64,96},{96,64},{1,33},{33,1},{65,97},{97,65},{8,40}... | collective-permute-start | bytes 2359304 | tf_op jit(solution)/shard_map/ppermute | solution.py:293
  3.6 8.7 %collective-permute-start = (bf16[4,8,24,512]{3,2,1,0:T(8,128)(2,1)S(1)}, bf16[4,8,24,512]{3,2,1,0:T(8,128)(2,1)S(1)}, u32[]{:S(2)}, u32[]{:S(2)}) collective-permute-start(bf16[4,8,24,512]{3,2,1,0:T(8,128)(2,1)S(1)} %get-tuple-element.34), channel_id=1, source_target_pairs={{0,32},{32,0},{64,96},{96,64},{1,33},{33,1},{65,97},{97,65},{8,40}... | collective-permute-start | bytes 2359304 | tf_op jit(solution)/shard_map/ppermute | solution.py:293
  5.6 10.9 %collective-permute-start.6 = (bf16[9,24,512]{2,1,0:T(8,128)(2,1)S(1)}, bf16[9,24,512]{2,1,0:T(8,128)(2,1)S(1)}, u32[]{:S(2)}, u32[]{:S(2)}) collective-permute-start(bf16[9,24,512]{2,1,0:T(8,128)(2,1)S(1)} %get-tuple-element.41), channel_id=1, source_target_pairs={{8,0},{0,8},{10,2},{2,10},{12,4},{4,12},{14,6},{6,14},{16,24},{24,... | collective-permute-start | bytes 663560 | tf_op jit(solution)/shard_map/ppermute | solution.py:293
  8.5 9.3 %collective-permute-start.7 = (bf16[9,24,512]{2,1,0:T(8,128)(2,1)S(1)}, bf16[9,24,512]{2,1,0:T(8,128)(2,1)S(1)}, u32[]{:S(2)}, u32[]{:S(2)}) collective-permute-start(bf16[9,24,512]{2,1,0:T(8,128)(2,1)S(1)} %get-tuple-element.42), channel_id=1, source_target_pairs={{2,0},{10,8},{4,2},{12,10},{6,4},{14,12},{0,6},{8,14},{26,24},{18,... | collective-permute-start | bytes 663560 | tf_op jit(solution)/shard_map/ppermute | solution.py:293
  12.3 7.4 %collective-permute-start.8 = (bf16[9,24,512]{2,1,0:T(8,128)(2,1)S(1)}, bf16[9,24,512]{2,1,0:T(8,128)(2,1)S(1)}, u32[]{:S(2)}, u32[]{:S(2)}) collective-permute-start(bf16[9,24,512]{2,1,0:T(8,128)(2,1)S(1)} %get-tuple-element.43), channel_id=1, source_target_pairs={{6,0},{14,8},{0,2},{8,10},{2,4},{10,12},{4,6},{12,14},{30,24},{22,... | collective-permute-start | bytes 663560 | tf_op jit(solution)/shard_map/ppermute | solution.py:293
  12.4 8.5 %collective-permute-start.1 = (bf16[9,24,512]{2,1,0:T(8,128)(2,1)S(1)}, bf16[9,24,512]{2,1,0:T(8,128)(2,1)S(1)}, u32[]{:S(2)}, u32[]{:S(2)}) collective-permute-start(bf16[9,24,512]{2,1,0:T(8,128)(2,1)S(1)} %get-tuple-element.35), channel_id=1, source_target_pairs={{12,0},{4,8},{14,2},{6,10},{8,4},{0,12},{10,6},{2,14},{20,24},{28,... | collective-permute-start | bytes 663560 | tf_op jit(solution)/shard_map/ppermute | solution.py:293
  13.5 10.9 %collective-permute-start.2 = (bf16[9,24,512]{2,1,0:T(8,128)(2,1)S(1)}, bf16[9,24,512]{2,1,0:T(8,128)(2,1)S(1)}, u32[]{:S(2)}, u32[]{:S(2)}) collective-permute-start(bf16[9,24,512]{2,1,0:T(8,128)(2,1)S(1)} %get-tuple-element.36), channel_id=1, source_target_pairs={{10,0},{2,8},{12,2},{4,10},{14,4},{6,12},{8,6},{0,14},{18,24},{26,... | collective-permute-start | bytes 663560 | tf_op jit(solution)/shard_map/ppermute | solution.py:293
  16.5 9.2 %collective-permute-start.3 = (bf16[9,24,512]{2,1,0:T(8,128)(2,1)S(1)}, bf16[9,24,512]{2,1,0:T(8,128)(2,1)S(1)}, u32[]{:S(2)}, u32[]{:S(2)}) collective-permute-start(bf16[9,24,512]{2,1,0:T(8,128)(2,1)S(1)} %get-tuple-element.37), channel_id=1, source_target_pairs={{14,0},{6,8},{8,2},{0,10},{10,4},{2,12},{12,6},{4,14},{22,24},{30,... | collective-permute-start | bytes 663560 | tf_op jit(solution)/shard_map/ppermute | solution.py:293
  17.8 8.7 %collective-permute-start.4 = (bf16[9,24,512]{2,1,0:T(8,128)(2,1)S(1)}, bf16[9,24,512]{2,1,0:T(8,128)(2,1)S(1)}, u32[]{:S(2)}, u32[]{:S(2)}) collective-permute-start(bf16[9,24,512]{2,1,0:T(8,128)(2,1)S(1)} %get-tuple-element.38), channel_id=1, source_target_pairs={{4,0},{12,8},{6,2},{14,10},{0,4},{8,12},{2,6},{10,14},{28,24},{20,... | collective-permute-start | bytes 663560 | tf_op jit(solution)/shard_map/ppermute | solution.py:293
  27.3 9.5 %all-to-all-start = ((bf16[8,24,512]{2,1,0:T(8,128)(2,1)}), bf16[8,24,512]{2,1,0:T(8,128)(2,1)S(1)}, u32[]{:S(2)}, u32[]{:S(2)}) async-start(bf16[8,24,512]{2,1,0:T(8,128)(2,1)} %get-tuple-element.45), calls=%async_computation | async-start | bytes 393216 | tf_op jit(solution)/shard_map/all_to_all | solution.py:89
  45.4 7.5 %collective-permute-start.9 = (bf16[9,24,512]{2,1,0:T(8,128)(2,1)S(1)}, bf16[9,24,512]{2,1,0:T(8,128)(2,1)S(1)}, u32[]{:S(2)}, u32[]{:S(2)}) collective-permute-start(bf16[9,24,512]{2,1,0:T(8,128)(2,1)S(1)} %shard_map.100.refs_7_.refs_0_), channel_id=1, source_target_pairs={{8,0},{0,8},{10,2},{2,10},{12,4},{4,12},{14,6},{6,14},{16,24},{24,... | collective-permute-start | bytes 663560 | tf_op jit(solution)/shard_map/ppermute | solution.py:293
  47.7 8.6 %collective-permute-start.15 = (bf16[9,24,512]{2,1,0:T(8,128)(2,1)S(1)}, bf16[9,24,512]{2,1,0:T(8,128)(2,1)S(1)}, u32[]{:S(2)}, u32[]{:S(2)}) collective-permute-start(bf16[9,24,512]{2,1,0:T(8,128)(2,1)S(1)} %shard_map.100.refs_7_.refs_0_), channel_id=1, source_target_pairs={{6,0},{14,8},{0,2},{8,10},{2,4},{10,12},{4,6},{12,14},{30,24},{22,... | collective-permute-start | bytes 663560 | tf_op jit(solution)/shard_map/ppermute | solution.py:293
  47.7 9.7 %collective-permute-start.14 = (bf16[9,24,512]{2,1,0:T(8,128)(2,1)S(1)}, bf16[9,24,512]{2,1,0:T(8,128)(2,1)S(1)}, u32[]{:S(2)}, u32[]{:S(2)}) collective-permute-start(bf16[9,24,512]{2,1,0:T(8,128)(2,1)S(1)} %shard_map.100.refs_7_.refs_0_), channel_id=1, source_target_pairs={{2,0},{10,8},{4,2},{12,10},{6,4},{14,12},{0,6},{8,14},{26,24},{18,... | collective-permute-start | bytes 663560 | tf_op jit(solution)/shard_map/ppermute | solution.py:293
  50.4 4.5 %collective-permute-start.17 = (bf16[8,24,512]{2,1,0:T(8,128)(2,1)S(1)}, bf16[8,24,512]{2,1,0:T(8,128)(2,1)S(1)}, u32[]{:S(2)}, u32[]{:S(2)}) collective-permute-start(bf16[8,24,512]{2,1,0:T(8,128)(2,1)S(1)} %get-tuple-element.51.refs_0_), channel_id=1, source_target_pairs={{24,0},{0,24},{88,64},{64,88},{25,1},{1,25},{89,65},{65,89},{16,8}... | collective-permute-start | bytes 589832 | tf_op jit(solution)/shard_map/ppermute | solution.py:293
  50.7 7.1 %collective-permute-start.13 = (bf16[9,24,512]{2,1,0:T(8,128)(2,1)S(1)}, bf16[9,24,512]{2,1,0:T(8,128)(2,1)S(1)}, u32[]{:S(2)}, u32[]{:S(2)}) collective-permute-start(bf16[9,24,512]{2,1,0:T(8,128)(2,1)S(1)} %shard_map.100.refs_7_.refs_0_), channel_id=1, source_target_pairs={{4,0},{12,8},{6,2},{14,10},{0,4},{8,12},{2,6},{10,14},{28,24},{20,... | collective-permute-start | bytes 663560 | tf_op jit(solution)/shard_map/ppermute | solution.py:293
  52.9 6.7 %collective-permute-start.12 = (bf16[9,24,512]{2,1,0:T(8,128)(2,1)S(1)}, bf16[9,24,512]{2,1,0:T(8,128)(2,1)S(1)}, u32[]{:S(2)}, u32[]{:S(2)}) collective-permute-start(bf16[9,24,512]{2,1,0:T(8,128)(2,1)S(1)} %collective-permute-done.9.refs_4_.refs_1_), channel_id=1, source_target_pairs={{6,0},{14,8},{0,2},{8,10},{2,4},{10,12},{4,6},{12,14},{30,24},{22,... | collective-permute-start | bytes 663560 | tf_op jit(solution)/shard_map/ppermute | solution.py:293
  55.0 27.5 %collective-permute-start.20 = (bf16[2,8,24,512]{3,2,1,0:T(8,128)(2,1)S(1)}, bf16[2,8,24,512]{3,2,1,0:T(8,128)(2,1)S(1)}, u32[]{:S(2)}, u32[]{:S(2)}) collective-permute-start(bf16[2,8,24,512]{3,2,1,0:T(8,128)(2,1)S(1)} %shard_map.103.refs_4_), channel_id=1, source_target_pairs={{1,0},{25,24},{65,64},{89,88},{0,1},{24,25},{64,65},{88,89},{9,8},... | collective-permute-start | bytes 1179656 | tf_op jit(solution)/shard_map/ppermute | solution.py:293
  56.3 26.1 %collective-permute-start.19 = (bf16[2,8,24,512]{3,2,1,0:T(8,128)(2,1)S(1)}, bf16[2,8,24,512]{3,2,1,0:T(8,128)(2,1)S(1)}, u32[]{:S(2)}, u32[]{:S(2)}) collective-permute-start(bf16[2,8,24,512]{3,2,1,0:T(8,128)(2,1)S(1)} %shard_map.103.refs_4_), channel_id=1, source_target_pairs={{64,0},{88,24},{1,64},{25,88},{65,1},{89,25},{0,65},{24,89},{72,8}... | collective-permute-start | bytes 1179656 | tf_op jit(solution)/shard_map/ppermute | solution.py:293
  57.5 25.0 %collective-permute-start.18 = (bf16[2,8,24,512]{3,2,1,0:T(8,128)(2,1)S(1)}, bf16[2,8,24,512]{3,2,1,0:T(8,128)(2,1)S(1)}, u32[]{:S(2)}, u32[]{:S(2)}) collective-permute-start(bf16[2,8,24,512]{3,2,1,0:T(8,128)(2,1)S(1)} %shard_map.103.refs_4_), channel_id=1, source_target_pairs={{65,0},{89,24},{0,64},{24,88},{64,1},{88,25},{1,65},{25,89},{73,8}... | collective-permute-start | bytes 1179656 | tf_op jit(solution)/shard_map/ppermute | solution.py:293
  57.8 5.1 %collective-permute-start.11 = (bf16[9,24,512]{2,1,0:T(8,128)(2,1)S(1)}, bf16[9,24,512]{2,1,0:T(8,128)(2,1)S(1)}, u32[]{:S(2)}, u32[]{:S(2)}) collective-permute-start(bf16[9,24,512]{2,1,0:T(8,128)(2,1)S(1)} %collective-permute-done.9.refs_4_.refs_1_), channel_id=1, source_target_pairs={{2,0},{10,8},{4,2},{12,10},{6,4},{14,12},{0,6},{8,14},{26,24},{18,... | collective-permute-start | bytes 663560 | tf_op jit(solution)/shard_map/ppermute | solution.py:293
  59.7 6.6 %collective-permute-start.10 = (bf16[9,24,512]{2,1,0:T(8,128)(2,1)S(1)}, bf16[9,24,512]{2,1,0:T(8,128)(2,1)S(1)}, u32[]{:S(2)}, u32[]{:S(2)}) collective-permute-start(bf16[9,24,512]{2,1,0:T(8,128)(2,1)S(1)} %collective-permute-done.9.refs_4_.refs_1_), channel_id=1, source_target_pairs={{4,0},{12,8},{6,2},{14,10},{0,4},{8,12},{2,6},{10,14},{28,24},{20,... | collective-permute-start | bytes 663560 | tf_op jit(solution)/shard_map/ppermute | solution.py:293
  66.3 15.9 %collective-permute-start.16 = (f32[8,128]{1,0:T(8,128)S(1)}, f32[8,128]{1,0:T(8,128)S(1)}, u32[]{:S(2)}, u32[]{:S(2)}) collective-permute-start(f32[8,128]{1,0:T(8,128)S(1)} %shard_map.101.total), channel_id=1, source_target_pairs={{0,32},{32,0},{64,96},{96,64},{1,33},{33,1},{65,97},{97,65},{8,40}... | collective-permute-start | bytes 12296 | tf_op jit(solution)/shard_map/ppermute | solution.py:293
  82.9 2.4 %collective-permute-start.22 = (bf16[4,8,24,512]{3,2,1,0:T(8,128)(2,1)S(1)}, bf16[4,8,24,512]{3,2,1,0:T(8,128)(2,1)S(1)}, u32[]{:S(2)}, u32[]{:S(2)}) collective-permute-start(bf16[4,8,24,512]{3,2,1,0:T(8,128)(2,1)S(1)} %shard_map.104.refs_0_), channel_id=1, source_target_pairs={{0,32},{32,0},{64,96},{96,64},{1,33},{33,1},{65,97},{97,65},{8,40}... | collective-permute-start | bytes 2359304 | tf_op jit(solution)/shard_map/ppermute | solution.py:293
  83.8 2.6 %collective-permute-start.21 = (bf16[4,8,24,512]{3,2,1,0:T(8,128)(2,1)S(1)}, bf16[4,8,24,512]{3,2,1,0:T(8,128)(2,1)S(1)}, u32[]{:S(2)}, u32[]{:S(2)}) collective-permute-start(bf16[4,8,24,512]{3,2,1,0:T(8,128)(2,1)S(1)} %shard_map.105.refs_1_), channel_id=1, source_target_pairs={{0,32},{32,0},{64,96},{96,64},{1,33},{33,1},{65,97},{97,65},{8,40}... | collective-permute-start | bytes 2359304 | tf_op jit(solution)/shard_map/ppermute | solution.py:293
  (4 other events, 94.8 us)

commit v6 on v5

--- a/solution.py
+++ b/solution.py
@@ -56,7 +56,7 @@
     return jnp.where(core == 0, p, q), jnp.where(core == 0, q, p)
 
 
-OFFSETS = ((2, 1), (3, 1), (1, 1), (2, 0), (0, 1), (3, 0), (1, 0))
+OFFSETS = ((1, 1), (3, 1), (2, 1), (2, 0), (1, 0), (3, 0), (0, 1))
 OWN = (0, 0)
 HALVES = (OFFSETS[:4], OFFSETS[4:] + (OWN,))
 RINGS = (0, 1, 3, 2)
@@ -146,10 +146,10 @@
 def open_kernel(got, updates):
     total = jnp.zeros((1, 128), F32)
     for k in range(GROUP):
-        updates[k] = got[k, 0:ROWS]
+        updates[k * ROWS : (k + 1) * ROWS] = got[k, 0:ROWS]
         three = got[k, ROWS:, 0:128].astype(F32)
         total = total + ((three[0:1] + three[1:2]) + three[2:3])
-    updates[GROUP] = jnp.concatenate([in_three(total), jnp.zeros((ROWS - 8, COLS), F32)], axis=0).astype(BF16)
+    updates[GROUP * ROWS :] = in_three(total).astype(BF16)
 
 
 def trust_and_runs(total):
@@ -175,7 +175,7 @@
     parts, (out, totals) = refs[:GROUP], refs[GROUP:]
     place = group_places(me[0])[0]
     for part, offset in zip(parts, OFFSETS + (OWN,)):
-        three = part[GROUP, 0:8, 0:128].astype(F32)
+        three = part[GROUP * ROWS :, 0:128].astype(F32)
         total = (three[0:1] + three[1:2]) + three[2:3]
         totals[source_place(place, offset)] = jnp.broadcast_to(total, (8, 128))
     total = totals[0]
@@ -204,7 +204,7 @@
             for j, offset in enumerate(offsets):
                 factor = row_trust(owner_of(core, source_place(place, offset), b) * ROWS, *three)
                 member = (OFFSETS + (OWN,)).index(offset)
-                block = weights[pair, member].astype(F32) - step_size * (factor * updates[j][b].astype(F32))
+                block = weights[pair, member].astype(F32) - step_size * (factor * updates[j][pl.ds(pl.multiple_of(b * ROWS, 8), ROWS)].astype(F32))
                 params[j, b] = block.astype(BF16)
 
 
@@ -324,7 +324,7 @@
 
     pay = kernel(pay_kernel, [VMEM] * 2, VMEM, of((GROUP, PAY, COLS), BF16))(update, sums)
     got = exchange(pay, NARROW)
-    updates = kernel(open_kernel, [VMEM], VMEM, more)(got)
+    updates = kernel(open_kernel, [VMEM], VMEM, pltpu.VMEM((GROUP * ROWS + 8, COLS), BF16))(got)
     beside = send(updates, shift(WIDE, (0, 1)))
     wide = {OWN: updates, (0, 1): beside}
     for pair, value in enumerate((updates, beside)):

time: 87.7 us -> 87.5 us (level)
  waiting for transfers between devices: 23.5 us -> 21 us
  starting transfers between devices: 45.9 us -> 48.1 us
    ppermute x23, waiting for transfers between devices: 18.6 us -> 16.1 us  [send(): return lax.ppermute(value, 'i', pairs)]
    ppermute x23, starting transfers between devices: 41.9 us -> 44 us  [send(): return lax.ppermute(value, 'i', pairs)]
  transfers between devices with their start and end apart: 24 -> 24, of which waited for: 13 -> 12; matrix products, arithmetic and copies ran while one was open for 0% -> 0% of each run, Pallas kernels for 6% -> 6%
where the time goes in v6:
time: 87.5 us; the launch traced here: 87 us
  starting transfers between devices  48.1 us (55%)
  waiting for transfers between devices  21 us (24%)
  Pallas kernels  8.83 us (10%)
  blocking collectives  8.3 us (9%)
    ppermute x23, starting transfers between devices, send(): return lax.ppermute(value, 'i', pairs)  44 us
    ppermute x23, waiting for transfers between devices, send(): return lax.ppermute(value, 'i', pairs)  16.1 us
    all_to_all x1, blocking collectives, exchange(): lax.all_to_all(value, 'i', 0, 0, axis_index_groups=groups, tiled=True)  8.3 us
    all_to_all x1, waiting for transfers between devices, exchange(): lax.all_to_all(value, 'i', 0, 0, axis_index_groups=groups, tiled=True)  4.88 us
    all_to_all x1, starting transfers between devices, exchange(): lax.all_to_all(value, 'i', 0, 0, axis_index_groups=groups, tiled=True)  4.02 us
    pallas_call x3, Pallas kernels, place(): kernel(functools.partial(place_kernel, arrays=len(arrays), chunks=chunks,...  2.94 us
    pallas_call x2, Pallas kernels, take(): kernel(body, [SMEM, HBM], [VMEM] * 2, [half] * 2, scratch_shapes=[pltpu.S...  2.83 us
  transfers between devices with their start and end apart: 24, of which 12 were waited for; matrix products, arithmetic and copies ran while one was open for 0% of the time, Pallas kernels for 6%

profile of v6, /device:TPU:1, one launch (start us, length us, event | category | flops | bytes accessed | tf_op | source)
XLA Modules:
  0.0 87.0 jit_solution(7323701879877611149)
XLA Ops:
  0.6 1.5 %shard_map.93 = (bf16[4,8,24,512]{3,2,1,0:T(8,128)(2,1)S(1)}, bf16[4,8,24,512]{3,2,1,0:T(8,128)(2,1)S(1)}) custom-call(s32[1]{0:T(128)} %bitcast.me, bf16[128,24,512]{2,1,0:T(8,128)(2,1)} %bitcast.4), custom_call_target="tpu_custom_call" | custom-call | tf_op jit(solution)/shard_map/pallas_call | solution.py:300
  2.1 1.5 %collective-permute-start.5 = (bf16[4,8,24,512]{3,2,1,0:T(8,128)(2,1)S(1)}, bf16[4,8,24,512]{3,2,1,0:T(8,128)(2,1)S(1)}, u32[]{:S(2)}, u32[]{:S(2)}) collective-permute-start(bf16[4,8,24,512]{3,2,1,0:T(8,128)(2,1)S(1)} %get-tuple-element.40), channel_id=1, source_target_pairs={{0,32},{32,0},{64,96},{96,64},{1,33},{33,1},{65,97},{97,65},{8,40}... | collective-permute-start | bytes 2359304 | tf_op jit(solution)/shard_map/ppermute | solution.py:293
  3.7 1.4 %shard_map.92 = (bf16[4,8,24,512]{3,2,1,0:T(8,128)(2,1)S(1)}, bf16[4,8,24,512]{3,2,1,0:T(8,128)(2,1)S(1)}) custom-call(s32[1]{0:T(128)} %bitcast.me, bf16[128,24,512]{2,1,0:T(8,128)(2,1)} %bitcast.5), custom_call_target="tpu_custom_call" | custom-call | tf_op jit(solution)/shard_map/pallas_call | solution.py:300
  5.6 1.8 %collective-permute-start.6 = (bf16[9,24,512]{2,1,0:T(8,128)(2,1)S(1)}, bf16[9,24,512]{2,1,0:T(8,128)(2,1)S(1)}, u32[]{:S(2)}, u32[]{:S(2)}) collective-permute-start(bf16[9,24,512]{2,1,0:T(8,128)(2,1)S(1)} %get-tuple-element.41), channel_id=1, source_target_pairs={{6,0},{14,8},{0,2},{8,10},{2,4},{10,12},{4,6},{12,14},{30,24},{22,... | collective-permute-start | bytes 663560 | tf_op jit(solution)/shard_map/ppermute | solution.py:293
  7.4 2.2 %collective-permute-start.7 = (bf16[9,24,512]{2,1,0:T(8,128)(2,1)S(1)}, bf16[9,24,512]{2,1,0:T(8,128)(2,1)S(1)}, u32[]{:S(2)}, u32[]{:S(2)}) collective-permute-start(bf16[9,24,512]{2,1,0:T(8,128)(2,1)S(1)} %get-tuple-element.42), channel_id=1, source_target_pairs={{2,0},{10,8},{4,2},{12,10},{6,4},{14,12},{0,6},{8,14},{26,24},{18,... | collective-permute-start | bytes 663560 | tf_op jit(solution)/shard_map/ppermute | solution.py:293
  9.6 2.7 %collective-permute-start.8 = (bf16[9,24,512]{2,1,0:T(8,128)(2,1)S(1)}, bf16[9,24,512]{2,1,0:T(8,128)(2,1)S(1)}, u32[]{:S(2)}, u32[]{:S(2)}) collective-permute-start(bf16[9,24,512]{2,1,0:T(8,128)(2,1)S(1)} %get-tuple-element.43), channel_id=1, source_target_pairs={{8,0},{0,8},{10,2},{2,10},{12,4},{4,12},{14,6},{6,14},{16,24},{24,... | collective-permute-start | bytes 663560 | tf_op jit(solution)/shard_map/ppermute | solution.py:293
  12.5 4.8 %collective-permute-start.2 = (bf16[9,24,512]{2,1,0:T(8,128)(2,1)S(1)}, bf16[9,24,512]{2,1,0:T(8,128)(2,1)S(1)}, u32[]{:S(2)}, u32[]{:S(2)}) collective-permute-start(bf16[9,24,512]{2,1,0:T(8,128)(2,1)S(1)} %get-tuple-element.36), channel_id=1, source_target_pairs={{10,0},{2,8},{12,2},{4,10},{14,4},{6,12},{8,6},{0,14},{18,24},{26,... | collective-permute-start | bytes 663560 | tf_op jit(solution)/shard_map/ppermute | solution.py:293
  17.3 2.7 %collective-permute-start.4 = (bf16[9,24,512]{2,1,0:T(8,128)(2,1)S(1)}, bf16[9,24,512]{2,1,0:T(8,128)(2,1)S(1)}, u32[]{:S(2)}, u32[]{:S(2)}) collective-permute-start(bf16[9,24,512]{2,1,0:T(8,128)(2,1)S(1)} %get-tuple-element.38), channel_id=1, source_target_pairs={{4,0},{12,8},{6,2},{14,10},{0,4},{8,12},{2,6},{10,14},{28,24},{20,... | collective-permute-start | bytes 663560 | tf_op jit(solution)/shard_map/ppermute | solution.py:293
  21.5 4.3 %collective-permute-done.3.refs_2_ = bf16[9,24,512]{2,1,0:T(8,128)(2,1)S(1)} collective-permute-done((bf16[9,24,512]{2,1,0:T(8,128)(2,1)S(1)}, bf16[9,24,512]{2,1,0:T(8,128)(2,1)S(1)}, u32[]{:S(2)}, u32[]{:S(2)}) %collective-permute-start.3) | collective-permute-done | bytes 221216 | tf_op jit(solution)/shard_map/ppermute | solution.py:293
  26.9 4.0 %all-to-all-start = ((bf16[8,24,512]{2,1,0:T(8,128)(2,1)}), bf16[8,24,512]{2,1,0:T(8,128)(2,1)S(1)}, u32[]{:S(2)}, u32[]{:S(2)}) async-start(bf16[8,24,512]{2,1,0:T(8,128)(2,1)} %get-tuple-element.45), calls=%async_computation | async-start | bytes 393216 | tf_op jit(solution)/shard_map/all_to_all | solution.py:89
  31.6 4.9 %all-to-all-done.parts = bf16[8,24,512]{2,1,0:T(8,128)(2,1)S(1)} async-done(((bf16[8,24,512]{2,1,0:T(8,128)(2,1)}), bf16[8,24,512]{2,1,0:T(8,128)(2,1)S(1)}, u32[]{:S(2)}, u32[]{:S(2)}) %all-to-all-start) | async-done | bytes 196640 | tf_op jit(solution)/shard_map/all_to_all | solution.py:89
  36.6 8.3 %all_to_all.10.got = bf16[8,32,512]{2,1,0:T(8,128)(2,1)S(1)} all-to-all(bf16[8,32,512]{2,1,0:T(8,128)(2,1)S(1)} %shard_map.99), channel_id=1, replica_groups={{0,24,64,88,1,25,65,89},{8,16,72,80,9,17,73,81},{2,26,66,90,3,27,67,91}..., dimensions={0} | all-to-all | bytes 524288 | tf_op jit(solution)/shard_map/all_to_all | solution.py:89
  45.0 2.4 %collective-permute-start.9 = (bf16[200,512]{1,0:T(8,128)(2,1)S(1)}, bf16[200,512]{1,0:T(8,128)(2,1)S(1)}, u32[]{:S(2)}, u32[]{:S(2)}) collective-permute-start(bf16[200,512]{1,0:T(8,128)(2,1)S(1)} %shard_map.100.refs_7_.refs_0_), channel_id=1, source_target_pairs={{8,0},{0,8},{10,2},{2,10},{12,4},{4,12},{14,6},{6,14},{16,24},{24,... | collective-permute-start | bytes 614408 | tf_op jit(solution)/shard_map/ppermute | solution.py:293
  47.4 2.1 %collective-permute-start.15 = (bf16[200,512]{1,0:T(8,128)(2,1)S(1)}, bf16[200,512]{1,0:T(8,128)(2,1)S(1)}, u32[]{:S(2)}, u32[]{:S(2)}) collective-permute-start(bf16[200,512]{1,0:T(8,128)(2,1)S(1)} %shard_map.100.refs_7_.refs_0_), channel_id=1, source_target_pairs={{2,0},{10,8},{4,2},{12,10},{6,4},{14,12},{0,6},{8,14},{26,24},{18,... | collective-permute-start | bytes 614408 | tf_op jit(solution)/shard_map/ppermute | solution.py:293
  49.8 1.9 %collective-permute-start.13 = (bf16[200,512]{1,0:T(8,128)(2,1)S(1)}, bf16[200,512]{1,0:T(8,128)(2,1)S(1)}, u32[]{:S(2)}, u32[]{:S(2)}) collective-permute-start(bf16[200,512]{1,0:T(8,128)(2,1)S(1)} %shard_map.100.refs_7_.refs_0_), channel_id=1, source_target_pairs={{4,0},{12,8},{6,2},{14,10},{0,4},{8,12},{2,6},{10,14},{28,24},{20,... | collective-permute-start | bytes 614408 | tf_op jit(solution)/shard_map/ppermute | solution.py:293
  52.6 1.9 %collective-permute-start.12 = (bf16[200,512]{1,0:T(8,128)(2,1)S(1)}, bf16[200,512]{1,0:T(8,128)(2,1)S(1)}, u32[]{:S(2)}, u32[]{:S(2)}) collective-permute-start(bf16[200,512]{1,0:T(8,128)(2,1)S(1)} %collective-permute-done.9.refs_6_.refs_3_), channel_id=1, source_target_pairs={{4,0},{12,8},{6,2},{14,10},{0,4},{8,12},{2,6},{10,14},{28,24},{20,... | collective-permute-start | bytes 614408 | tf_op jit(solution)/shard_map/ppermute | solution.py:293
  54.5 1.3 %collective-permute-start.20 = (bf16[2,8,24,512]{3,2,1,0:T(8,128)(2,1)S(1)}, bf16[2,8,24,512]{3,2,1,0:T(8,128)(2,1)S(1)}, u32[]{:S(2)}, u32[]{:S(2)}) collective-permute-start(bf16[2,8,24,512]{3,2,1,0:T(8,128)(2,1)S(1)} %shard_map.103.refs_4_), channel_id=1, source_target_pairs={{1,0},{25,24},{65,64},{89,88},{0,1},{24,25},{64,65},{88,89},{9,8},... | collective-permute-start | bytes 1179656 | tf_op jit(solution)/shard_map/ppermute | solution.py:293
  55.8 1.2 %collective-permute-start.19 = (bf16[2,8,24,512]{3,2,1,0:T(8,128)(2,1)S(1)}, bf16[2,8,24,512]{3,2,1,0:T(8,128)(2,1)S(1)}, u32[]{:S(2)}, u32[]{:S(2)}) collective-permute-start(bf16[2,8,24,512]{3,2,1,0:T(8,128)(2,1)S(1)} %shard_map.103.refs_4_), channel_id=1, source_target_pairs={{64,0},{88,24},{1,64},{25,88},{65,1},{89,25},{0,65},{24,89},{72,8}... | collective-permute-start | bytes 1179656 | tf_op jit(solution)/shard_map/ppermute | solution.py:293
  57.0 3.0 %collective-permute-done.14.refs_4_.refs_1_ = bf16[200,512]{1,0:T(8,128)(2,1)S(1)} collective-permute-done((bf16[200,512]{1,0:T(8,128)(2,1)S(1)}, bf16[200,512]{1,0:T(8,128)(2,1)S(1)}, u32[]{:S(2)}, u32[]{:S(2)}) %collective-permute-start.14) | collective-permute-done | bytes 204832 | tf_op jit(solution)/shard_map/ppermute | solution.py:293
  60.0 1.5 %collective-permute-start.10 = (bf16[200,512]{1,0:T(8,128)(2,1)S(1)}, bf16[200,512]{1,0:T(8,128)(2,1)S(1)}, u32[]{:S(2)}, u32[]{:S(2)}) collective-permute-start(bf16[200,512]{1,0:T(8,128)(2,1)S(1)} %collective-permute-done.9.refs_6_.refs_3_), channel_id=1, source_target_pairs={{6,0},{14,8},{0,2},{8,10},{2,4},{10,12},{4,6},{12,14},{30,24},{22,... | collective-permute-start | bytes 614408 | tf_op jit(solution)/shard_map/ppermute | solution.py:293
  61.4 3.4 %collective-permute-done.11.refs_1_.refs_2_ = bf16[200,512]{1,0:T(8,128)(2,1)S(1)} collective-permute-done((bf16[200,512]{1,0:T(8,128)(2,1)S(1)}, bf16[200,512]{1,0:T(8,128)(2,1)S(1)}, u32[]{:S(2)}, u32[]{:S(2)}) %collective-permute-start.11) | collective-permute-done | bytes 204832 | tf_op jit(solution)/shard_map/ppermute | solution.py:293
  64.9 1.3 %collective-permute-done.10.refs_0_.refs_1_ = bf16[200,512]{1,0:T(8,128)(2,1)S(1)} collective-permute-done((bf16[200,512]{1,0:T(8,128)(2,1)S(1)}, bf16[200,512]{1,0:T(8,128)(2,1)S(1)}, u32[]{:S(2)}, u32[]{:S(2)}) %collective-permute-start.10) | collective-permute-done | bytes 204832 | tf_op jit(solution)/shard_map/ppermute | solution.py:293
  66.2 14.9 %collective-permute-start.16 = (f32[8,128]{1,0:T(8,128)S(1)}, f32[8,128]{1,0:T(8,128)S(1)}, u32[]{:S(2)}, u32[]{:S(2)}) collective-permute-start(f32[8,128]{1,0:T(8,128)S(1)} %shard_map.101.total), channel_id=1, source_target_pairs={{0,32},{32,0},{64,96},{96,64},{1,33},{33,1},{65,97},{97,65},{8,40}... | collective-permute-start | bytes 12296 | tf_op jit(solution)/shard_map/ppermute | solution.py:293
  83.8 1.2 %shard_map.106 = (bf16[128,24,512]{2,1,0:T(8,128)(2,1)}, f32[24,512]{1,0:T(8,128)}, f32[24,512]{1,0:T(8,128)}, f32[24,512]{1,0:T(8,128)}, f32[24,512]{1,0:T(8,128)}) custom-call(s32[1]{0:T(128)} %bitcast.me, bf16[4,8,24,512]{3,2,1,0:T(8,128)(2,1)S(1)} %shard_map.104.refs_0_, bf16[4,8,24,512]{3,2,1,0:T(8,128)(2,1)S(1)} %shard_map.105.refs_1_, ...), custom_call_target="tpu_custom_call" | custom-call | tf_op jit(solution)/shard_map/pallas_call | solution.py:360
  (50 shorter events, 10.1 us)
Async XLA Ops:
  2.1 3.4 %collective-permute-start.5 = (bf16[4,8,24,512]{3,2,1,0:T(8,128)(2,1)S(1)}, bf16[4,8,24,512]{3,2,1,0:T(8,128)(2,1)S(1)}, u32[]{:S(2)}, u32[]{:S(2)}) collective-permute-start(bf16[4,8,24,512]{3,2,1,0:T(8,128)(2,1)S(1)} %get-tuple-element.40), channel_id=1, source_target_pairs={{0,32},{32,0},{64,96},{96,64},{1,33},{33,1},{65,97},{97,65},{8,40}... | collective-permute-start | bytes 2359304 | tf_op jit(solution)/shard_map/ppermute | solution.py:293
  3.6 8.8 %collective-permute-start = (bf16[4,8,24,512]{3,2,1,0:T(8,128)(2,1)S(1)}, bf16[4,8,24,512]{3,2,1,0:T(8,128)(2,1)S(1)}, u32[]{:S(2)}, u32[]{:S(2)}) collective-permute-start(bf16[4,8,24,512]{3,2,1,0:T(8,128)(2,1)S(1)} %get-tuple-element.34), channel_id=1, source_target_pairs={{0,32},{32,0},{64,96},{96,64},{1,33},{33,1},{65,97},{97,65},{8,40}... | collective-permute-start | bytes 2359304 | tf_op jit(solution)/shard_map/ppermute | solution.py:293
  5.6 11.7 %collective-permute-start.6 = (bf16[9,24,512]{2,1,0:T(8,128)(2,1)S(1)}, bf16[9,24,512]{2,1,0:T(8,128)(2,1)S(1)}, u32[]{:S(2)}, u32[]{:S(2)}) collective-permute-start(bf16[9,24,512]{2,1,0:T(8,128)(2,1)S(1)} %get-tuple-element.41), channel_id=1, source_target_pairs={{6,0},{14,8},{0,2},{8,10},{2,4},{10,12},{4,6},{12,14},{30,24},{22,... | collective-permute-start | bytes 663560 | tf_op jit(solution)/shard_map/ppermute | solution.py:293
  7.4 9.9 %collective-permute-start.7 = (bf16[9,24,512]{2,1,0:T(8,128)(2,1)S(1)}, bf16[9,24,512]{2,1,0:T(8,128)(2,1)S(1)}, u32[]{:S(2)}, u32[]{:S(2)}) collective-permute-start(bf16[9,24,512]{2,1,0:T(8,128)(2,1)S(1)} %get-tuple-element.42), channel_id=1, source_target_pairs={{2,0},{10,8},{4,2},{12,10},{6,4},{14,12},{0,6},{8,14},{26,24},{18,... | collective-permute-start | bytes 663560 | tf_op jit(solution)/shard_map/ppermute | solution.py:293
  9.6 10.4 %collective-permute-start.8 = (bf16[9,24,512]{2,1,0:T(8,128)(2,1)S(1)}, bf16[9,24,512]{2,1,0:T(8,128)(2,1)S(1)}, u32[]{:S(2)}, u32[]{:S(2)}) collective-permute-start(bf16[9,24,512]{2,1,0:T(8,128)(2,1)S(1)} %get-tuple-element.43), channel_id=1, source_target_pairs={{8,0},{0,8},{10,2},{2,10},{12,4},{4,12},{14,6},{6,14},{16,24},{24,... | collective-permute-start | bytes 663560 | tf_op jit(solution)/shard_map/ppermute | solution.py:293
  12.4 8.2 %collective-permute-start.1 = (bf16[9,24,512]{2,1,0:T(8,128)(2,1)S(1)}, bf16[9,24,512]{2,1,0:T(8,128)(2,1)S(1)}, u32[]{:S(2)}, u32[]{:S(2)}) collective-permute-start(bf16[9,24,512]{2,1,0:T(8,128)(2,1)S(1)} %get-tuple-element.35), channel_id=1, source_target_pairs={{14,0},{6,8},{8,2},{0,10},{10,4},{2,12},{12,6},{4,14},{22,24},{30,... | collective-permute-start | bytes 663560 | tf_op jit(solution)/shard_map/ppermute | solution.py:293
  12.5 9.0 %collective-permute-start.2 = (bf16[9,24,512]{2,1,0:T(8,128)(2,1)S(1)}, bf16[9,24,512]{2,1,0:T(8,128)(2,1)S(1)}, u32[]{:S(2)}, u32[]{:S(2)}) collective-permute-start(bf16[9,24,512]{2,1,0:T(8,128)(2,1)S(1)} %get-tuple-element.36), channel_id=1, source_target_pairs={{10,0},{2,8},{12,2},{4,10},{14,4},{6,12},{8,6},{0,14},{18,24},{26,... | collective-permute-start | bytes 663560 | tf_op jit(solution)/shard_map/ppermute | solution.py:293
  17.3 8.5 %collective-permute-start.3 = (bf16[9,24,512]{2,1,0:T(8,128)(2,1)S(1)}, bf16[9,24,512]{2,1,0:T(8,128)(2,1)S(1)}, u32[]{:S(2)}, u32[]{:S(2)}) collective-permute-start(bf16[9,24,512]{2,1,0:T(8,128)(2,1)S(1)} %get-tuple-element.37), channel_id=1, source_target_pairs={{12,0},{4,8},{14,2},{6,10},{8,4},{0,12},{10,6},{2,14},{20,24},{28,... | collective-permute-start | bytes 663560 | tf_op jit(solution)/shard_map/ppermute | solution.py:293
  17.3 8.7 %collective-permute-start.4 = (bf16[9,24,512]{2,1,0:T(8,128)(2,1)S(1)}, bf16[9,24,512]{2,1,0:T(8,128)(2,1)S(1)}, u32[]{:S(2)}, u32[]{:S(2)}) collective-permute-start(bf16[9,24,512]{2,1,0:T(8,128)(2,1)S(1)} %get-tuple-element.38), channel_id=1, source_target_pairs={{4,0},{12,8},{6,2},{14,10},{0,4},{8,12},{2,6},{10,14},{28,24},{20,... | collective-permute-start | bytes 663560 | tf_op jit(solution)/shard_map/ppermute | solution.py:293
  26.9 9.5 %all-to-all-start = ((bf16[8,24,512]{2,1,0:T(8,128)(2,1)}), bf16[8,24,512]{2,1,0:T(8,128)(2,1)S(1)}, u32[]{:S(2)}, u32[]{:S(2)}) async-start(bf16[8,24,512]{2,1,0:T(8,128)(2,1)} %get-tuple-element.45), calls=%async_computation | async-start | bytes 393216 | tf_op jit(solution)/shard_map/all_to_all | solution.py:89
  45.0 7.6 %collective-permute-start.9 = (bf16[200,512]{1,0:T(8,128)(2,1)S(1)}, bf16[200,512]{1,0:T(8,128)(2,1)S(1)}, u32[]{:S(2)}, u32[]{:S(2)}) collective-permute-start(bf16[200,512]{1,0:T(8,128)(2,1)S(1)} %shard_map.100.refs_7_.refs_0_), channel_id=1, source_target_pairs={{8,0},{0,8},{10,2},{2,10},{12,4},{4,12},{14,6},{6,14},{16,24},{24,... | collective-permute-start | bytes 614408 | tf_op jit(solution)/shard_map/ppermute | solution.py:293
  47.4 8.4 %collective-permute-start.15 = (bf16[200,512]{1,0:T(8,128)(2,1)S(1)}, bf16[200,512]{1,0:T(8,128)(2,1)S(1)}, u32[]{:S(2)}, u32[]{:S(2)}) collective-permute-start(bf16[200,512]{1,0:T(8,128)(2,1)S(1)} %shard_map.100.refs_7_.refs_0_), channel_id=1, source_target_pairs={{2,0},{10,8},{4,2},{12,10},{6,4},{14,12},{0,6},{8,14},{26,24},{18,... | collective-permute-start | bytes 614408 | tf_op jit(solution)/shard_map/ppermute | solution.py:293
  49.5 10.5 %collective-permute-start.14 = (bf16[200,512]{1,0:T(8,128)(2,1)S(1)}, bf16[200,512]{1,0:T(8,128)(2,1)S(1)}, u32[]{:S(2)}, u32[]{:S(2)}) collective-permute-start(bf16[200,512]{1,0:T(8,128)(2,1)S(1)} %shard_map.100.refs_7_.refs_0_), channel_id=1, source_target_pairs={{6,0},{14,8},{0,2},{8,10},{2,4},{10,12},{4,6},{12,14},{30,24},{22,... | collective-permute-start | bytes 614408 | tf_op jit(solution)/shard_map/ppermute | solution.py:293
  49.5 5.0 %collective-permute-start.17 = (bf16[8,24,512]{2,1,0:T(8,128)(2,1)S(1)}, bf16[8,24,512]{2,1,0:T(8,128)(2,1)S(1)}, u32[]{:S(2)}, u32[]{:S(2)}) collective-permute-start(bf16[8,24,512]{2,1,0:T(8,128)(2,1)S(1)} %get-tuple-element.51.refs_0_), channel_id=1, source_target_pairs={{24,0},{0,24},{88,64},{64,88},{25,1},{1,25},{89,65},{65,89},{16,8}... | collective-permute-start | bytes 589832 | tf_op jit(solution)/shard_map/ppermute | solution.py:293
  49.8 10.2 %collective-permute-start.13 = (bf16[200,512]{1,0:T(8,128)(2,1)S(1)}, bf16[200,512]{1,0:T(8,128)(2,1)S(1)}, u32[]{:S(2)}, u32[]{:S(2)}) collective-permute-start(bf16[200,512]{1,0:T(8,128)(2,1)S(1)} %shard_map.100.refs_7_.refs_0_), channel_id=1, source_target_pairs={{4,0},{12,8},{6,2},{14,10},{0,4},{8,12},{2,6},{10,14},{28,24},{20,... | collective-permute-start | bytes 614408 | tf_op jit(solution)/shard_map/ppermute | solution.py:293
  52.6 7.4 %collective-permute-start.12 = (bf16[200,512]{1,0:T(8,128)(2,1)S(1)}, bf16[200,512]{1,0:T(8,128)(2,1)S(1)}, u32[]{:S(2)}, u32[]{:S(2)}) collective-permute-start(bf16[200,512]{1,0:T(8,128)(2,1)S(1)} %collective-permute-done.9.refs_6_.refs_3_), channel_id=1, source_target_pairs={{4,0},{12,8},{6,2},{14,10},{0,4},{8,12},{2,6},{10,14},{28,24},{20,... | collective-permute-start | bytes 614408 | tf_op jit(solution)/shard_map/ppermute | solution.py:293
  54.5 27.7 %collective-permute-start.20 = (bf16[2,8,24,512]{3,2,1,0:T(8,128)(2,1)S(1)}, bf16[2,8,24,512]{3,2,1,0:T(8,128)(2,1)S(1)}, u32[]{:S(2)}, u32[]{:S(2)}) collective-permute-start(bf16[2,8,24,512]{3,2,1,0:T(8,128)(2,1)S(1)} %shard_map.103.refs_4_), channel_id=1, source_target_pairs={{1,0},{25,24},{65,64},{89,88},{0,1},{24,25},{64,65},{88,89},{9,8},... | collective-permute-start | bytes 1179656 | tf_op jit(solution)/shard_map/ppermute | solution.py:293
  55.8 26.4 %collective-permute-start.19 = (bf16[2,8,24,512]{3,2,1,0:T(8,128)(2,1)S(1)}, bf16[2,8,24,512]{3,2,1,0:T(8,128)(2,1)S(1)}, u32[]{:S(2)}, u32[]{:S(2)}) collective-permute-start(bf16[2,8,24,512]{3,2,1,0:T(8,128)(2,1)S(1)} %shard_map.103.refs_4_), channel_id=1, source_target_pairs={{64,0},{88,24},{1,64},{25,88},{65,1},{89,25},{0,65},{24,89},{72,8}... | collective-permute-start | bytes 1179656 | tf_op jit(solution)/shard_map/ppermute | solution.py:293
  60.0 22.3 %collective-permute-start.18 = (bf16[2,8,24,512]{3,2,1,0:T(8,128)(2,1)S(1)}, bf16[2,8,24,512]{3,2,1,0:T(8,128)(2,1)S(1)}, u32[]{:S(2)}, u32[]{:S(2)}) collective-permute-start(bf16[2,8,24,512]{3,2,1,0:T(8,128)(2,1)S(1)} %shard_map.103.refs_4_), channel_id=1, source_target_pairs={{65,0},{89,24},{0,64},{24,88},{64,1},{88,25},{1,65},{25,89},{73,8}... | collective-permute-start | bytes 1179656 | tf_op jit(solution)/shard_map/ppermute | solution.py:293
  60.0 4.9 %collective-permute-start.11 = (bf16[200,512]{1,0:T(8,128)(2,1)S(1)}, bf16[200,512]{1,0:T(8,128)(2,1)S(1)}, u32[]{:S(2)}, u32[]{:S(2)}) collective-permute-start(bf16[200,512]{1,0:T(8,128)(2,1)S(1)} %collective-permute-done.9.refs_6_.refs_3_), channel_id=1, source_target_pairs={{2,0},{10,8},{4,2},{12,10},{6,4},{14,12},{0,6},{8,14},{26,24},{18,... | collective-permute-start | bytes 614408 | tf_op jit(solution)/shard_map/ppermute | solution.py:293
  60.0 6.2 %collective-permute-start.10 = (bf16[200,512]{1,0:T(8,128)(2,1)S(1)}, bf16[200,512]{1,0:T(8,128)(2,1)S(1)}, u32[]{:S(2)}, u32[]{:S(2)}) collective-permute-start(bf16[200,512]{1,0:T(8,128)(2,1)S(1)} %collective-permute-done.9.refs_6_.refs_3_), channel_id=1, source_target_pairs={{6,0},{14,8},{0,2},{8,10},{2,4},{10,12},{4,6},{12,14},{30,24},{22,... | collective-permute-start | bytes 614408 | tf_op jit(solution)/shard_map/ppermute | solution.py:293
  66.2 15.8 %collective-permute-start.16 = (f32[8,128]{1,0:T(8,128)S(1)}, f32[8,128]{1,0:T(8,128)S(1)}, u32[]{:S(2)}, u32[]{:S(2)}) collective-permute-start(f32[8,128]{1,0:T(8,128)S(1)} %shard_map.101.total), channel_id=1, source_target_pairs={{0,32},{32,0},{64,96},{96,64},{1,33},{33,1},{65,97},{97,65},{8,40}... | collective-permute-start | bytes 12296 | tf_op jit(solution)/shard_map/ppermute | solution.py:293
  82.7 2.4 %collective-permute-start.22 = (bf16[4,8,24,512]{3,2,1,0:T(8,128)(2,1)S(1)}, bf16[4,8,24,512]{3,2,1,0:T(8,128)(2,1)S(1)}, u32[]{:S(2)}, u32[]{:S(2)}) collective-permute-start(bf16[4,8,24,512]{3,2,1,0:T(8,128)(2,1)S(1)} %shard_map.104.refs_0_), channel_id=1, source_target_pairs={{0,32},{32,0},{64,96},{96,64},{1,33},{33,1},{65,97},{97,65},{8,40}... | collective-permute-start | bytes 2359304 | tf_op jit(solution)/shard_map/ppermute | solution.py:293
  83.5 2.6 %collective-permute-start.21 = (bf16[4,8,24,512]{3,2,1,0:T(8,128)(2,1)S(1)}, bf16[4,8,24,512]{3,2,1,0:T(8,128)(2,1)S(1)}, u32[]{:S(2)}, u32[]{:S(2)}) collective-permute-start(bf16[4,8,24,512]{3,2,1,0:T(8,128)(2,1)S(1)} %shard_map.105.refs_1_), channel_id=1, source_target_pairs={{0,32},{32,0},{64,96},{96,64},{1,33},{33,1},{65,97},{97,65},{8,40}... | collective-permute-start | bytes 2359304 | tf_op jit(solution)/shard_map/ppermute | solution.py:293
  (4 other events, 93.5 us)

commit v7 on v6

--- a/solution.py
+++ b/solution.py
@@ -56,9 +56,9 @@
     return jnp.where(core == 0, p, q), jnp.where(core == 0, q, p)
 
 
-OFFSETS = ((1, 1), (3, 1), (2, 1), (2, 0), (1, 0), (3, 0), (0, 1))
+OFFSETS = ((1, 1), (3, 1), (2, 0), (2, 1), (0, 1), (1, 0), (3, 0))
 OWN = (0, 0)
-HALVES = (OFFSETS[:4], OFFSETS[4:] + (OWN,))
+HALVES = (OFFSETS[:3], OFFSETS[3:] + (OWN,))
 RINGS = (0, 1, 3, 2)
 
 
@@ -293,13 +293,11 @@
         return lax.ppermute(value, "i", pairs)
 
     blocks = pltpu.with_memory_space_constraint(gradients.reshape(2 * CHIPS, ROWS, COLS), pltpu.HBM)
-    half = pltpu.VMEM((4, GROUP, ROWS, COLS), BF16)
+    half = [pltpu.VMEM((len(offsets), GROUP, ROWS, COLS), BF16) for offsets in HALVES]
 
     def take(other):
         body = functools.partial(take_kernel, other=other)
-        return kernel(
-            body, [SMEM, HBM], [VMEM] * 2, [half] * 2, scratch_shapes=[pltpu.SemaphoreType.DMA((2,))]
-        )(me, blocks)
+        return kernel(body, [SMEM, HBM], [VMEM] * 2, half, scratch_shapes=[pltpu.SemaphoreType.DMA((2,))])(me, blocks)
 
     sent = take(True)
     arrived = [send(sent[k], CORE_SWAP) for k in range(2)]
@@ -307,7 +305,9 @@
     chunks = []
     more = pltpu.VMEM((GROUP + 1, ROWS, COLS), BF16)
     for k in range(2):
-        chunks += kernel(add_kernel, [VMEM] * 3, [VMEM] * 4, [more] * 4)(kept[k], arrived[k], master_weights)
+        chunks += kernel(add_kernel, [VMEM] * 3, [VMEM] * len(HALVES[k]), [more] * len(HALVES[k]))(
+            kept[k], arrived[k], master_weights
+        )
     tensor, sums = kernel(
         before_kernel, [VMEM, SMEM], (VMEM, VMEM), (pltpu.VMEM((ROWS, 128), jnp.int32), pltpu.VMEM((8, 128), F32))
     )(master_weights, tensor_ids)

time: 87.5 us -> 87.3 us (level)
  no operation moved by 1% of the time
where the time goes in v7:
time: 87.3 us; the launch traced here: 86.8 us
  starting transfers between devices  48.3 us (55%)
  waiting for transfers between devices  20.6 us (24%)
  Pallas kernels  8.83 us (10%)
  blocking collectives  8.3 us (10%)
    ppermute x23, starting transfers between devices, send(): return lax.ppermute(value, 'i', pairs)  44.3 us
    ppermute x23, waiting for transfers between devices, send(): return lax.ppermute(value, 'i', pairs)  15.7 us
    all_to_all x1, blocking collectives, exchange(): lax.all_to_all(value, 'i', 0, 0, axis_index_groups=groups, tiled=True)  8.3 us
    all_to_all x1, waiting for transfers between devices, exchange(): lax.all_to_all(value, 'i', 0, 0, axis_index_groups=groups, tiled=True)  4.88 us
    all_to_all x1, starting transfers between devices, exchange(): lax.all_to_all(value, 'i', 0, 0, axis_index_groups=groups, tiled=True)  4.02 us
    pallas_call x3, Pallas kernels, place(): kernel(functools.partial(place_kernel, arrays=len(arrays), chunks=chunks,...  2.94 us
    pallas_call x2, Pallas kernels, take(): kernel(body, [SMEM, HBM], [VMEM] * 2, half, scratch_shapes=[pltpu.Semapho...  2.83 us
  transfers between devices with their start and end apart: 24, of which 12 were waited for; matrix products, arithmetic and copies ran while one was open for 0% of the time, Pallas kernels for 6%

profile of v7, /device:TPU:1, one launch (start us, length us, event | category | flops | bytes accessed | tf_op | source)
XLA Modules:
  0.0 86.8 jit_solution(12617904140715946378)
XLA Ops:
  0.6 1.5 %shard_map.93 = (bf16[3,8,24,512]{3,2,1,0:T(8,128)(2,1)S(1)}, bf16[5,8,24,512]{3,2,1,0:T(8,128)(2,1)S(1)}) custom-call(s32[1]{0:T(128)} %bitcast.me, bf16[128,24,512]{2,1,0:T(8,128)(2,1)} %bitcast.4), custom_call_target="tpu_custom_call" | custom-call | tf_op jit(solution)/shard_map/pallas_call | solution.py:300
  2.1 1.5 %collective-permute-start.4 = (bf16[5,8,24,512]{3,2,1,0:T(8,128)(2,1)S(1)}, bf16[5,8,24,512]{3,2,1,0:T(8,128)(2,1)S(1)}, u32[]{:S(2)}, u32[]{:S(2)}) collective-permute-start(bf16[5,8,24,512]{3,2,1,0:T(8,128)(2,1)S(1)} %get-tuple-element.39), channel_id=1, source_target_pairs={{0,32},{32,0},{64,96},{96,64},{1,33},{33,1},{65,97},{97,65},{8,40}... | collective-permute-start | bytes 2949128 | tf_op jit(solution)/shard_map/ppermute | solution.py:293
  3.7 1.4 %shard_map.92 = (bf16[3,8,24,512]{3,2,1,0:T(8,128)(2,1)S(1)}, bf16[5,8,24,512]{3,2,1,0:T(8,128)(2,1)S(1)}) custom-call(s32[1]{0:T(128)} %bitcast.me, bf16[128,24,512]{2,1,0:T(8,128)(2,1)} %bitcast.5), custom_call_target="tpu_custom_call" | custom-call | tf_op jit(solution)/shard_map/pallas_call | solution.py:300
  5.1 1.5 %collective-permute-done.arrived = bf16[3,8,24,512]{3,2,1,0:T(8,128)(2,1)S(1)} collective-permute-done((bf16[3,8,24,512]{3,2,1,0:T(8,128)(2,1)S(1)}, bf16[3,8,24,512]{3,2,1,0:T(8,128)(2,1)S(1)}, u32[]{:S(2)}, u32[]{:S(2)}) %collective-permute-start) | collective-permute-done | bytes 589856 | tf_op jit(solution)/shard_map/ppermute | solution.py:293
  6.7 4.3 %collective-permute-start.1 = (bf16[9,24,512]{2,1,0:T(8,128)(2,1)S(1)}, bf16[9,24,512]{2,1,0:T(8,128)(2,1)S(1)}, u32[]{:S(2)}, u32[]{:S(2)}) collective-permute-start(bf16[9,24,512]{2,1,0:T(8,128)(2,1)S(1)} %get-tuple-element.35), channel_id=1, source_target_pairs={{14,0},{6,8},{8,2},{0,10},{10,4},{2,12},{12,6},{4,14},{22,24},{30,... | collective-permute-start | bytes 663560 | tf_op jit(solution)/shard_map/ppermute | solution.py:293
  10.9 2.2 %collective-permute-start.2 = (bf16[9,24,512]{2,1,0:T(8,128)(2,1)S(1)}, bf16[9,24,512]{2,1,0:T(8,128)(2,1)S(1)}, u32[]{:S(2)}, u32[]{:S(2)}) collective-permute-start(bf16[9,24,512]{2,1,0:T(8,128)(2,1)S(1)} %get-tuple-element.36), channel_id=1, source_target_pairs={{10,0},{2,8},{12,2},{4,10},{14,4},{6,12},{8,6},{0,14},{18,24},{26,... | collective-permute-start | bytes 663560 | tf_op jit(solution)/shard_map/ppermute | solution.py:293
  14.4 2.9 %collective-permute-start.5 = (bf16[9,24,512]{2,1,0:T(8,128)(2,1)S(1)}, bf16[9,24,512]{2,1,0:T(8,128)(2,1)S(1)}, u32[]{:S(2)}, u32[]{:S(2)}) collective-permute-start(bf16[9,24,512]{2,1,0:T(8,128)(2,1)S(1)} %get-tuple-element.40), channel_id=1, source_target_pairs={{12,0},{4,8},{14,2},{6,10},{8,4},{0,12},{10,6},{2,14},{20,24},{28,... | collective-permute-start | bytes 663560 | tf_op jit(solution)/shard_map/ppermute | solution.py:293
  17.3 1.4 %collective-permute-start.6 = (bf16[9,24,512]{2,1,0:T(8,128)(2,1)S(1)}, bf16[9,24,512]{2,1,0:T(8,128)(2,1)S(1)}, u32[]{:S(2)}, u32[]{:S(2)}) collective-permute-start(bf16[9,24,512]{2,1,0:T(8,128)(2,1)S(1)} %get-tuple-element.41), channel_id=1, source_target_pairs={{8,0},{0,8},{10,2},{2,10},{12,4},{4,12},{14,6},{6,14},{16,24},{24,... | collective-permute-start | bytes 663560 | tf_op jit(solution)/shard_map/ppermute | solution.py:293
  18.7 2.7 %collective-permute-start.8 = (bf16[9,24,512]{2,1,0:T(8,128)(2,1)S(1)}, bf16[9,24,512]{2,1,0:T(8,128)(2,1)S(1)}, u32[]{:S(2)}, u32[]{:S(2)}) collective-permute-start(bf16[9,24,512]{2,1,0:T(8,128)(2,1)S(1)} %get-tuple-element.43), channel_id=1, source_target_pairs={{2,0},{10,8},{4,2},{12,10},{6,4},{14,12},{0,6},{8,14},{26,24},{18,... | collective-permute-start | bytes 663560 | tf_op jit(solution)/shard_map/ppermute | solution.py:293
  21.4 1.6 %collective-permute-done.5.refs_3_ = bf16[9,24,512]{2,1,0:T(8,128)(2,1)S(1)} collective-permute-done((bf16[9,24,512]{2,1,0:T(8,128)(2,1)S(1)}, bf16[9,24,512]{2,1,0:T(8,128)(2,1)S(1)}, u32[]{:S(2)}, u32[]{:S(2)}) %collective-permute-start.5) | collective-permute-done | bytes 221216 | tf_op jit(solution)/shard_map/ppermute | solution.py:293
  23.0 1.4 %collective-permute-done.6.refs_4_ = bf16[9,24,512]{2,1,0:T(8,128)(2,1)S(1)} collective-permute-done((bf16[9,24,512]{2,1,0:T(8,128)(2,1)S(1)}, bf16[9,24,512]{2,1,0:T(8,128)(2,1)S(1)}, u32[]{:S(2)}, u32[]{:S(2)}) %collective-permute-start.6) | collective-permute-done | bytes 221216 | tf_op jit(solution)/shard_map/ppermute | solution.py:293
  26.1 4.0 %all-to-all-start = ((bf16[8,24,512]{2,1,0:T(8,128)(2,1)}), bf16[8,24,512]{2,1,0:T(8,128)(2,1)S(1)}, u32[]{:S(2)}, u32[]{:S(2)}) async-start(bf16[8,24,512]{2,1,0:T(8,128)(2,1)} %get-tuple-element.45), calls=%async_computation | async-start | bytes 393216 | tf_op jit(solution)/shard_map/all_to_all | solution.py:89
  30.8 4.9 %all-to-all-done.parts = bf16[8,24,512]{2,1,0:T(8,128)(2,1)S(1)} async-done(((bf16[8,24,512]{2,1,0:T(8,128)(2,1)}), bf16[8,24,512]{2,1,0:T(8,128)(2,1)S(1)}, u32[]{:S(2)}, u32[]{:S(2)}) %all-to-all-start) | async-done | bytes 196640 | tf_op jit(solution)/shard_map/all_to_all | solution.py:89
  35.9 8.3 %all_to_all.10.got = bf16[8,32,512]{2,1,0:T(8,128)(2,1)S(1)} all-to-all(bf16[8,32,512]{2,1,0:T(8,128)(2,1)S(1)} %shard_map.99), channel_id=1, replica_groups={{0,24,64,88,1,25,65,89},{8,16,72,80,9,17,73,81},{2,26,66,90,3,27,67,91}..., dimensions={0} | all-to-all | bytes 524288 | tf_op jit(solution)/shard_map/all_to_all | solution.py:89
  44.2 2.8 %collective-permute-start.9 = (bf16[200,512]{1,0:T(8,128)(2,1)S(1)}, bf16[200,512]{1,0:T(8,128)(2,1)S(1)}, u32[]{:S(2)}, u32[]{:S(2)}) collective-permute-start(bf16[200,512]{1,0:T(8,128)(2,1)S(1)} %shard_map.100.refs_7_.refs_0_), channel_id=1, source_target_pairs={{8,0},{0,8},{10,2},{2,10},{12,4},{4,12},{14,6},{6,14},{16,24},{24,... | collective-permute-start | bytes 614408 | tf_op jit(solution)/shard_map/ppermute | solution.py:293
  47.0 2.4 %collective-permute-start.15 = (bf16[200,512]{1,0:T(8,128)(2,1)S(1)}, bf16[200,512]{1,0:T(8,128)(2,1)S(1)}, u32[]{:S(2)}, u32[]{:S(2)}) collective-permute-start(bf16[200,512]{1,0:T(8,128)(2,1)S(1)} %shard_map.100.refs_7_.refs_0_), channel_id=1, source_target_pairs={{2,0},{10,8},{4,2},{12,10},{6,4},{14,12},{0,6},{8,14},{26,24},{18,... | collective-permute-start | bytes 614408 | tf_op jit(solution)/shard_map/ppermute | solution.py:293
  51.7 1.7 %collective-permute-start.13 = (bf16[200,512]{1,0:T(8,128)(2,1)S(1)}, bf16[200,512]{1,0:T(8,128)(2,1)S(1)}, u32[]{:S(2)}, u32[]{:S(2)}) collective-permute-start(bf16[200,512]{1,0:T(8,128)(2,1)S(1)} %collective-permute-done.9.refs_4_.refs_1_), channel_id=1, source_target_pairs={{4,0},{12,8},{6,2},{14,10},{0,4},{8,12},{2,6},{10,14},{28,24},{20,... | collective-permute-start | bytes 614408 | tf_op jit(solution)/shard_map/ppermute | solution.py:293
  54.0 1.3 %collective-permute-start.20 = (bf16[2,8,24,512]{3,2,1,0:T(8,128)(2,1)S(1)}, bf16[2,8,24,512]{3,2,1,0:T(8,128)(2,1)S(1)}, u32[]{:S(2)}, u32[]{:S(2)}) collective-permute-start(bf16[2,8,24,512]{3,2,1,0:T(8,128)(2,1)S(1)} %shard_map.103.refs_4_), channel_id=1, source_target_pairs={{1,0},{25,24},{65,64},{89,88},{0,1},{24,25},{64,65},{88,89},{9,8},... | collective-permute-start | bytes 1179656 | tf_op jit(solution)/shard_map/ppermute | solution.py:293
  55.2 1.2 %collective-permute-start.19 = (bf16[2,8,24,512]{3,2,1,0:T(8,128)(2,1)S(1)}, bf16[2,8,24,512]{3,2,1,0:T(8,128)(2,1)S(1)}, u32[]{:S(2)}, u32[]{:S(2)}) collective-permute-start(bf16[2,8,24,512]{3,2,1,0:T(8,128)(2,1)S(1)} %shard_map.103.refs_4_), channel_id=1, source_target_pairs={{64,0},{88,24},{1,64},{25,88},{65,1},{89,25},{0,65},{24,89},{72,8}... | collective-permute-start | bytes 1179656 | tf_op jit(solution)/shard_map/ppermute | solution.py:293
  56.5 3.1 %collective-permute-done.14.refs_5_.refs_2_ = bf16[200,512]{1,0:T(8,128)(2,1)S(1)} collective-permute-done((bf16[200,512]{1,0:T(8,128)(2,1)S(1)}, bf16[200,512]{1,0:T(8,128)(2,1)S(1)}, u32[]{:S(2)}, u32[]{:S(2)}) %collective-permute-start.14) | collective-permute-done | bytes 204832 | tf_op jit(solution)/shard_map/ppermute | solution.py:293
  60.0 1.5 %collective-permute-start.10 = (bf16[200,512]{1,0:T(8,128)(2,1)S(1)}, bf16[200,512]{1,0:T(8,128)(2,1)S(1)}, u32[]{:S(2)}, u32[]{:S(2)}) collective-permute-start(bf16[200,512]{1,0:T(8,128)(2,1)S(1)} %collective-permute-done.9.refs_4_.refs_1_), channel_id=1, source_target_pairs={{6,0},{14,8},{0,2},{8,10},{2,4},{10,12},{4,6},{12,14},{30,24},{22,... | collective-permute-start | bytes 614408 | tf_op jit(solution)/shard_map/ppermute | solution.py:293
  61.4 3.4 %collective-permute-done.11.refs_1_.refs_2_ = bf16[200,512]{1,0:T(8,128)(2,1)S(1)} collective-permute-done((bf16[200,512]{1,0:T(8,128)(2,1)S(1)}, bf16[200,512]{1,0:T(8,128)(2,1)S(1)}, u32[]{:S(2)}, u32[]{:S(2)}) %collective-permute-start.11) | collective-permute-done | bytes 204832 | tf_op jit(solution)/shard_map/ppermute | solution.py:293
  64.9 1.3 %collective-permute-done.10.refs_0_.refs_1_ = bf16[200,512]{1,0:T(8,128)(2,1)S(1)} collective-permute-done((bf16[200,512]{1,0:T(8,128)(2,1)S(1)}, bf16[200,512]{1,0:T(8,128)(2,1)S(1)}, u32[]{:S(2)}, u32[]{:S(2)}) %collective-permute-start.10) | collective-permute-done | bytes 204832 | tf_op jit(solution)/shard_map/ppermute | solution.py:293
  66.2 14.8 %collective-permute-start.16 = (f32[8,128]{1,0:T(8,128)S(1)}, f32[8,128]{1,0:T(8,128)S(1)}, u32[]{:S(2)}, u32[]{:S(2)}) collective-permute-start(f32[8,128]{1,0:T(8,128)S(1)} %shard_map.101.total), channel_id=1, source_target_pairs={{0,32},{32,0},{64,96},{96,64},{1,33},{33,1},{65,97},{97,65},{8,40}... | collective-permute-start | bytes 12296 | tf_op jit(solution)/shard_map/ppermute | solution.py:293
  (50 shorter events, 13.0 us)
Async XLA Ops:
  2.1 12.1 %collective-permute-start.4 = (bf16[5,8,24,512]{3,2,1,0:T(8,128)(2,1)S(1)}, bf16[5,8,24,512]{3,2,1,0:T(8,128)(2,1)S(1)}, u32[]{:S(2)}, u32[]{:S(2)}) collective-permute-start(bf16[5,8,24,512]{3,2,1,0:T(8,128)(2,1)S(1)} %get-tuple-element.39), channel_id=1, source_target_pairs={{0,32},{32,0},{64,96},{96,64},{1,33},{33,1},{65,97},{97,65},{8,40}... | collective-permute-start | bytes 2949128 | tf_op jit(solution)/shard_map/ppermute | solution.py:293
  3.6 3.0 %collective-permute-start = (bf16[3,8,24,512]{3,2,1,0:T(8,128)(2,1)S(1)}, bf16[3,8,24,512]{3,2,1,0:T(8,128)(2,1)S(1)}, u32[]{:S(2)}, u32[]{:S(2)}) collective-permute-start(bf16[3,8,24,512]{3,2,1,0:T(8,128)(2,1)S(1)} %get-tuple-element.34), channel_id=1, source_target_pairs={{0,32},{32,0},{64,96},{96,64},{1,33},{33,1},{65,97},{97,65},{8,40}... | collective-permute-start | bytes 1769480 | tf_op jit(solution)/shard_map/ppermute | solution.py:293
  6.7 12.0 %collective-permute-start.1 = (bf16[9,24,512]{2,1,0:T(8,128)(2,1)S(1)}, bf16[9,24,512]{2,1,0:T(8,128)(2,1)S(1)}, u32[]{:S(2)}, u32[]{:S(2)}) collective-permute-start(bf16[9,24,512]{2,1,0:T(8,128)(2,1)S(1)} %get-tuple-element.35), channel_id=1, source_target_pairs={{14,0},{6,8},{8,2},{0,10},{10,4},{2,12},{12,6},{4,14},{22,24},{30,... | collective-permute-start | bytes 663560 | tf_op jit(solution)/shard_map/ppermute | solution.py:293
  10.9 7.8 %collective-permute-start.2 = (bf16[9,24,512]{2,1,0:T(8,128)(2,1)S(1)}, bf16[9,24,512]{2,1,0:T(8,128)(2,1)S(1)}, u32[]{:S(2)}, u32[]{:S(2)}) collective-permute-start(bf16[9,24,512]{2,1,0:T(8,128)(2,1)S(1)} %get-tuple-element.36), channel_id=1, source_target_pairs={{10,0},{2,8},{12,2},{4,10},{14,4},{6,12},{8,6},{0,14},{18,24},{26,... | collective-permute-start | bytes 663560 | tf_op jit(solution)/shard_map/ppermute | solution.py:293
  13.1 8.2 %collective-permute-start.3 = (bf16[9,24,512]{2,1,0:T(8,128)(2,1)S(1)}, bf16[9,24,512]{2,1,0:T(8,128)(2,1)S(1)}, u32[]{:S(2)}, u32[]{:S(2)}) collective-permute-start(bf16[9,24,512]{2,1,0:T(8,128)(2,1)S(1)} %get-tuple-element.37), channel_id=1, source_target_pairs={{4,0},{12,8},{6,2},{14,10},{0,4},{8,12},{2,6},{10,14},{28,24},{20,... | collective-permute-start | bytes 663560 | tf_op jit(solution)/shard_map/ppermute | solution.py:293
  14.4 8.6 %collective-permute-start.5 = (bf16[9,24,512]{2,1,0:T(8,128)(2,1)S(1)}, bf16[9,24,512]{2,1,0:T(8,128)(2,1)S(1)}, u32[]{:S(2)}, u32[]{:S(2)}) collective-permute-start(bf16[9,24,512]{2,1,0:T(8,128)(2,1)S(1)} %get-tuple-element.40), channel_id=1, source_target_pairs={{12,0},{4,8},{14,2},{6,10},{8,4},{0,12},{10,6},{2,14},{20,24},{28,... | collective-permute-start | bytes 663560 | tf_op jit(solution)/shard_map/ppermute | solution.py:293
  17.3 7.1 %collective-permute-start.6 = (bf16[9,24,512]{2,1,0:T(8,128)(2,1)S(1)}, bf16[9,24,512]{2,1,0:T(8,128)(2,1)S(1)}, u32[]{:S(2)}, u32[]{:S(2)}) collective-permute-start(bf16[9,24,512]{2,1,0:T(8,128)(2,1)S(1)} %get-tuple-element.41), channel_id=1, source_target_pairs={{8,0},{0,8},{10,2},{2,10},{12,4},{4,12},{14,6},{6,14},{16,24},{24,... | collective-permute-start | bytes 663560 | tf_op jit(solution)/shard_map/ppermute | solution.py:293
  18.7 6.5 %collective-permute-start.7 = (bf16[9,24,512]{2,1,0:T(8,128)(2,1)S(1)}, bf16[9,24,512]{2,1,0:T(8,128)(2,1)S(1)}, u32[]{:S(2)}, u32[]{:S(2)}) collective-permute-start(bf16[9,24,512]{2,1,0:T(8,128)(2,1)S(1)} %get-tuple-element.42), channel_id=1, source_target_pairs={{6,0},{14,8},{0,2},{8,10},{2,4},{10,12},{4,6},{12,14},{30,24},{22,... | collective-permute-start | bytes 663560 | tf_op jit(solution)/shard_map/ppermute | solution.py:293
  18.7 6.5 %collective-permute-start.8 = (bf16[9,24,512]{2,1,0:T(8,128)(2,1)S(1)}, bf16[9,24,512]{2,1,0:T(8,128)(2,1)S(1)}, u32[]{:S(2)}, u32[]{:S(2)}) collective-permute-start(bf16[9,24,512]{2,1,0:T(8,128)(2,1)S(1)} %get-tuple-element.43), channel_id=1, source_target_pairs={{2,0},{10,8},{4,2},{12,10},{6,4},{14,12},{0,6},{8,14},{26,24},{18,... | collective-permute-start | bytes 663560 | tf_op jit(solution)/shard_map/ppermute | solution.py:293
  26.1 9.5 %all-to-all-start = ((bf16[8,24,512]{2,1,0:T(8,128)(2,1)}), bf16[8,24,512]{2,1,0:T(8,128)(2,1)S(1)}, u32[]{:S(2)}, u32[]{:S(2)}) async-start(bf16[8,24,512]{2,1,0:T(8,128)(2,1)} %get-tuple-element.45), calls=%async_computation | async-start | bytes 393216 | tf_op jit(solution)/shard_map/all_to_all | solution.py:89
  44.2 7.5 %collective-permute-start.9 = (bf16[200,512]{1,0:T(8,128)(2,1)S(1)}, bf16[200,512]{1,0:T(8,128)(2,1)S(1)}, u32[]{:S(2)}, u32[]{:S(2)}) collective-permute-start(bf16[200,512]{1,0:T(8,128)(2,1)S(1)} %shard_map.100.refs_7_.refs_0_), channel_id=1, source_target_pairs={{8,0},{0,8},{10,2},{2,10},{12,4},{4,12},{14,6},{6,14},{16,24},{24,... | collective-permute-start | bytes 614408 | tf_op jit(solution)/shard_map/ppermute | solution.py:293
  47.0 8.2 %collective-permute-start.15 = (bf16[200,512]{1,0:T(8,128)(2,1)S(1)}, bf16[200,512]{1,0:T(8,128)(2,1)S(1)}, u32[]{:S(2)}, u32[]{:S(2)}) collective-permute-start(bf16[200,512]{1,0:T(8,128)(2,1)S(1)} %shard_map.100.refs_7_.refs_0_), channel_id=1, source_target_pairs={{2,0},{10,8},{4,2},{12,10},{6,4},{14,12},{0,6},{8,14},{26,24},{18,... | collective-permute-start | bytes 614408 | tf_op jit(solution)/shard_map/ppermute | solution.py:293
  49.4 10.2 %collective-permute-start.14 = (bf16[200,512]{1,0:T(8,128)(2,1)S(1)}, bf16[200,512]{1,0:T(8,128)(2,1)S(1)}, u32[]{:S(2)}, u32[]{:S(2)}) collective-permute-start(bf16[200,512]{1,0:T(8,128)(2,1)S(1)} %shard_map.100.refs_7_.refs_0_), channel_id=1, source_target_pairs={{6,0},{14,8},{0,2},{8,10},{2,4},{10,12},{4,6},{12,14},{30,24},{22,... | collective-permute-start | bytes 614408 | tf_op jit(solution)/shard_map/ppermute | solution.py:293
  49.4 4.5 %collective-permute-start.17 = (bf16[8,24,512]{2,1,0:T(8,128)(2,1)S(1)}, bf16[8,24,512]{2,1,0:T(8,128)(2,1)S(1)}, u32[]{:S(2)}, u32[]{:S(2)}) collective-permute-start(bf16[8,24,512]{2,1,0:T(8,128)(2,1)S(1)} %get-tuple-element.51.refs_0_), channel_id=1, source_target_pairs={{24,0},{0,24},{88,64},{64,88},{25,1},{1,25},{89,65},{65,89},{16,8}... | collective-permute-start | bytes 589832 | tf_op jit(solution)/shard_map/ppermute | solution.py:293
  49.7 10.2 %collective-permute-start.12 = (bf16[200,512]{1,0:T(8,128)(2,1)S(1)}, bf16[200,512]{1,0:T(8,128)(2,1)S(1)}, u32[]{:S(2)}, u32[]{:S(2)}) collective-permute-start(bf16[200,512]{1,0:T(8,128)(2,1)S(1)} %shard_map.100.refs_7_.refs_0_), channel_id=1, source_target_pairs={{4,0},{12,8},{6,2},{14,10},{0,4},{8,12},{2,6},{10,14},{28,24},{20,... | collective-permute-start | bytes 614408 | tf_op jit(solution)/shard_map/ppermute | solution.py:293
  51.7 8.3 %collective-permute-start.13 = (bf16[200,512]{1,0:T(8,128)(2,1)S(1)}, bf16[200,512]{1,0:T(8,128)(2,1)S(1)}, u32[]{:S(2)}, u32[]{:S(2)}) collective-permute-start(bf16[200,512]{1,0:T(8,128)(2,1)S(1)} %collective-permute-done.9.refs_4_.refs_1_), channel_id=1, source_target_pairs={{4,0},{12,8},{6,2},{14,10},{0,4},{8,12},{2,6},{10,14},{28,24},{20,... | collective-permute-start | bytes 614408 | tf_op jit(solution)/shard_map/ppermute | solution.py:293
  54.0 28.0 %collective-permute-start.20 = (bf16[2,8,24,512]{3,2,1,0:T(8,128)(2,1)S(1)}, bf16[2,8,24,512]{3,2,1,0:T(8,128)(2,1)S(1)}, u32[]{:S(2)}, u32[]{:S(2)}) collective-permute-start(bf16[2,8,24,512]{3,2,1,0:T(8,128)(2,1)S(1)} %shard_map.103.refs_4_), channel_id=1, source_target_pairs={{1,0},{25,24},{65,64},{89,88},{0,1},{24,25},{64,65},{88,89},{9,8},... | collective-permute-start | bytes 1179656 | tf_op jit(solution)/shard_map/ppermute | solution.py:293
  55.2 26.8 %collective-permute-start.19 = (bf16[2,8,24,512]{3,2,1,0:T(8,128)(2,1)S(1)}, bf16[2,8,24,512]{3,2,1,0:T(8,128)(2,1)S(1)}, u32[]{:S(2)}, u32[]{:S(2)}) collective-permute-start(bf16[2,8,24,512]{3,2,1,0:T(8,128)(2,1)S(1)} %shard_map.103.refs_4_), channel_id=1, source_target_pairs={{64,0},{88,24},{1,64},{25,88},{65,1},{89,25},{0,65},{24,89},{72,8}... | collective-permute-start | bytes 1179656 | tf_op jit(solution)/shard_map/ppermute | solution.py:293
  59.6 22.4 %collective-permute-start.18 = (bf16[2,8,24,512]{3,2,1,0:T(8,128)(2,1)S(1)}, bf16[2,8,24,512]{3,2,1,0:T(8,128)(2,1)S(1)}, u32[]{:S(2)}, u32[]{:S(2)}) collective-permute-start(bf16[2,8,24,512]{3,2,1,0:T(8,128)(2,1)S(1)} %shard_map.103.refs_4_), channel_id=1, source_target_pairs={{65,0},{89,24},{0,64},{24,88},{64,1},{88,25},{1,65},{25,89},{73,8}... | collective-permute-start | bytes 1179656 | tf_op jit(solution)/shard_map/ppermute | solution.py:293
  60.0 4.9 %collective-permute-start.11 = (bf16[200,512]{1,0:T(8,128)(2,1)S(1)}, bf16[200,512]{1,0:T(8,128)(2,1)S(1)}, u32[]{:S(2)}, u32[]{:S(2)}) collective-permute-start(bf16[200,512]{1,0:T(8,128)(2,1)S(1)} %collective-permute-done.9.refs_4_.refs_1_), channel_id=1, source_target_pairs={{2,0},{10,8},{4,2},{12,10},{6,4},{14,12},{0,6},{8,14},{26,24},{18,... | collective-permute-start | bytes 614408 | tf_op jit(solution)/shard_map/ppermute | solution.py:293
  60.0 6.2 %collective-permute-start.10 = (bf16[200,512]{1,0:T(8,128)(2,1)S(1)}, bf16[200,512]{1,0:T(8,128)(2,1)S(1)}, u32[]{:S(2)}, u32[]{:S(2)}) collective-permute-start(bf16[200,512]{1,0:T(8,128)(2,1)S(1)} %collective-permute-done.9.refs_4_.refs_1_), channel_id=1, source_target_pairs={{6,0},{14,8},{0,2},{8,10},{2,4},{10,12},{4,6},{12,14},{30,24},{22,... | collective-permute-start | bytes 614408 | tf_op jit(solution)/shard_map/ppermute | solution.py:293
  66.2 15.6 %collective-permute-start.16 = (f32[8,128]{1,0:T(8,128)S(1)}, f32[8,128]{1,0:T(8,128)S(1)}, u32[]{:S(2)}, u32[]{:S(2)}) collective-permute-start(f32[8,128]{1,0:T(8,128)S(1)} %shard_map.101.total), channel_id=1, source_target_pairs={{0,32},{32,0},{64,96},{96,64},{1,33},{33,1},{65,97},{97,65},{8,40}... | collective-permute-start | bytes 12296 | tf_op jit(solution)/shard_map/ppermute | solution.py:293
  82.5 2.4 %collective-permute-start.22 = (bf16[4,8,24,512]{3,2,1,0:T(8,128)(2,1)S(1)}, bf16[4,8,24,512]{3,2,1,0:T(8,128)(2,1)S(1)}, u32[]{:S(2)}, u32[]{:S(2)}) collective-permute-start(bf16[4,8,24,512]{3,2,1,0:T(8,128)(2,1)S(1)} %shard_map.104.refs_0_), channel_id=1, source_target_pairs={{0,32},{32,0},{64,96},{96,64},{1,33},{33,1},{65,97},{97,65},{8,40}... | collective-permute-start | bytes 2359304 | tf_op jit(solution)/shard_map/ppermute | solution.py:293
  83.3 2.6 %collective-permute-start.21 = (bf16[4,8,24,512]{3,2,1,0:T(8,128)(2,1)S(1)}, bf16[4,8,24,512]{3,2,1,0:T(8,128)(2,1)S(1)}, u32[]{:S(2)}, u32[]{:S(2)}) collective-permute-start(bf16[4,8,24,512]{3,2,1,0:T(8,128)(2,1)S(1)} %shard_map.105.refs_1_), channel_id=1, source_target_pairs={{0,32},{32,0},{64,96},{96,64},{1,33},{33,1},{65,97},{97,65},{8,40}... | collective-permute-start | bytes 2359304 | tf_op jit(solution)/shard_map/ppermute | solution.py:293
  (4 other events, 92.3 us)
